TPU v7x, 128 devices: a whole 4x4x4 slice. The times are simulated.
128 devices in a mesh: seq: 16 (over x, z), feat: 8 (over y, core).
Axes of the slice: x: 4, y: 4, z: 4, core: 2. Of those that a mesh axis runs over, the one named last changes fastest.
Arguments:
- injection: bfloat16 [2048, 5120], P('seq', 'feat'), may hold values from -8 to 8
- warm_start: bfloat16 [2048, 5120], P('seq', 'feat'), may hold values from -12 to 12
- gain_in: float32 [5120], replicated, may hold values from 0.5 to 1.5
- gain_out: float32 [5120], replicated, may hold values from 0.5 to 1.5
- w_query: bfloat16 [5120, 5120], P(None, 'feat'), may hold values from -0.0848993624 to 0.0848993624
- w_key: bfloat16 [5120, 1024], P(None, 'feat'), may hold values from -0.0848993624 to 0.0848993624
- w_value: bfloat16 [5120, 1024], P(None, 'feat'), may hold values from -0.078125 to 0.078125
- w_out: bfloat16 [5120, 5120], P('feat'), may hold values from -0.078125 to 0.078125
Outputs:
- equilibrium: float32 [2048, 5120], P('seq', 'feat')
All inputs are finite; a program needn't handle non-finite values.
Results may differ from a plain program's by a relative error of at most 0.009.
Values may be sent and summed in bfloat16 or wider, within the bound.
No kernel may reach another device: no remote copies, remote signals or barrier semaphores. Data moves between devices by JAX's collectives and lax.ppermute only.
A program may use at most 128 MiB of HBM per device.

v0:
```python
import functools
import math

import jax
import jax.numpy as jnp
from jax import lax
from jax.experimental import pallas as pl
from jax.experimental.pallas import tpu as pltpu
from jax.sharding import Mesh
from jax.sharding import PartitionSpec as P


D = 5120
HEADS = 40
KV_HEADS = 8
HEAD_DIM = 128
GROUP = HEADS // KV_HEADS
ITERS = 4
TOKENS = 2048
SEQ = ("x", "z")
FEAT = ("y", "c")
EVERY = ("x", "z", "y", "c")
EPS = 1e-06
LAMBDA = 0.03
SCORE_SCALE = 1.0 / math.sqrt(HEAD_DIM)
F32 = jnp.float32
BF16 = jnp.bfloat16

VMEM = pl.BlockSpec(memory_space=pltpu.VMEM)
HBM = pl.BlockSpec(memory_space=pltpu.HBM)


def shift(n, by):
    return [(at, (at + by) % n) for at in range(n)]


def call(kernel, outs, *args, specs=None, scratch=(), vmem=8, flops=0, touched=0):
    specs = [VMEM] * len(args) if specs is None else specs
    args = [
        pltpu.with_memory_space_constraint(arg, pltpu.HBM) if spec is HBM else arg
        for arg, spec in zip(args, specs)
    ]
    return pl.pallas_call(
        kernel,
        out_shape=outs,
        in_specs=specs,
        out_specs=jax.tree.map(lambda out: HBM if out.memory_space == pltpu.HBM else VMEM, outs),
        scratch_shapes=list(scratch),
        compiler_params=pltpu.CompilerParams(vmem_limit_bytes=vmem * 1024 * 1024),
        cost_estimate=pl.CostEstimate(flops=flops, bytes_accessed=touched, transcendentals=0),
    )(*args)


def total(x):
    return jnp.sum(jnp.sum(x, axis=1, keepdims=True), axis=0, keepdims=True)


def row_offset(row):
    y, c = lax.axis_index("y"), lax.axis_index("c")
    half, block, inner = row // 64, (row // 16) % 4, row % 16
    return (((y - block + 4) % 4) * 2 + (c + half) % 2) * 16 + inner


def load_keys(wk_ref, wv_ref, held, sem):
    copies = [
        pltpu.make_async_copy(wk_ref, held.at[:, :HEAD_DIM], sem.at[0]),
        pltpu.make_async_copy(wv_ref, held.at[:, HEAD_DIM:], sem.at[1]),
    ]
    for copy in copies:
        copy.start()
    return copies


def first_kernel(wk_ref, wv_ref, gain_ref, *refs):
    pieces, (rows_out, raw_out, rows_ref, held, raw_ref, sem) = refs[:2], refs[2:]
    loads = load_keys(wk_ref, wv_ref, held, sem)
    y, c = lax.axis_index("y"), lax.axis_index("c")
    for half in range(2):
        for block in range(4):
            column = (((y - block + 4) % 4) * 2 + (c + half) % 2) * 640
            columns = pl.ds(pl.multiple_of(column, 640), 640)
            for at in range(8):
                source = pl.multiple_of(row_offset(16 * at), 16)
                rows_ref[16 * at : 16 * at + 16, columns] = pieces[half][block, pl.ds(source, 16), :]
    keep = pltpu.make_async_copy(rows_ref, rows_out, sem.at[2])
    keep.start()

    def one_part(n, squares):
        at = pl.ds(pl.multiple_of(n * 640, 640), 640)
        part = rows_ref[:, at].astype(F32) * (1.0 / gain_ref[:, at])
        return squares + jnp.sum(part * part, axis=1, keepdims=True)

    squares = lax.fori_loop(0, 8, one_part, jnp.zeros((128, 1), F32))
    raw_ref[:, 256:] = jnp.broadcast_to(squares, (128, 128))
    for load in loads:
        load.wait()
    raw_ref[:, :256] = jnp.dot(rows_ref[...], held[...], preferred_element_type=F32)
    save = pltpu.make_async_copy(raw_ref, raw_out, sem.at[3])
    save.start()
    save.wait()
    keep.wait()


def project_kernel(k, *refs):
    (wk_ref, wv_ref, gain_ref), refs = refs[:3], refs[3:]
    older_hbm, pieces = refs[:k], refs[k : k + 2]
    rows_out, raw_out, rows_ref, held, raw_ref, sem, older_ref, older_sem = refs[k + 2 :]
    for n in range(8):
        for at in range(k):
            columns = slice(640 * n, 640 * n + 640)
            pltpu.make_async_copy(
                older_hbm[at].at[:, columns], older_ref.at[at, :, columns], older_sem.at[at, n]
            ).start()
    loads = load_keys(wk_ref, wv_ref, held, sem)

    def one_part(n, sums):
        at = pl.ds(pl.multiple_of(n * 640, 640), 640)
        newest = jnp.concatenate([piece[:, at] for piece in pieces], axis=0)
        rows_ref[:, at] = newest
        newest = newest.astype(F32)
        inverse = 1.0 / gain_ref[:, at]
        weighed = newest * (inverse * inverse)
        sums = list(sums)
        for old in range(k):
            pltpu.make_async_copy(
                older_hbm[old].at[:, at], older_ref.at[old, :, at], older_sem.at[old, n]
            ).wait()
            other = older_ref[old, :, at].astype(F32)
            sums[old] = sums[old] + jnp.sum(weighed * other, axis=1, keepdims=True)
        sums[k] = sums[k] + jnp.sum(weighed * newest, axis=1, keepdims=True)
        return tuple(sums)

    sums = lax.fori_loop(0, 8, one_part, tuple(jnp.zeros((128, 1), F32) for _ in range(k + 1)))
    keep = pltpu.make_async_copy(rows_ref, rows_out, sem.at[2])
    keep.start()
    lane = lax.broadcasted_iota(jnp.int32, (1, 128), 1)
    raw_ref[:, 256:] = functools.reduce(
        lambda a, b: a + b, [jnp.where(lane == at, value, 0.0) for at, value in enumerate(sums)]
    )
    for load in loads:
        load.wait()
    raw_ref[:, :256] = jnp.dot(rows_ref[...], held[...], preferred_element_type=F32)
    save = pltpu.make_async_copy(raw_ref, raw_out, sem.at[3])
    save.start()
    save.wait()
    keep.wait()


def share_kernel(k, *refs):
    raw_hbm, (share_ref, scale_out, kv_ref) = refs[k : 2 * k + 1], refs[2 * k + 1 : 2 * k + 4]
    raws, scale_ref, kv_held, sem = refs[2 * k + 4 :]
    loads = [
        pltpu.make_async_copy(raw, raws.at[at], sem.at[at]) for at, raw in enumerate(raw_hbm)
    ]
    for load in loads:
        load.start()
    shares = mix_shares(k, refs[:k])
    lane = lax.broadcasted_iota(jnp.int32, (1, 128), 1)
    share_ref[...] = functools.reduce(
        lambda a, b: a + b, [jnp.where(lane == at, share, 0.0) for at, share in enumerate(shares)]
    )
    for load in loads:
        load.wait()
    squares = jnp.zeros((128, 1), F32)
    for at in range(k + 1):
        for other in range(at + 1):
            twice = 1.0 if other == at else 2.0
            pair = raws[at, :, 256 + other : 257 + other]
            squares = squares + (twice * shares[at] * shares[other]) * pair
    scale = lax.rsqrt(jnp.maximum(squares, 0.0) / D + EPS)
    scale_ref[...] = jnp.broadcast_to(scale, (128, 128))
    kv = functools.reduce(
        lambda a, b: a + b, [share * raws[at, :, :256] for at, share in enumerate(shares)]
    )
    kv_held[...] = (kv * scale).astype(BF16)
    stores = [pltpu.make_async_copy(kv_held, kv_ref.at[at], sem.at[at]) for at in range(16)]
    stores.append(pltpu.make_async_copy(scale_ref, scale_out, sem.at[16]))
    for store in stores:
        store.start()
    for store in stores:
        store.wait()


def take_share(share_ref, at):
    lane = lax.broadcasted_iota(jnp.int32, (1, 128), 1)
    return jnp.sum(jnp.where(lane == at, share_ref[...], 0.0), axis=1, keepdims=True)


def query_kernel(k, share_ref, *refs):
    parts, (w_ref, q_ref, acc) = refs[: k + 1], refs[k + 1 :]

    @pl.when(pl.program_id(0) == 0)
    def _():
        acc[...] = jnp.zeros_like(acc)

    if k == 0:
        rows = parts[0][...]
    else:
        rows = functools.reduce(
            lambda a, b: a + b,
            [take_share(share_ref, at) * part[...].astype(F32) for at, part in enumerate(parts)],
        ).astype(BF16)
    acc[...] += jnp.dot(rows, w_ref[...], preferred_element_type=F32)

    @pl.when(pl.program_id(0) == 4)
    def _():
        q_ref[...] = acc[...].astype(BF16)


def query_dot(share, parts, w_query):
    return pl.pallas_call(
        functools.partial(query_kernel, len(parts) - 1),
        grid=(5,),
        out_shape=pltpu.VMEM((128, 640), BF16),
        in_specs=[pl.BlockSpec((1, 128), lambda n: (0, 0))]
        + [pl.BlockSpec((128, 1024), lambda n: (0, n))] * len(parts)
        + [pl.BlockSpec((1024, 640), lambda n: (n, 0))],
        out_specs=pl.BlockSpec((128, 640), lambda n: (0, 0)),
        scratch_shapes=[pltpu.VMEM((128, 640), F32)],
        compiler_params=pltpu.CompilerParams(vmem_limit_bytes=10 * 1024 * 1024),
        cost_estimate=pl.CostEstimate(
            flops=2 * 128 * D * 640, bytes_accessed=8_000_000, transcendentals=0
        ),
    )(share, *[pltpu.with_memory_space_constraint(part, pltpu.HBM) for part in (*parts, w_query)])


def attend_kernel(
    q_ref, scale_hbm, kv_ref, w_ref, own_ref, send_ref, w_held, scale_ref, attended, sem
):
    small = pltpu.make_async_copy(scale_hbm, scale_ref, sem.at[1])
    small.start()
    load = pltpu.make_async_copy(w_ref, w_held, sem.at[0])
    load.start()
    s = lax.axis_index("x") * 4 + lax.axis_index("z")
    row_at = s * 128 + row_offset(lax.broadcasted_iota(jnp.int32, (128, 1), 0))
    column = lax.broadcasted_iota(jnp.int32, (1, TOKENS), 1)
    allowed = row_at >= (column // 128) * 128 + row_offset(column % 128)
    small.wait()
    factor = scale_ref[:, :1] * (SCORE_SCALE / math.log(2.0))

    def one_head(g, carry):
        at = pl.ds(pl.multiple_of(g * HEAD_DIM, HEAD_DIM), HEAD_DIM)
        keys = kv_ref[:, :, :HEAD_DIM].reshape(TOKENS, HEAD_DIM)
        values = kv_ref[:, :, HEAD_DIM:].reshape(TOKENS, HEAD_DIM)
        raw = lax.dot_general(
            q_ref[:, at], keys, (((1,), (1,)), ((), ())), preferred_element_type=F32
        )
        raw = jnp.where(allowed, raw, -1e30)
        weight = jnp.exp2((raw - jnp.max(raw, axis=1, keepdims=True)) * factor)
        row_sum = jnp.sum(weight, axis=1, keepdims=True)
        summed = jnp.dot(weight.astype(BF16), values, preferred_element_type=F32)
        attended[:, at] = (summed / row_sum).astype(BF16)
        return carry

    lax.fori_loop(0, GROUP, one_head, 0)
    load.wait()

    def one_part(n, carry):
        at = pl.ds(pl.multiple_of(n * 1280, 1280), 1280)
        part = jnp.dot(attended[...], w_held[:, at], preferred_element_type=F32)
        own_ref[:, at] = part[:64]
        send_ref[:, at] = part[64:].astype(BF16)
        return carry

    lax.fori_loop(0, 4, one_part, 0)


def home_copies(held, target, sem, start):
    y, c = lax.axis_index("y"), lax.axis_index("c")
    copies = []
    for by in range(4):
        for half in range(2):
            column = (((y + by) % 4) * 2 + (c + half) % 2) * 640
            columns = pl.ds(pl.multiple_of(column, 640), 640)
            copies.append(
                pltpu.make_async_copy(
                    held.at[:, columns], target(by, half), sem.at[start + 2 * by + half]
                )
            )
    return copies


def pack_kernel(*refs):
    images, outs, (held, sem) = refs[:3], refs[3:7], refs[7:]
    loads = [
        pltpu.make_async_copy(image, held.at[at], sem.at[at]) for at, image in enumerate(images)
    ]
    for load in loads:
        load.start()
    copies = []
    for at in range(3):
        loads[at].wait()
        fresh = home_copies(
            held.at[at], lambda by, half: outs[by].at[half, at], sem, 3 + 8 * at
        )
        for copy in fresh:
            copy.start()
        copies += fresh
    for copy in copies:
        copy.wait()


def finish_kernel(k, own_ref, a_ref, b_ref, d_ref, inj_ref, x_ref, gain_ref, gain_in_ref, *rest):
    older, rest = rest[:k], rest[k:]
    image_held, residual_held, dots_held, sem = rest[-4:]
    image_out, residual_out = rest[:2]
    inj, x = inj_ref[...].astype(F32), x_ref[...].astype(F32)
    summed = (x + inj) + (
        own_ref[...] + a_ref[...].astype(F32) + b_ref[...].astype(F32) + d_ref[...].astype(F32)
    )
    scale = lax.rsqrt(jnp.sum(summed * summed, axis=1, keepdims=True) / D + EPS)
    image = summed * scale * gain_ref[...]
    residual = image - x
    image_held[...] = image
    residual_held[...] = residual
    copies = [
        pltpu.make_async_copy(image_held, image_out, sem.at[0]),
        pltpu.make_async_copy(residual_held, residual_out, sem.at[1]),
    ]
    if k == ITERS - 1:
        copies += home_copies(image_held, lambda by, half: rest[2 + by].at[half], sem, 2)
    for copy in copies:
        copy.start()
    if k < ITERS - 1:
        rest[2][...] = ((image + inj) * gain_in_ref[...]).astype(BF16)
    if k > 0:
        lane = lax.broadcasted_iota(jnp.int32, (1, 128), 1)
        dots = jnp.where(lane == k, total(residual * residual), 0.0)
        for at, other in enumerate(older):
            dots = dots + jnp.where(lane == at, total(residual * other[...]), 0.0)
        if k == 1:
            dots = dots + jnp.where(lane == 7, total(older[0][...] * older[0][...]), 0.0)
        dots_held[...] = jnp.broadcast_to(dots.reshape(1, 1, 128), (128, 1, 128))
        table_out = rest[3] if k < ITERS - 1 else rest[6]
        copies.append(pltpu.make_async_copy(dots_held, table_out, sem.at[10]))
        copies[-1].start()
    for copy in copies:
        copy.wait()


def solve_small(matrix, size_now):
    rows = [list(row) for row in matrix]
    values = [jnp.ones((1, 1), F32) for _ in range(size_now)]
    for pivot in range(size_now):
        for below in range(pivot + 1, size_now):
            ratio = rows[below][pivot] / rows[pivot][pivot]
            rows[below] = [b - ratio * p for b, p in zip(rows[below], rows[pivot])]
            values[below] = values[below] - ratio * values[pivot]
    result = [None] * size_now
    for pivot in reversed(range(size_now)):
        running = values[pivot]
        for later in range(pivot + 1, size_now):
            running = running - rows[pivot][later] * result[later]
        result[pivot] = running / rows[pivot][pivot]
    return result


def mix_shares(k, tables):
    if k == 0:
        return [1.0]
    lane = lax.broadcasted_iota(jnp.int32, (1, 128), 1)
    gram = {}
    for at, table in enumerate(tables):
        sums = jnp.sum(table[:, 0, :], axis=0, keepdims=True)
        for other in range(at + 2):
            gram[at + 1, other] = jnp.sum(jnp.where(lane == other, sums, 0.0), axis=1, keepdims=True)
        if at == 0:
            gram[0, 0] = jnp.sum(jnp.where(lane == 7, sums, 0.0), axis=1, keepdims=True)
    system = [
        [
            gram[max(i, j), min(i, j)] / float(TOKENS * D) + (LAMBDA if i == j else 0.0)
            for j in range(k + 1)
        ]
        for i in range(k + 1)
    ]
    unscaled = solve_small(system, k + 1)
    whole = functools.reduce(lambda a, b: a + b, unscaled)
    return [u / whole for u in unscaled]


def mix_kernel(share_ref, *refs):
    refs[-1][...] = functools.reduce(
        lambda a, b: a + b,
        [take_share(share_ref, at) * image[...] for at, image in enumerate(refs[:-1])],
    )


def last_kernel(k, *refs):
    shares = mix_shares(k, refs[:k])
    older, newest, (out_hbm, out_ref, sem) = refs[k : k + 5], refs[k + 5 : k + 10], refs[-3:]
    y, c = lax.axis_index("y"), lax.axis_index("c")
    for by in range(4):
        for half in range(2):
            row = (((y - by + 4) % 4) * 2 + (c + half) % 2) * 16
            rows = pl.ds(pl.multiple_of(row, 16), 16)
            old = older[by][0] if half == 0 else older[4][by]
            mixed = shares[k] * (newest[by][0] if half == 0 else newest[4][by])
            for at in range(k):
                mixed = mixed + shares[at] * old[at]
            out_ref[rows, :] = mixed
    store = pltpu.make_async_copy(out_ref, out_hbm, sem)
    store.start()
    store.wait()


def start_kernel(inj_hbm, warm_hbm, gain_hbm, payload_ref, *refs):
    home_refs, (inj_ref, warm_ref, gain_ref, sem) = refs[:4], refs[4:]
    loads = [
        pltpu.make_async_copy(gain_hbm, gain_ref, sem.at[2]),
        pltpu.make_async_copy(inj_hbm, inj_ref, sem.at[0]),
        pltpu.make_async_copy(warm_hbm, warm_ref, sem.at[1]),
    ]
    for load in loads:
        load.start()
    y, c = lax.axis_index("y"), lax.axis_index("c")
    for load in loads:
        load.wait()
    gain = gain_ref[:, pl.ds(pl.multiple_of((y * 2 + c) * 640, 640), 640)]
    inj, warm = inj_ref[...].astype(F32), warm_ref[...].astype(F32)
    payload_ref[...] = ((inj + warm) * gain).astype(BF16)
    for by in range(4):
        for half in range(2):
            row = (((y + by) % 4) * 2 + (c + half) % 2) * 16
            rows = pl.ds(pl.multiple_of(row, 16), 16)
            home_refs[by][half, 0] = inj_ref[rows, :]
            home_refs[by][half, 1] = warm_ref[rows, :]


def settle_kernel(*refs):
    inj_ref, warm_ref = refs[5:]
    y, c = lax.axis_index("y"), lax.axis_index("c")
    for by in range(4):
        for half in range(2):
            column = (((y - by + 4) % 4) * 2 + (c + half) % 2) * 640
            columns = pl.ds(pl.multiple_of(column, 640), 640)
            piece = refs[by][0] if half == 0 else refs[4][by]
            inj_ref[:, columns] = piece[0]
            warm_ref[:, columns] = piece[1]


def move_home(pieces):
    near = [pieces[0]] + [lax.ppermute(pieces[by], "y", shift(4, by)) for by in (1, 2, 3)]
    joined = jnp.stack([piece[1] for piece in near])
    return [*near, lax.ppermute(joined, "c", shift(2, 1))]


def on_device(injection, warm_start, gain_in, gain_out, w_query, w_key, w_value, w_out):
    gain_in, gain_out = gain_in.reshape(1, D), gain_out.reshape(1, D)
    tokens = pltpu.HBM((16, D), F32)
    wide = pltpu.VMEM((16, D), F32)
    narrow = pltpu.VMEM((16, D), BF16)
    home_narrow = pltpu.VMEM((2, 2, 16, 640), BF16)
    home_wide = pltpu.HBM((2, 16, 640), F32)
    payload, *home = call(
        start_kernel,
        (pltpu.VMEM((128, 640), BF16), *[home_narrow] * 4),
        injection,
        warm_start,
        gain_in,
        specs=[HBM, HBM, HBM],
        scratch=[
            pltpu.VMEM((128, 640), BF16),
            pltpu.VMEM((128, 640), BF16),
            pltpu.VMEM((1, D), F32),
            pltpu.SemaphoreType.DMA((3,)),
        ],
    )
    settled = []
    images, residuals, parts, tables, dots = [], [], [], [], None
    raws = []
    projected = (pltpu.HBM((128, D), BF16), pltpu.HBM((128, 384), F32))
    project_scratch = [
        pltpu.VMEM((128, D), BF16),
        pltpu.VMEM((D, 2 * HEAD_DIM), BF16),
        pltpu.VMEM((128, 384), F32),
        pltpu.SemaphoreType.DMA((4,)),
    ]
    for k in range(ITERS):
        pieces = [payload] + [lax.ppermute(payload, "y", shift(4, by)) for by in (1, 2, 3)]
        if dots is not None:
            tables.append(lax.all_to_all(dots, EVERY, split_axis=0, concat_axis=0, tiled=True))
        mine = jnp.stack(pieces) if k == 0 else jnp.concatenate(pieces, axis=0)
        pieces = [mine, lax.ppermute(mine, "c", shift(2, 1))]
        if k == 1:
            parts, raws = [], []
        if k == 0:
            rows, raw = call(
                first_kernel,
                projected,
                w_key,
                w_value,
                gain_in,
                *pieces,
                specs=[HBM] * 2 + [VMEM] * 3,
                vmem=8,
                scratch=project_scratch,
                flops=2 * 128 * D * 256,
                touched=4_000_000,
            )
        else:
            rows, raw = call(
                functools.partial(project_kernel, k - 1),
                projected,
                w_key,
                w_value,
                gain_in,
                *parts,
                *pieces,
                specs=[HBM] * 2 + [VMEM] + [HBM] * len(parts) + [VMEM] * 2,
                vmem=10,
                scratch=project_scratch
                + [
                    pltpu.VMEM((k - 1, 128, D) if k > 1 else (1, 8, 128), BF16),
                    pltpu.SemaphoreType.DMA((max(k - 1, 1), 8)),
                ],
                flops=2 * 128 * D * 256,
                touched=4_000_000,
            )
        parts.append(rows)
        raws.append(raw)
        share, scale, kv = call(
            functools.partial(share_kernel, len(parts) - 1),
            (
                pltpu.VMEM((1, 128), F32),
                pltpu.HBM((128, 128), F32),
                pltpu.HBM((16, 128, 2 * HEAD_DIM), BF16),
            ),
            *tables,
            *raws,
            specs=[VMEM] * len(tables) + [HBM] * len(raws),
            vmem=4,
            scratch=[
                pltpu.VMEM((len(raws), 128, 384), F32),
                pltpu.VMEM((128, 128), F32),
                pltpu.VMEM((128, 2 * HEAD_DIM), BF16),
                pltpu.SemaphoreType.DMA((17,)),
            ],
        )
        kv_all = lax.all_to_all(kv, SEQ, split_axis=0, concat_axis=0, tiled=True)
        q = query_dot(share, parts, w_query)
        if k == ITERS - 1:
            home = call(
                pack_kernel,
                [pltpu.HBM((2, 3, 16, 640), F32)] * 4,
                *images,
                specs=[HBM] * 3,
                scratch=[pltpu.VMEM((3, 16, D), F32), pltpu.SemaphoreType.DMA((27,))],
            )
        if k in (0, ITERS - 1):
            home = move_home(home)
            kv_all, home = lax.optimization_barrier((kv_all, home))
        if k == 0:
            inj, current = call(settle_kernel, (narrow, narrow), *home)
        if k == ITERS - 1:
            settled = home
        if k > 1:
            current = call(mix_kernel, wide, share, *images)
        own, send = call(
            attend_kernel,
            (pltpu.VMEM((64, D), F32), pltpu.VMEM((64, D), BF16)),
            q,
            scale,
            kv_all,
            w_out,
            specs=[VMEM, HBM, VMEM, HBM],
            vmem=16,
            scratch=[
                pltpu.VMEM((640, D), BF16),
                pltpu.VMEM((128, 128), F32),
                pltpu.VMEM((128, 640), BF16),
                pltpu.SemaphoreType.DMA((2,)),
            ],
            flops=2 * 128 * 640 * (2 * TOKENS + D),
            touched=9_000_000,
        )
        pair = own + lax.ppermute(send, "c", shift(2, 1)).astype(F32)
        arrived = [
            lax.ppermute(pair[16 * by : 16 * by + 16].astype(BF16), "y", shift(4, -by))
            for by in (1, 2, 3)
        ]
        shapes = [tokens, tokens] + ([home_wide] * 4 if k == ITERS - 1 else [])
        if k < ITERS - 1:
            shapes.append(narrow)
        if k > 0:
            shapes.append(pltpu.HBM((128, 1, 128), F32))
        outs = call(
            functools.partial(finish_kernel, k),
            tuple(shapes),
            pair[:16],
            *arrived,
            inj,
            current,
            gain_out,
            gain_in,
            *residuals,
            scratch=[
                pltpu.VMEM((16, D), F32),
                pltpu.VMEM((16, D), F32),
                pltpu.VMEM((128, 1, 128), F32),
                pltpu.SemaphoreType.DMA((11,)),
            ],
        )
        images.append(outs[0])
        residuals.append(outs[1])
        home = outs[2:6]
        payload = outs[2]
        if k == 0:
            current = outs[0]
        else:
            dots = outs[-1]
    settled = settled + move_home(home)
    tables.append(lax.all_to_all(dots, EVERY, split_axis=0, concat_axis=0, tiled=True))
    return call(
        functools.partial(last_kernel, ITERS - 1),
        pltpu.HBM((128, 640), F32),
        *tables,
        *settled,
        scratch=[pltpu.VMEM((128, 640), F32), pltpu.SemaphoreType.DMA],
    )


def solution(mesh):
    split = Mesh(mesh.devices.reshape(4, 4, 4, 2), EVERY)
    placed = (
        P(SEQ, FEAT),
        P(SEQ, FEAT),
        P(),
        P(),
        P(None, FEAT),
        P(None, FEAT),
        P(None, FEAT),
        P(FEAT, None),
    )
    return jax.shard_map(
        on_device, mesh=split, in_specs=placed, out_specs=P(SEQ, FEAT), check_vma=False
    )
```

profile of v0, /device:TPU:1, one launch (start us, length us, event | category | flops | bytes accessed | tf_op | source)
XLA Modules:
  0.0 317.8 jit_solution(4626666584417838727)
XLA Ops:
  1.1 3.6 %collective-permute-start.2 = (bf16[128,640]{1,0:T(8,128)(2,1)S(1)}, bf16[128,640]{1,0:T(8,128)(2,1)S(1)}, u32[]{:S(2)}, u32[]{:S(2)}) collective-permute-start(bf16[128,640]{1,0:T(8,128)(2,1)S(1)} %get-tuple-element.72), channel_id=1, source_target_pairs={{0,6},{2,0},{4,2},{6,4},{1,7},{3,1},{5,3},{7,5},{8,14},{10,8},{12,... | collective-permute-start | bytes 491528 | tf_op jit(solution)/shard_map/ppermute | solution.py:479
  5.8 5.4 %collective-permute-done.2 = bf16[128,640]{1,0:T(8,128)(2,1)S(1)} collective-permute-done((bf16[128,640]{1,0:T(8,128)(2,1)S(1)}, bf16[128,640]{1,0:T(8,128)(2,1)S(1)}, u32[]{:S(2)}, u32[]{:S(2)}) %collective-permute-start.2) | collective-permute-done | bytes 163872 | tf_op jit(solution)/shard_map/ppermute | solution.py:479
  11.2 4.7 %collective-permute-done = bf16[128,640]{1,0:T(8,128)(2,1)S(1)} collective-permute-done((bf16[128,640]{1,0:T(8,128)(2,1)S(1)}, bf16[128,640]{1,0:T(8,128)(2,1)S(1)}, u32[]{:S(2)}, u32[]{:S(2)}) %collective-permute-start) | collective-permute-done | bytes 163872 | tf_op jit(solution)/shard_map/ppermute | solution.py:479
  18.3 3.5 %shard_map.83 = (bf16[128,5120]{1,0:T(8,128)(2,1)}, f32[128,384]{1,0:T(8,128)}) custom-call(bf16[5120,128]{1,0:T(8,128)(2,1)} %refs_0_.5, bf16[5120,128]{1,0:T(8,128)(2,1)} %refs_1_.9, f32[1,5120]{1,0:T(1,128)S(1)} %bitcast.7, bf16[4,128,640]{2,1,0:T(8,128)(2,1)S(1)} %pad_maximum_fusion.refs_0_, bf16[4,128,640]{2,1,0:T(8,128)(2,1)S(1)} %collective-permute-done.3.refs_1_), custom_call_target="tpu_custom_call" | custom-call | flops 335544320 | bytes 4000000 | tf_op jit(solution)/shard_map/pallas_call | solution.py:43
  23.9 7.6 %all-to-all-start = ((bf16[16,128,256]{2,1,0:T(8,128)(2,1)}), bf16[16,128,256]{2,1,0:T(8,128)(2,1)S(1)}, u32[]{:S(2)}, u32[]{:S(2)}) async-start(bf16[16,128,256]{2,1,0:T(8,128)(2,1)} %get-tuple-element.77), calls=%async_computation | async-start | bytes 2097152 | tf_op jit(solution)/shard_map/all_to_all | solution.py:539
  40.2 5.5 %shard_map.85.q_ref = bf16[128,640]{1,0:T(8,128)(2,1)S(1)} custom-call(f32[1,128]{1,0:T(1,128)S(1)} %get-tuple-element.74.share_ref, bf16[128,5120]{1,0:T(8,128)(2,1)} %get-tuple-element.75.refs_0_, bf16[5120,640]{1,0:T(8,128)(2,1)} %refs_3_.1), custom_call_target="tpu_custom_call" | custom-call | flops 838860800 | bytes 8000000 | tf_op jit(solution)/shard_map/pallas_call | solution.py:211
  47.2 6.6 %shard_map.86 = (f32[64,5120]{1,0:T(8,128)S(1)}, bf16[64,5120]{1,0:T(8,128)(2,1)S(1)}) custom-call(bf16[128,640]{1,0:T(8,128)(2,1)S(1)} %shard_map.85.q_ref, f32[128,128]{1,0:T(8,128)} %get-tuple-element.76.scale_hbm, bf16[16,128,256]{2,1,0:T(8,128)(2,1)S(1)} %all-to-all-done.kv_ref, bf16[640,5120]{1,0:T(8,128)(2,1)} %w_ref.7), custom_call_target="tpu_custom_call" | custom-call | flops 1509949440 | bytes 9000000 | tf_op jit(solution)/shard_map/pallas_call | solution.py:43
  53.8 3.2 %collective-permute-start.8 = (bf16[64,5120]{1,0:T(8,128)(2,1)S(1)}, bf16[64,5120]{1,0:T(8,128)(2,1)S(1)}, u32[]{:S(2)}, u32[]{:S(2)}) collective-permute-start(bf16[64,5120]{1,0:T(8,128)(2,1)S(1)} %get-tuple-element.84), channel_id=1, source_target_pairs={{0,1},{1,0},{2,3},{3,2},{4,5},{5,4},{6,7},{7,6},{8,9},{9,8},{10,11... | collective-permute-start | bytes 1966088 | tf_op jit(solution)/shard_map/ppermute | solution.py:576
  60.5 3.8 %collective-permute-done.9.a_ref = bf16[16,5120]{1,0:T(8,128)(2,1)S(1)} collective-permute-done((bf16[16,5120]{1,0:T(8,128)(2,1)S(1)}, bf16[16,5120]{1,0:T(8,128)(2,1)S(1)}, u32[]{:S(2)}, u32[]{:S(2)}) %collective-permute-start.9) | collective-permute-done | bytes 163872 | tf_op jit(solution)/shard_map/ppermute | solution.py:578
  66.0 4.5 %collective-permute-done.11.d_ref = bf16[16,5120]{1,0:T(8,128)(2,1)S(1)} collective-permute-done((bf16[16,5120]{1,0:T(8,128)(2,1)S(1)}, bf16[16,5120]{1,0:T(8,128)(2,1)S(1)}, u32[]{:S(2)}, u32[]{:S(2)}) %collective-permute-start.11) | collective-permute-done | bytes 163872 | tf_op jit(solution)/shard_map/ppermute | solution.py:578
  74.6 7.4 %collective-permute-done.12 = bf16[16,5120]{1,0:T(8,128)(2,1)S(1)} collective-permute-done((bf16[16,5120]{1,0:T(8,128)(2,1)S(1)}, bf16[16,5120]{1,0:T(8,128)(2,1)S(1)}, u32[]{:S(2)}, u32[]{:S(2)}) %collective-permute-start.12) | collective-permute-done | bytes 163872 | tf_op jit(solution)/shard_map/ppermute | solution.py:479
  85.6 3.0 shard_map.89
  90.8 3.7 %all-to-all-start.1 = ((bf16[16,128,256]{2,1,0:T(8,128)(2,1)}), bf16[16,128,256]{2,1,0:T(8,128)(2,1)S(1)}, u32[]{:S(2)}, u32[]{:S(2)}) async-start(bf16[16,128,256]{2,1,0:T(8,128)(2,1)} %get-tuple-element.97), calls=%async_computation.1 | async-start | bytes 2097152 | tf_op jit(solution)/shard_map/all_to_all | solution.py:539
  94.5 5.5 %shard_map.91.q_ref = bf16[128,640]{1,0:T(8,128)(2,1)S(1)} custom-call(f32[1,128]{1,0:T(1,128)S(1)} %get-tuple-element.94.share_ref, bf16[128,5120]{1,0:T(8,128)(2,1)} %get-tuple-element.95.refs_0_.refs_3_, bf16[5120,640]{1,0:T(8,128)(2,1)} %refs_3_.1), custom_call_target="tpu_custom_call" | custom-call | flops 838860800 | bytes 8000000 | tf_op jit(solution)/shard_map/pallas_call | solution.py:211
  100.0 10.6 %all-to-all-done.1.kv_ref = bf16[16,128,256]{2,1,0:T(8,128)(2,1)S(1)} async-done(((bf16[16,128,256]{2,1,0:T(8,128)(2,1)}), bf16[16,128,256]{2,1,0:T(8,128)(2,1)S(1)}, u32[]{:S(2)}, u32[]{:S(2)}) %all-to-all-start.1) | async-done | bytes 1048608 | tf_op jit(solution)/shard_map/all_to_all | solution.py:539
  110.6 6.6 %shard_map.92 = (f32[64,5120]{1,0:T(8,128)S(1)}, bf16[64,5120]{1,0:T(8,128)(2,1)S(1)}) custom-call(bf16[128,640]{1,0:T(8,128)(2,1)S(1)} %shard_map.91.q_ref, f32[128,128]{1,0:T(8,128)} %get-tuple-element.96.scale_hbm, bf16[16,128,256]{2,1,0:T(8,128)(2,1)S(1)} %all-to-all-done.1.kv_ref, bf16[640,5120]{1,0:T(8,128)(2,1)} %w_ref.7), custom_call_target="tpu_custom_call" | custom-call | flops 1509949440 | bytes 9000000 | tf_op jit(solution)/shard_map/pallas_call | solution.py:43
  117.2 2.6 collective-permute-start.16
  121.8 2.4 collective-permute-start.17
  124.8 2.9 collective-permute-done.17.a_ref
  127.8 3.1 collective-permute-done.18.b_ref
  130.8 3.9 %collective-permute-done.19.d_ref = bf16[16,5120]{1,0:T(8,128)(2,1)S(1)} collective-permute-done((bf16[16,5120]{1,0:T(8,128)(2,1)S(1)}, bf16[16,5120]{1,0:T(8,128)(2,1)S(1)}, u32[]{:S(2)}, u32[]{:S(2)}) %collective-permute-start.19) | collective-permute-done | bytes 163872 | tf_op jit(solution)/shard_map/ppermute | solution.py:578
  139.0 7.3 %collective-permute-done.20 = bf16[16,5120]{1,0:T(8,128)(2,1)S(1)} collective-permute-done((bf16[16,5120]{1,0:T(8,128)(2,1)S(1)}, bf16[16,5120]{1,0:T(8,128)(2,1)S(1)}, u32[]{:S(2)}, u32[]{:S(2)}) %collective-permute-start.20) | collective-permute-done | bytes 163872 | tf_op jit(solution)/shard_map/ppermute | solution.py:479
  148.3 5.0 %all-to-all-start.2 = ((f32[128,1,128]{2,1,0:T(1,128)}), f32[128,1,128]{2,1,0:T(1,128)S(1)}, u32[]{:S(2)}, u32[]{:S(2)}) async-start(f32[128,1,128]{2,1,0:T(1,128)} %get-tuple-element.102), calls=%async_computation.2 | async-start | bytes 131072 | tf_op jit(solution)/shard_map/all_to_all | solution.py:481
  153.4 3.7 %shard_map.94 = (bf16[128,5120]{1,0:T(8,128)(2,1)}, f32[128,384]{1,0:T(8,128)}) custom-call(bf16[5120,128]{1,0:T(8,128)(2,1)} %refs_0_.5, bf16[5120,128]{1,0:T(8,128)(2,1)} %refs_1_.9, f32[1,5120]{1,0:T(1,128)S(1)} %bitcast.11, bf16[128,5120]{1,0:T(8,128)(2,1)} %get-tuple-element.95.refs_0_.refs_3_, ...), custom_call_target="tpu_custom_call" | custom-call | flops 335544320 | bytes 4000000 | tf_op jit(solution)/shard_map/pallas_call | solution.py:43
  157.1 5.8 %all-to-all-done.2.refs_0_ = f32[128,1,128]{2,1,0:T(1,128)S(1)} async-done(((f32[128,1,128]{2,1,0:T(1,128)}), f32[128,1,128]{2,1,0:T(1,128)S(1)}, u32[]{:S(2)}, u32[]{:S(2)}) %all-to-all-start.2) | async-done | bytes 65568 | tf_op jit(solution)/shard_map/all_to_all | solution.py:481
  162.9 2.4 shard_map.95
  165.2 3.7 %all-to-all-start.3 = ((bf16[16,128,256]{2,1,0:T(8,128)(2,1)}), bf16[16,128,256]{2,1,0:T(8,128)(2,1)S(1)}, u32[]{:S(2)}, u32[]{:S(2)}) async-start(bf16[16,128,256]{2,1,0:T(8,128)(2,1)} %get-tuple-element.108), calls=%async_computation.3 | async-start | bytes 2097152 | tf_op jit(solution)/shard_map/all_to_all | solution.py:539
  168.9 5.9 %shard_map.96.q_ref = bf16[128,640]{1,0:T(8,128)(2,1)S(1)} custom-call(f32[1,128]{1,0:T(1,128)S(1)} %get-tuple-element.105.share_ref, bf16[128,5120]{1,0:T(8,128)(2,1)} %get-tuple-element.95.refs_0_.refs_3_, bf16[128,5120]{1,0:T(8,128)(2,1)} %get-tuple-element.106.refs_1_.refs_4_, bf16[5120,640]{1,0:T(8,128)(2,1)} %refs_3_.1), custom_call_target="tpu_custom_call" | custom-call | flops 838860800 | bytes 8000000 | tf_op jit(solution)/shard_map/pallas_call | solution.py:211
  174.8 9.8 %all-to-all-done.3.kv_ref = bf16[16,128,256]{2,1,0:T(8,128)(2,1)S(1)} async-done(((bf16[16,128,256]{2,1,0:T(8,128)(2,1)}), bf16[16,128,256]{2,1,0:T(8,128)(2,1)S(1)}, u32[]{:S(2)}, u32[]{:S(2)}) %all-to-all-start.3) | async-done | bytes 1048608 | tf_op jit(solution)/shard_map/all_to_all | solution.py:539
  184.6 6.5 %shard_map.97 = (f32[64,5120]{1,0:T(8,128)S(1)}, bf16[64,5120]{1,0:T(8,128)(2,1)S(1)}) custom-call(bf16[128,640]{1,0:T(8,128)(2,1)S(1)} %shard_map.96.q_ref, f32[128,128]{1,0:T(8,128)} %get-tuple-element.107.scale_hbm, bf16[16,128,256]{2,1,0:T(8,128)(2,1)S(1)} %all-to-all-done.3.kv_ref, bf16[640,5120]{1,0:T(8,128)(2,1)} %w_ref.7), custom_call_target="tpu_custom_call" | custom-call | flops 1509949440 | bytes 9000000 | tf_op jit(solution)/shard_map/pallas_call | solution.py:43
  191.1 3.1 collective-permute-start.24
  198.6 3.0 collective-permute-done.25.a_ref
  201.6 2.4 collective-permute-done.26.b_ref
  204.0 4.5 %collective-permute-done.27.d_ref = bf16[16,5120]{1,0:T(8,128)(2,1)S(1)} collective-permute-done((bf16[16,5120]{1,0:T(8,128)(2,1)S(1)}, bf16[16,5120]{1,0:T(8,128)(2,1)S(1)}, u32[]{:S(2)}, u32[]{:S(2)}) %collective-permute-start.27) | collective-permute-done | bytes 163872 | tf_op jit(solution)/shard_map/ppermute | solution.py:578
  213.1 7.0 %collective-permute-done.28 = bf16[16,5120]{1,0:T(8,128)(2,1)S(1)} collective-permute-done((bf16[16,5120]{1,0:T(8,128)(2,1)S(1)}, bf16[16,5120]{1,0:T(8,128)(2,1)S(1)}, u32[]{:S(2)}, u32[]{:S(2)}) %collective-permute-start.28) | collective-permute-done | bytes 163872 | tf_op jit(solution)/shard_map/ppermute | solution.py:479
  222.1 5.1 %all-to-all-start.4 = ((f32[128,1,128]{2,1,0:T(1,128)}), f32[128,1,128]{2,1,0:T(1,128)S(1)}, u32[]{:S(2)}, u32[]{:S(2)}) async-start(f32[128,1,128]{2,1,0:T(1,128)} %get-tuple-element.113), calls=%async_computation.4 | async-start | bytes 131072 | tf_op jit(solution)/shard_map/all_to_all | solution.py:481
  227.2 4.8 %shard_map.100 = (bf16[128,5120]{1,0:T(8,128)(2,1)}, f32[128,384]{1,0:T(8,128)}) custom-call(bf16[5120,128]{1,0:T(8,128)(2,1)} %refs_0_.5, bf16[5120,128]{1,0:T(8,128)(2,1)} %refs_1_.9, f32[1,5120]{1,0:T(1,128)S(1)} %bitcast.13, bf16[128,5120]{1,0:T(8,128)(2,1)} %get-tuple-element.95.refs_0_.refs_3_, bf16[128,5120]{1,0:T(8,128)(2,1)} %get-tuple-element.106.refs_1_.refs_4_, ...), custom_call_target="tpu_custom_call" | custom-call | flops 335544320 | bytes 4000000 | tf_op jit(solution)/shard_map/pallas_call | solution.py:43
  232.0 4.7 %all-to-all-done.4.refs_1_ = f32[128,1,128]{2,1,0:T(1,128)S(1)} async-done(((f32[128,1,128]{2,1,0:T(1,128)}), f32[128,1,128]{2,1,0:T(1,128)S(1)}, u32[]{:S(2)}, u32[]{:S(2)}) %all-to-all-start.4) | async-done | bytes 65568 | tf_op jit(solution)/shard_map/all_to_all | solution.py:481
  236.7 2.5 shard_map.101
  239.3 3.7 %all-to-all-start.5 = ((bf16[16,128,256]{2,1,0:T(8,128)(2,1)}), bf16[16,128,256]{2,1,0:T(8,128)(2,1)S(1)}, u32[]{:S(2)}, u32[]{:S(2)}) async-start(bf16[16,128,256]{2,1,0:T(8,128)(2,1)} %get-tuple-element.119), calls=%async_computation.5 | async-start | bytes 2097152 | tf_op jit(solution)/shard_map/all_to_all | solution.py:539
  248.5 3.5 %collective-permute-done.34.refs_6_ = f32[2,3,16,640]{3,2,1,0:T(8,128)S(1)} collective-permute-done((f32[2,3,16,640]{3,2,1,0:T(8,128)}, f32[2,3,16,640]{3,2,1,0:T(8,128)S(1)}, u32[]{:S(2)}, u32[]{:S(2)}) %collective-permute-start.34) | collective-permute-done | bytes 245792 | tf_op jit(solution)/shard_map/ppermute | solution.py:442
  252.1 2.8 collective-permute-done.33.refs_5_
  254.9 6.5 %collective-permute-done.32.refs_4_ = f32[2,3,16,640]{3,2,1,0:T(8,128)S(1)} collective-permute-done((f32[2,3,16,640]{3,2,1,0:T(8,128)}, f32[2,3,16,640]{3,2,1,0:T(8,128)S(1)}, u32[]{:S(2)}, u32[]{:S(2)}) %collective-permute-start.32) | collective-permute-done | bytes 245792 | tf_op jit(solution)/shard_map/ppermute | solution.py:442
  262.0 6.2 %shard_map.102.q_ref = bf16[128,640]{1,0:T(8,128)(2,1)S(1)} custom-call(f32[1,128]{1,0:T(1,128)S(1)} %get-tuple-element.116.share_ref, bf16[128,5120]{1,0:T(8,128)(2,1)} %get-tuple-element.95.refs_0_.refs_3_, bf16[128,5120]{1,0:T(8,128)(2,1)} %get-tuple-element.106.refs_1_.refs_4_, bf16[128,5120]{1,0:T(8,128)(2,1)} %get-tuple-element.117.refs_2_, ...), custom_call_target="tpu_custom_call" | custom-call | flops 838860800 | bytes 8000000 | tf_op jit(solution)/shard_map/pallas_call | solution.py:211
  268.3 6.5 %shard_map.104 = (f32[64,5120]{1,0:T(8,128)S(1)}, bf16[64,5120]{1,0:T(8,128)(2,1)S(1)}) custom-call(bf16[128,640]{1,0:T(8,128)(2,1)S(1)} %shard_map.102.q_ref, f32[128,128]{1,0:T(8,128)} %get-tuple-element.118.scale_hbm, bf16[16,128,256]{2,1,0:T(8,128)(2,1)S(1)} %all-to-all-done.5.kv_ref, bf16[640,5120]{1,0:T(8,128)(2,1)} %w_ref.7), custom_call_target="tpu_custom_call" | custom-call | flops 1509949440 | bytes 9000000 | tf_op jit(solution)/shard_map/pallas_call | solution.py:43
  279.2 3.7 %collective-permute-done.37.a_ref = bf16[16,5120]{1,0:T(8,128)(2,1)S(1)} collective-permute-done((bf16[16,5120]{1,0:T(8,128)(2,1)S(1)}, bf16[16,5120]{1,0:T(8,128)(2,1)S(1)}, u32[]{:S(2)}, u32[]{:S(2)}) %collective-permute-start.37) | collective-permute-done | bytes 163872 | tf_op jit(solution)/shard_map/ppermute | solution.py:578
  284.5 4.2 %collective-permute-done.39.d_ref = bf16[16,5120]{1,0:T(8,128)(2,1)S(1)} collective-permute-done((bf16[16,5120]{1,0:T(8,128)(2,1)S(1)}, bf16[16,5120]{1,0:T(8,128)(2,1)S(1)}, u32[]{:S(2)}, u32[]{:S(2)}) %collective-permute-start.39) | collective-permute-done | bytes 163872 | tf_op jit(solution)/shard_map/ppermute | solution.py:578
  298.9 16.8 %all_to_all.35.refs_2_ = f32[128,1,128]{2,1,0:T(1,128)S(1)} all-to-all(f32[128,1,128]{2,1,0:T(1,128)} %get-tuple-element.129), channel_id=1, replica_groups=mesh['x'=4,'z'=4,'y'=4,'c'=2] {'x','z','y','c'}, dimensions={0} | all-to-all | bytes 131072 | tf_op jit(solution)/shard_map/all_to_all | solution.py:612
  (143 shorter events, 75.9 us)
Async XLA Ops:
  1.1 10.1 %collective-permute-start.2 = (bf16[128,640]{1,0:T(8,128)(2,1)S(1)}, bf16[128,640]{1,0:T(8,128)(2,1)S(1)}, u32[]{:S(2)}, u32[]{:S(2)}) collective-permute-start(bf16[128,640]{1,0:T(8,128)(2,1)S(1)} %get-tuple-element.72), channel_id=1, source_target_pairs={{0,6},{2,0},{4,2},{6,4},{1,7},{3,1},{5,3},{7,5},{8,14},{10,8},{12,... | collective-permute-start | bytes 491528 | tf_op jit(solution)/shard_map/ppermute | solution.py:479
  4.7 6.4 %collective-permute-start.1 = (bf16[128,640]{1,0:T(8,128)(2,1)S(1)}, bf16[128,640]{1,0:T(8,128)(2,1)S(1)}, u32[]{:S(2)}, u32[]{:S(2)}) collective-permute-start(bf16[128,640]{1,0:T(8,128)(2,1)S(1)} %get-tuple-element.72), channel_id=1, source_target_pairs={{0,4},{2,6},{4,0},{6,2},{1,5},{3,7},{5,1},{7,3},{8,12},{10,14},{12... | collective-permute-start | bytes 491528 | tf_op jit(solution)/shard_map/ppermute | solution.py:479
  5.1 10.8 %collective-permute-start = (bf16[128,640]{1,0:T(8,128)(2,1)S(1)}, bf16[128,640]{1,0:T(8,128)(2,1)S(1)}, u32[]{:S(2)}, u32[]{:S(2)}) collective-permute-start(bf16[128,640]{1,0:T(8,128)(2,1)S(1)} %get-tuple-element.72), channel_id=1, source_target_pairs={{0,2},{2,4},{4,6},{6,0},{1,3},{3,5},{5,7},{7,1},{8,10},{10,12},{12... | collective-permute-start | bytes 491528 | tf_op jit(solution)/shard_map/ppermute | solution.py:479
  23.9 23.3 %all-to-all-start = ((bf16[16,128,256]{2,1,0:T(8,128)(2,1)}), bf16[16,128,256]{2,1,0:T(8,128)(2,1)S(1)}, u32[]{:S(2)}, u32[]{:S(2)}) async-start(bf16[16,128,256]{2,1,0:T(8,128)(2,1)} %get-tuple-element.77), calls=%async_computation | async-start | bytes 2097152 | tf_op jit(solution)/shard_map/all_to_all | solution.py:539
  31.6 3.4 %collective-permute-start.6 = (bf16[2,2,16,640]{3,2,1,0:T(8,128)(2,1)S(1)}, bf16[2,2,16,640]{3,2,1,0:T(8,128)(2,1)S(1)}, u32[]{:S(2)}, u32[]{:S(2)}) collective-permute-start(bf16[2,2,16,640]{3,2,1,0:T(8,128)(2,1)S(1)} %get-tuple-element.81), channel_id=1, source_target_pairs={{0,6},{2,0},{4,2},{6,4},{1,7},{3,1},{5,3},{7,5},{8,14},{10,8},{12,... | collective-permute-start | bytes 245768 | tf_op jit(solution)/shard_map/ppermute | solution.py:442
  32.0 5.1 %collective-permute-start.5 = (bf16[2,2,16,640]{3,2,1,0:T(8,128)(2,1)S(1)}, bf16[2,2,16,640]{3,2,1,0:T(8,128)(2,1)S(1)}, u32[]{:S(2)}, u32[]{:S(2)}) collective-permute-start(bf16[2,2,16,640]{3,2,1,0:T(8,128)(2,1)S(1)} %get-tuple-element.80), channel_id=1, source_target_pairs={{0,4},{2,6},{4,0},{6,2},{1,5},{3,7},{5,1},{7,3},{8,12},{10,14},{12... | collective-permute-start | bytes 245768 | tf_op jit(solution)/shard_map/ppermute | solution.py:442
  32.3 6.8 %collective-permute-start.4 = (bf16[2,2,16,640]{3,2,1,0:T(8,128)(2,1)S(1)}, bf16[2,2,16,640]{3,2,1,0:T(8,128)(2,1)S(1)}, u32[]{:S(2)}, u32[]{:S(2)}) collective-permute-start(bf16[2,2,16,640]{3,2,1,0:T(8,128)(2,1)S(1)} %get-tuple-element.79), channel_id=1, source_target_pairs={{0,2},{2,4},{4,6},{6,0},{1,3},{3,5},{5,7},{7,1},{8,10},{10,12},{12... | collective-permute-start | bytes 245768 | tf_op jit(solution)/shard_map/ppermute | solution.py:442
  39.1 6.6 %collective-permute-start.7 = (bf16[4,2,16,640]{3,2,1,0:T(8,128)(2,1)S(1)}, bf16[4,2,16,640]{3,2,1,0:T(8,128)(2,1)S(1)}, u32[]{:S(2)}, u32[]{:S(2)}) collective-permute-start(bf16[4,2,16,640]{3,2,1,0:T(8,128)(2,1)S(1)} %pad_maximum_fusion.2), channel_id=1, source_target_pairs={{0,1},{1,0},{2,3},{3,2},{4,5},{5,4},{6,7},{7,6},{8,9},{9,8},{10,11... | collective-permute-start | bytes 491528 | tf_op jit(solution)/shard_map/ppermute | solution.py:444
  53.8 4.9 %collective-permute-start.8 = (bf16[64,5120]{1,0:T(8,128)(2,1)S(1)}, bf16[64,5120]{1,0:T(8,128)(2,1)S(1)}, u32[]{:S(2)}, u32[]{:S(2)}) collective-permute-start(bf16[64,5120]{1,0:T(8,128)(2,1)S(1)} %get-tuple-element.84), channel_id=1, source_target_pairs={{0,1},{1,0},{2,3},{3,2},{4,5},{5,4},{6,7},{7,6},{8,9},{9,8},{10,11... | collective-permute-start | bytes 1966088 | tf_op jit(solution)/shard_map/ppermute | solution.py:576
  58.9 5.5 %collective-permute-start.9 = (bf16[16,5120]{1,0:T(8,128)(2,1)S(1)}, bf16[16,5120]{1,0:T(8,128)(2,1)S(1)}, u32[]{:S(2)}, u32[]{:S(2)}) collective-permute-start(bf16[16,5120]{1,0:T(8,128)(2,1)S(1)} %get-tuple-element.158), channel_id=1, source_target_pairs={{0,6},{2,0},{4,2},{6,4},{1,7},{3,1},{5,3},{7,5},{8,14},{10,8},{12,... | collective-permute-start | bytes 491528 | tf_op jit(solution)/shard_map/ppermute | solution.py:578
  59.3 6.6 %collective-permute-start.10 = (bf16[16,5120]{1,0:T(8,128)(2,1)S(1)}, bf16[16,5120]{1,0:T(8,128)(2,1)S(1)}, u32[]{:S(2)}, u32[]{:S(2)}) collective-permute-start(bf16[16,5120]{1,0:T(8,128)(2,1)S(1)} %get-tuple-element.157), channel_id=1, source_target_pairs={{0,4},{2,6},{4,0},{6,2},{1,5},{3,7},{5,1},{7,3},{8,12},{10,14},{12... | collective-permute-start | bytes 491528 | tf_op jit(solution)/shard_map/ppermute | solution.py:578
  59.6 10.8 %collective-permute-start.11 = (bf16[16,5120]{1,0:T(8,128)(2,1)S(1)}, bf16[16,5120]{1,0:T(8,128)(2,1)S(1)}, u32[]{:S(2)}, u32[]{:S(2)}) collective-permute-start(bf16[16,5120]{1,0:T(8,128)(2,1)S(1)} %get-tuple-element.156), channel_id=1, source_target_pairs={{0,2},{2,4},{4,6},{6,0},{1,3},{3,5},{5,7},{7,1},{8,10},{10,12},{12... | collective-permute-start | bytes 491528 | tf_op jit(solution)/shard_map/ppermute | solution.py:578
  71.7 10.3 %collective-permute-start.12 = (bf16[16,5120]{1,0:T(8,128)(2,1)S(1)}, bf16[16,5120]{1,0:T(8,128)(2,1)S(1)}, u32[]{:S(2)}, u32[]{:S(2)}) collective-permute-start(bf16[16,5120]{1,0:T(8,128)(2,1)S(1)} %get-tuple-element.92), channel_id=1, source_target_pairs={{0,2},{2,4},{4,6},{6,0},{1,3},{3,5},{5,7},{7,1},{8,10},{10,12},{12... | collective-permute-start | bytes 491528 | tf_op jit(solution)/shard_map/ppermute | solution.py:479
  71.8 10.2 %collective-permute-start.13 = (bf16[16,5120]{1,0:T(8,128)(2,1)S(1)}, bf16[16,5120]{1,0:T(8,128)(2,1)S(1)}, u32[]{:S(2)}, u32[]{:S(2)}) collective-permute-start(bf16[16,5120]{1,0:T(8,128)(2,1)S(1)} %get-tuple-element.92), channel_id=1, source_target_pairs={{0,4},{2,6},{4,0},{6,2},{1,5},{3,7},{5,1},{7,3},{8,12},{10,14},{12... | collective-permute-start | bytes 491528 | tf_op jit(solution)/shard_map/ppermute | solution.py:479
  72.9 9.4 %collective-permute-start.14 = (bf16[16,5120]{1,0:T(8,128)(2,1)S(1)}, bf16[16,5120]{1,0:T(8,128)(2,1)S(1)}, u32[]{:S(2)}, u32[]{:S(2)}) collective-permute-start(bf16[16,5120]{1,0:T(8,128)(2,1)S(1)} %get-tuple-element.92), channel_id=1, source_target_pairs={{0,6},{2,0},{4,2},{6,4},{1,7},{3,1},{5,3},{7,5},{8,14},{10,8},{12,... | collective-permute-start | bytes 491528 | tf_op jit(solution)/shard_map/ppermute | solution.py:479
  82.2 3.4 %collective-permute-start.15 = (bf16[64,5120]{1,0:T(8,128)(2,1)S(1)}, bf16[64,5120]{1,0:T(8,128)(2,1)S(1)}, u32[]{:S(2)}, u32[]{:S(2)}) collective-permute-start(bf16[64,5120]{1,0:T(8,128)(2,1)S(1)} %constant_dynamic-update-slice_fusion.refs_3_), channel_id=1, source_target_pairs={{0,1},{1,0},{2,3},{3,2},{4,5},{5,4},{6,7},{7,6},{8,9},{9,8},{10,11... | collective-permute-start | bytes 1966088 | tf_op jit(solution)/shard_map/ppermute | solution.py:483
  90.8 19.8 %all-to-all-start.1 = ((bf16[16,128,256]{2,1,0:T(8,128)(2,1)}), bf16[16,128,256]{2,1,0:T(8,128)(2,1)S(1)}, u32[]{:S(2)}, u32[]{:S(2)}) async-start(bf16[16,128,256]{2,1,0:T(8,128)(2,1)} %get-tuple-element.97), calls=%async_computation.1 | async-start | bytes 2097152 | tf_op jit(solution)/shard_map/all_to_all | solution.py:539
  117.2 4.3 %collective-permute-start.16 = (bf16[64,5120]{1,0:T(8,128)(2,1)S(1)}, bf16[64,5120]{1,0:T(8,128)(2,1)S(1)}, u32[]{:S(2)}, u32[]{:S(2)}) collective-permute-start(bf16[64,5120]{1,0:T(8,128)(2,1)S(1)} %get-tuple-element.99), channel_id=1, source_target_pairs={{0,1},{1,0},{2,3},{3,2},{4,5},{5,4},{6,7},{7,6},{8,9},{9,8},{10,11... | collective-permute-start | bytes 1966088 | tf_op jit(solution)/shard_map/ppermute | solution.py:576
  121.8 6.0 %collective-permute-start.17 = (bf16[16,5120]{1,0:T(8,128)(2,1)S(1)}, bf16[16,5120]{1,0:T(8,128)(2,1)S(1)}, u32[]{:S(2)}, u32[]{:S(2)}) collective-permute-start(bf16[16,5120]{1,0:T(8,128)(2,1)S(1)} %get-tuple-element.155), channel_id=1, source_target_pairs={{0,6},{2,0},{4,2},{6,4},{1,7},{3,1},{5,3},{7,5},{8,14},{10,8},{12,... | collective-permute-start | bytes 491528 | tf_op jit(solution)/shard_map/ppermute | solution.py:578
  124.1 6.7 %collective-permute-start.18 = (bf16[16,5120]{1,0:T(8,128)(2,1)S(1)}, bf16[16,5120]{1,0:T(8,128)(2,1)S(1)}, u32[]{:S(2)}, u32[]{:S(2)}) collective-permute-start(bf16[16,5120]{1,0:T(8,128)(2,1)S(1)} %get-tuple-element.154), channel_id=1, source_target_pairs={{0,4},{2,6},{4,0},{6,2},{1,5},{3,7},{5,1},{7,3},{8,12},{10,14},{12... | collective-permute-start | bytes 491528 | tf_op jit(solution)/shard_map/ppermute | solution.py:578
  124.1 10.6 %collective-permute-start.19 = (bf16[16,5120]{1,0:T(8,128)(2,1)S(1)}, bf16[16,5120]{1,0:T(8,128)(2,1)S(1)}, u32[]{:S(2)}, u32[]{:S(2)}) collective-permute-start(bf16[16,5120]{1,0:T(8,128)(2,1)S(1)} %get-tuple-element.153), channel_id=1, source_target_pairs={{0,2},{2,4},{4,6},{6,0},{1,3},{3,5},{5,7},{7,1},{8,10},{10,12},{12... | collective-permute-start | bytes 491528 | tf_op jit(solution)/shard_map/ppermute | solution.py:578
  136.1 10.2 %collective-permute-start.20 = (bf16[16,5120]{1,0:T(8,128)(2,1)S(1)}, bf16[16,5120]{1,0:T(8,128)(2,1)S(1)}, u32[]{:S(2)}, u32[]{:S(2)}) collective-permute-start(bf16[16,5120]{1,0:T(8,128)(2,1)S(1)} %get-tuple-element.103), channel_id=1, source_target_pairs={{0,2},{2,4},{4,6},{6,0},{1,3},{3,5},{5,7},{7,1},{8,10},{10,12},{12... | collective-permute-start | bytes 491528 | tf_op jit(solution)/shard_map/ppermute | solution.py:479
  136.2 10.1 %collective-permute-start.21 = (bf16[16,5120]{1,0:T(8,128)(2,1)S(1)}, bf16[16,5120]{1,0:T(8,128)(2,1)S(1)}, u32[]{:S(2)}, u32[]{:S(2)}) collective-permute-start(bf16[16,5120]{1,0:T(8,128)(2,1)S(1)} %get-tuple-element.103), channel_id=1, source_target_pairs={{0,4},{2,6},{4,0},{6,2},{1,5},{3,7},{5,1},{7,3},{8,12},{10,14},{12... | collective-permute-start | bytes 491528 | tf_op jit(solution)/shard_map/ppermute | solution.py:479
  137.4 9.0 %collective-permute-start.22 = (bf16[16,5120]{1,0:T(8,128)(2,1)S(1)}, bf16[16,5120]{1,0:T(8,128)(2,1)S(1)}, u32[]{:S(2)}, u32[]{:S(2)}) collective-permute-start(bf16[16,5120]{1,0:T(8,128)(2,1)S(1)} %get-tuple-element.103), channel_id=1, source_target_pairs={{0,6},{2,0},{4,2},{6,4},{1,7},{3,1},{5,3},{7,5},{8,14},{10,8},{12,... | collective-permute-start | bytes 491528 | tf_op jit(solution)/shard_map/ppermute | solution.py:479
  146.4 7.0 %collective-permute-start.23 = (bf16[64,5120]{1,0:T(8,128)(2,1)S(1)}, bf16[64,5120]{1,0:T(8,128)(2,1)S(1)}, u32[]{:S(2)}, u32[]{:S(2)}) collective-permute-start(bf16[64,5120]{1,0:T(8,128)(2,1)S(1)} %constant_dynamic-update-slice_fusion.4.refs_4_), channel_id=1, source_target_pairs={{0,1},{1,0},{2,3},{3,2},{4,5},{5,4},{6,7},{7,6},{8,9},{9,8},{10,11... | collective-permute-start | bytes 1966088 | tf_op jit(solution)/shard_map/ppermute | solution.py:483
  148.3 14.5 %all-to-all-start.2 = ((f32[128,1,128]{2,1,0:T(1,128)}), f32[128,1,128]{2,1,0:T(1,128)S(1)}, u32[]{:S(2)}, u32[]{:S(2)}) async-start(f32[128,1,128]{2,1,0:T(1,128)} %get-tuple-element.102), calls=%async_computation.2 | async-start | bytes 131072 | tf_op jit(solution)/shard_map/all_to_all | solution.py:481
  165.2 19.3 %all-to-all-start.3 = ((bf16[16,128,256]{2,1,0:T(8,128)(2,1)}), bf16[16,128,256]{2,1,0:T(8,128)(2,1)S(1)}, u32[]{:S(2)}, u32[]{:S(2)}) async-start(bf16[16,128,256]{2,1,0:T(8,128)(2,1)} %get-tuple-element.108), calls=%async_computation.3 | async-start | bytes 2097152 | tf_op jit(solution)/shard_map/all_to_all | solution.py:539
  191.1 4.8 %collective-permute-start.24 = (bf16[64,5120]{1,0:T(8,128)(2,1)S(1)}, bf16[64,5120]{1,0:T(8,128)(2,1)S(1)}, u32[]{:S(2)}, u32[]{:S(2)}) collective-permute-start(bf16[64,5120]{1,0:T(8,128)(2,1)S(1)} %get-tuple-element.110), channel_id=1, source_target_pairs={{0,1},{1,0},{2,3},{3,2},{4,5},{5,4},{6,7},{7,6},{8,9},{9,8},{10,11... | collective-permute-start | bytes 1966088 | tf_op jit(solution)/shard_map/ppermute | solution.py:576
  196.2 5.5 %collective-permute-start.25 = (bf16[16,5120]{1,0:T(8,128)(2,1)S(1)}, bf16[16,5120]{1,0:T(8,128)(2,1)S(1)}, u32[]{:S(2)}, u32[]{:S(2)}) collective-permute-start(bf16[16,5120]{1,0:T(8,128)(2,1)S(1)} %get-tuple-element.152), channel_id=1, source_target_pairs={{0,6},{2,0},{4,2},{6,4},{1,7},{3,1},{5,3},{7,5},{8,14},{10,8},{12,... | collective-permute-start | bytes 491528 | tf_op jit(solution)/shard_map/ppermute | solution.py:578
  197.4 6.6 %collective-permute-start.26 = (bf16[16,5120]{1,0:T(8,128)(2,1)S(1)}, bf16[16,5120]{1,0:T(8,128)(2,1)S(1)}, u32[]{:S(2)}, u32[]{:S(2)}) collective-permute-start(bf16[16,5120]{1,0:T(8,128)(2,1)S(1)} %get-tuple-element.151), channel_id=1, source_target_pairs={{0,4},{2,6},{4,0},{6,2},{1,5},{3,7},{5,1},{7,3},{8,12},{10,14},{12... | collective-permute-start | bytes 491528 | tf_op jit(solution)/shard_map/ppermute | solution.py:578
  198.4 10.1 %collective-permute-start.27 = (bf16[16,5120]{1,0:T(8,128)(2,1)S(1)}, bf16[16,5120]{1,0:T(8,128)(2,1)S(1)}, u32[]{:S(2)}, u32[]{:S(2)}) collective-permute-start(bf16[16,5120]{1,0:T(8,128)(2,1)S(1)} %get-tuple-element.150), channel_id=1, source_target_pairs={{0,2},{2,4},{4,6},{6,0},{1,3},{3,5},{5,7},{7,1},{8,10},{10,12},{12... | collective-permute-start | bytes 491528 | tf_op jit(solution)/shard_map/ppermute | solution.py:578
  209.9 10.3 %collective-permute-start.28 = (bf16[16,5120]{1,0:T(8,128)(2,1)S(1)}, bf16[16,5120]{1,0:T(8,128)(2,1)S(1)}, u32[]{:S(2)}, u32[]{:S(2)}) collective-permute-start(bf16[16,5120]{1,0:T(8,128)(2,1)S(1)} %get-tuple-element.114), channel_id=1, source_target_pairs={{0,2},{2,4},{4,6},{6,0},{1,3},{3,5},{5,7},{7,1},{8,10},{10,12},{12... | collective-permute-start | bytes 491528 | tf_op jit(solution)/shard_map/ppermute | solution.py:479
  210.0 10.2 %collective-permute-start.29 = (bf16[16,5120]{1,0:T(8,128)(2,1)S(1)}, bf16[16,5120]{1,0:T(8,128)(2,1)S(1)}, u32[]{:S(2)}, u32[]{:S(2)}) collective-permute-start(bf16[16,5120]{1,0:T(8,128)(2,1)S(1)} %get-tuple-element.114), channel_id=1, source_target_pairs={{0,4},{2,6},{4,0},{6,2},{1,5},{3,7},{5,1},{7,3},{8,12},{10,14},{12... | collective-permute-start | bytes 491528 | tf_op jit(solution)/shard_map/ppermute | solution.py:479
  211.1 9.3 %collective-permute-start.30 = (bf16[16,5120]{1,0:T(8,128)(2,1)S(1)}, bf16[16,5120]{1,0:T(8,128)(2,1)S(1)}, u32[]{:S(2)}, u32[]{:S(2)}) collective-permute-start(bf16[16,5120]{1,0:T(8,128)(2,1)S(1)} %get-tuple-element.114), channel_id=1, source_target_pairs={{0,6},{2,0},{4,2},{6,4},{1,7},{3,1},{5,3},{7,5},{8,14},{10,8},{12,... | collective-permute-start | bytes 491528 | tf_op jit(solution)/shard_map/ppermute | solution.py:479
  220.4 6.8 %collective-permute-start.31 = (bf16[64,5120]{1,0:T(8,128)(2,1)S(1)}, bf16[64,5120]{1,0:T(8,128)(2,1)S(1)}, u32[]{:S(2)}, u32[]{:S(2)}) collective-permute-start(bf16[64,5120]{1,0:T(8,128)(2,1)S(1)} %constant_dynamic-update-slice_fusion.8.refs_5_), channel_id=1, source_target_pairs={{0,1},{1,0},{2,3},{3,2},{4,5},{5,4},{6,7},{7,6},{8,9},{9,8},{10,11... | collective-permute-start | bytes 1966088 | tf_op jit(solution)/shard_map/ppermute | solution.py:483
  222.1 14.7 %all-to-all-start.4 = ((f32[128,1,128]{2,1,0:T(1,128)}), f32[128,1,128]{2,1,0:T(1,128)S(1)}, u32[]{:S(2)}, u32[]{:S(2)}) async-start(f32[128,1,128]{2,1,0:T(1,128)} %get-tuple-element.113), calls=%async_computation.4 | async-start | bytes 131072 | tf_op jit(solution)/shard_map/all_to_all | solution.py:481
  239.3 29.0 %all-to-all-start.5 = ((bf16[16,128,256]{2,1,0:T(8,128)(2,1)}), bf16[16,128,256]{2,1,0:T(8,128)(2,1)S(1)}, u32[]{:S(2)}, u32[]{:S(2)}) async-start(bf16[16,128,256]{2,1,0:T(8,128)(2,1)} %get-tuple-element.119), calls=%async_computation.5 | async-start | bytes 2097152 | tf_op jit(solution)/shard_map/all_to_all | solution.py:539
  245.2 6.9 %collective-permute-start.34 = (f32[2,3,16,640]{3,2,1,0:T(8,128)}, f32[2,3,16,640]{3,2,1,0:T(8,128)S(1)}, u32[]{:S(2)}, u32[]{:S(2)}) collective-permute-start(f32[2,3,16,640]{3,2,1,0:T(8,128)} %get-tuple-element.124), channel_id=1, source_target_pairs={{0,6},{2,0},{4,2},{6,4},{1,7},{3,1},{5,3},{7,5},{8,14},{10,8},{12,... | collective-permute-start | bytes 737288 | tf_op jit(solution)/shard_map/ppermute | solution.py:442
  246.6 8.3 %collective-permute-start.33 = (f32[2,3,16,640]{3,2,1,0:T(8,128)}, f32[2,3,16,640]{3,2,1,0:T(8,128)S(1)}, u32[]{:S(2)}, u32[]{:S(2)}) collective-permute-start(f32[2,3,16,640]{3,2,1,0:T(8,128)} %get-tuple-element.123), channel_id=1, source_target_pairs={{0,4},{2,6},{4,0},{6,2},{1,5},{3,7},{5,1},{7,3},{8,12},{10,14},{12... | collective-permute-start | bytes 737288 | tf_op jit(solution)/shard_map/ppermute | solution.py:442
  247.4 14.0 %collective-permute-start.32 = (f32[2,3,16,640]{3,2,1,0:T(8,128)}, f32[2,3,16,640]{3,2,1,0:T(8,128)S(1)}, u32[]{:S(2)}, u32[]{:S(2)}) collective-permute-start(f32[2,3,16,640]{3,2,1,0:T(8,128)} %get-tuple-element.122), channel_id=1, source_target_pairs={{0,2},{2,4},{4,6},{6,0},{1,3},{3,5},{5,7},{7,1},{8,10},{10,12},{12... | collective-permute-start | bytes 737288 | tf_op jit(solution)/shard_map/ppermute | solution.py:442
  261.5 6.8 %collective-permute-start.35 = (f32[4,3,16,640]{3,2,1,0:T(8,128)S(1)}, f32[4,3,16,640]{3,2,1,0:T(8,128)S(1)}, u32[]{:S(2)}, u32[]{:S(2)}) collective-permute-start(f32[4,3,16,640]{3,2,1,0:T(8,128)S(1)} %pad_maximum_fusion.1), channel_id=1, source_target_pairs={{0,1},{1,0},{2,3},{3,2},{4,5},{5,4},{6,7},{7,6},{8,9},{9,8},{10,11... | collective-permute-start | bytes 1474568 | tf_op jit(solution)/shard_map/ppermute | solution.py:444
  277.2 5.7 %collective-permute-start.37 = (bf16[16,5120]{1,0:T(8,128)(2,1)S(1)}, bf16[16,5120]{1,0:T(8,128)(2,1)S(1)}, u32[]{:S(2)}, u32[]{:S(2)}) collective-permute-start(bf16[16,5120]{1,0:T(8,128)(2,1)S(1)} %get-tuple-element.149), channel_id=1, source_target_pairs={{0,6},{2,0},{4,2},{6,4},{1,7},{3,1},{5,3},{7,5},{8,14},{10,8},{12,... | collective-permute-start | bytes 491528 | tf_op jit(solution)/shard_map/ppermute | solution.py:578
  277.6 6.9 %collective-permute-start.38 = (bf16[16,5120]{1,0:T(8,128)(2,1)S(1)}, bf16[16,5120]{1,0:T(8,128)(2,1)S(1)}, u32[]{:S(2)}, u32[]{:S(2)}) collective-permute-start(bf16[16,5120]{1,0:T(8,128)(2,1)S(1)} %get-tuple-element.148), channel_id=1, source_target_pairs={{0,4},{2,6},{4,0},{6,2},{1,5},{3,7},{5,1},{7,3},{8,12},{10,14},{12... | collective-permute-start | bytes 491528 | tf_op jit(solution)/shard_map/ppermute | solution.py:578
  278.5 10.3 %collective-permute-start.39 = (bf16[16,5120]{1,0:T(8,128)(2,1)S(1)}, bf16[16,5120]{1,0:T(8,128)(2,1)S(1)}, u32[]{:S(2)}, u32[]{:S(2)}) collective-permute-start(bf16[16,5120]{1,0:T(8,128)(2,1)S(1)} %get-tuple-element.147), channel_id=1, source_target_pairs={{0,2},{2,4},{4,6},{6,0},{1,3},{3,5},{5,7},{7,1},{8,10},{10,12},{12... | collective-permute-start | bytes 491528 | tf_op jit(solution)/shard_map/ppermute | solution.py:578
  290.2 3.6 %collective-permute-start.42 = (f32[2,16,640]{2,1,0:T(8,128)}, f32[2,16,640]{2,1,0:T(8,128)S(1)}, u32[]{:S(2)}, u32[]{:S(2)}) collective-permute-start(f32[2,16,640]{2,1,0:T(8,128)} %get-tuple-element.138), channel_id=1, source_target_pairs={{0,6},{2,0},{4,2},{6,4},{1,7},{3,1},{5,3},{7,5},{8,14},{10,8},{12,... | collective-permute-start | bytes 245768 | tf_op jit(solution)/shard_map/ppermute | solution.py:442
  290.4 5.0 %collective-permute-start.41 = (f32[2,16,640]{2,1,0:T(8,128)}, f32[2,16,640]{2,1,0:T(8,128)S(1)}, u32[]{:S(2)}, u32[]{:S(2)}) collective-permute-start(f32[2,16,640]{2,1,0:T(8,128)} %get-tuple-element.137), channel_id=1, source_target_pairs={{0,4},{2,6},{4,0},{6,2},{1,5},{3,7},{5,1},{7,3},{8,12},{10,14},{12... | collective-permute-start | bytes 245768 | tf_op jit(solution)/shard_map/ppermute | solution.py:442
  291.2 5.6 %collective-permute-start.40 = (f32[2,16,640]{2,1,0:T(8,128)}, f32[2,16,640]{2,1,0:T(8,128)S(1)}, u32[]{:S(2)}, u32[]{:S(2)}) collective-permute-start(f32[2,16,640]{2,1,0:T(8,128)} %get-tuple-element.136), channel_id=1, source_target_pairs={{0,2},{2,4},{4,6},{6,0},{1,3},{3,5},{5,7},{7,1},{8,10},{10,12},{12... | collective-permute-start | bytes 245768 | tf_op jit(solution)/shard_map/ppermute | solution.py:442
  296.9 18.8 %collective-permute-start.43 = (f32[4,16,640]{2,1,0:T(8,128)S(1)}, f32[4,16,640]{2,1,0:T(8,128)S(1)}, u32[]{:S(2)}, u32[]{:S(2)}) collective-permute-start(f32[4,16,640]{2,1,0:T(8,128)S(1)} %pad_maximum_fusion.3), channel_id=1, source_target_pairs={{0,1},{1,0},{2,3},{3,2},{4,5},{5,4},{6,7},{7,6},{8,9},{9,8},{10,11... | collective-permute-start | bytes 491528 | tf_op jit(solution)/shard_map/ppermute | solution.py:444
  (14 other events, 120.6 us)
where the time goes:
time: 319 us; the launch traced here: 318 us
  waiting for transfers between devices  137 us (43%)
  Pallas kernels  83.7 us (26%)
  starting transfers between devices  75.4 us (24%)
  blocking collectives  16.8 us (5%)
    pallas_call x22, Pallas kernels, call(): pl.pallas_call(kernel, out_shape=outs, in_specs=specs, out_specs=jax.tree...  60.5 us
    ppermute x12, waiting for transfers between devices, on_device(): lax.ppermute(pair[16 * by:16 * by + 16].astype(BF16), 'y', shift(4, -by))  39.2 us
    ppermute x12, waiting for transfers between devices, on_device(): lax.ppermute(payload, 'y', shift(4, by))  32.2 us
    pallas_call x4, Pallas kernels, query_dot(): pl.pallas_call(functools.partial(query_kernel, len(parts) - 1), grid=(5,)...  23.1 us
    ppermute x9, waiting for transfers between devices, move_home(): lax.ppermute(pieces[by], 'y', shift(4, by))  22.8 us
    all_to_all x4, waiting for transfers between devices, on_device(): kv_all = lax.all_to_all(kv, SEQ, split_axis=0, concat_axis=0, tiled=True)  21.9 us
    all_to_all x4, starting transfers between devices, on_device(): kv_all = lax.all_to_all(kv, SEQ, split_axis=0, concat_axis=0, tiled=True)  18.6 us
    all_to_all x1, blocking collectives, on_device(): lax.all_to_all(dots, EVERY, split_axis=0, concat_axis=0, tiled=True)  16.8 us
  transfers between devices with their start and end apart: 50, of which 39 were waited for; matrix products, arithmetic and copies ran while one was open for 1% of the time, Pallas kernels for 11%

commit v1 on v0

--- a/solution.py
+++ b/solution.py
@@ -34,7 +34,7 @@
     return [(at, (at + by) % n) for at in range(n)]
 
 
-def call(kernel, outs, *args, specs=None, scratch=(), vmem=8, flops=0, touched=0):
+def call(kernel, outs, *args, specs=None, scratch=(), vmem=8, flops=0, touched=0, aliases=None):
     specs = [VMEM] * len(args) if specs is None else specs
     args = [
         pltpu.with_memory_space_constraint(arg, pltpu.HBM) if spec is HBM else arg
@@ -44,6 +44,7 @@
         kernel,
         out_shape=outs,
         in_specs=specs,
+        input_output_aliases=aliases or {},
         out_specs=jax.tree.map(lambda out: HBM if out.memory_space == pltpu.HBM else VMEM, outs),
         scratch_shapes=list(scratch),
         compiler_params=pltpu.CompilerParams(vmem_limit_bytes=vmem * 1024 * 1024),
@@ -72,7 +73,7 @@
 
 
 def first_kernel(wk_ref, wv_ref, gain_ref, *refs):
-    pieces, (rows_out, raw_out, rows_ref, held, raw_ref, sem) = refs[:2], refs[2:]
+    pieces, (rows_out, scale_ref, kv_ref, rows_ref, held, kv_held, sem) = refs[:2], refs[2:]
     loads = load_keys(wk_ref, wv_ref, held, sem)
     y, c = lax.axis_index("y"), lax.axis_index("c")
     for half in range(2):
@@ -91,20 +92,28 @@
         return squares + jnp.sum(part * part, axis=1, keepdims=True)
 
     squares = lax.fori_loop(0, 8, one_part, jnp.zeros((128, 1), F32))
-    raw_ref[:, 256:] = jnp.broadcast_to(squares, (128, 128))
     for load in loads:
         load.wait()
-    raw_ref[:, :256] = jnp.dot(rows_ref[...], held[...], preferred_element_type=F32)
-    save = pltpu.make_async_copy(raw_ref, raw_out, sem.at[3])
-    save.start()
-    save.wait()
+    raw = jnp.dot(rows_ref[...], held[...], preferred_element_type=F32)
+    hand_out(raw, squares, scale_ref, kv_ref, kv_held, sem)
     keep.wait()
+
+
+def hand_out(raw, squares, scale_ref, kv_ref, kv_held, sem):
+    scale = lax.rsqrt(squares / D + EPS)
+    kv_held[...] = (raw * scale).astype(BF16)
+    stores = [pltpu.make_async_copy(kv_held, kv_ref.at[at], sem.at[3 + at]) for at in range(16)]
+    for store in stores:
+        store.start()
+    scale_ref[...] = jnp.broadcast_to(scale, (128, 128))
+    for store in stores:
+        store.wait()
 
 
 def project_kernel(k, *refs):
     (wk_ref, wv_ref, gain_ref), refs = refs[:3], refs[3:]
     older_hbm, pieces = refs[:k], refs[k : k + 2]
-    rows_out, raw_out, rows_ref, held, raw_ref, sem, older_ref, older_sem = refs[k + 2 :]
+    rows_out, raw_ref, *hand, rows_ref, held, sem, older_ref, older_sem = refs[k + 2 :]
     for n in range(8):
         for at in range(k):
             columns = slice(640 * n, 640 * n + 640)
@@ -139,46 +148,31 @@
     )
     for load in loads:
         load.wait()
-    raw_ref[:, :256] = jnp.dot(rows_ref[...], held[...], preferred_element_type=F32)
-    save = pltpu.make_async_copy(raw_ref, raw_out, sem.at[3])
-    save.start()
-    save.wait()
+    raw = jnp.dot(rows_ref[...], held[...], preferred_element_type=F32)
+    raw_ref[:, :256] = raw
+    if k == 0:
+        scale_ref, kv_ref, kv_held = hand
+        hand_out(raw, sums[0], scale_ref, kv_ref, kv_held, sem)
     keep.wait()
 
 
 def share_kernel(k, *refs):
-    raw_hbm, (share_ref, scale_out, kv_ref) = refs[k : 2 * k + 1], refs[2 * k + 1 : 2 * k + 4]
-    raws, scale_ref, kv_held, sem = refs[2 * k + 4 :]
-    loads = [
-        pltpu.make_async_copy(raw, raws.at[at], sem.at[at]) for at, raw in enumerate(raw_hbm)
-    ]
-    for load in loads:
-        load.start()
+    raws, (share_ref, scale_ref, kv_ref, kv_held, sem) = refs[k : 2 * k + 1], refs[2 * k + 1 :]
     shares = mix_shares(k, refs[:k])
     lane = lax.broadcasted_iota(jnp.int32, (1, 128), 1)
     share_ref[...] = functools.reduce(
         lambda a, b: a + b, [jnp.where(lane == at, share, 0.0) for at, share in enumerate(shares)]
     )
-    for load in loads:
-        load.wait()
     squares = jnp.zeros((128, 1), F32)
     for at in range(k + 1):
         for other in range(at + 1):
             twice = 1.0 if other == at else 2.0
-            pair = raws[at, :, 256 + other : 257 + other]
+            pair = raws[at][:, 256 + other : 257 + other]
             squares = squares + (twice * shares[at] * shares[other]) * pair
-    scale = lax.rsqrt(jnp.maximum(squares, 0.0) / D + EPS)
-    scale_ref[...] = jnp.broadcast_to(scale, (128, 128))
-    kv = functools.reduce(
-        lambda a, b: a + b, [share * raws[at, :, :256] for at, share in enumerate(shares)]
-    )
-    kv_held[...] = (kv * scale).astype(BF16)
-    stores = [pltpu.make_async_copy(kv_held, kv_ref.at[at], sem.at[at]) for at in range(16)]
-    stores.append(pltpu.make_async_copy(scale_ref, scale_out, sem.at[16]))
-    for store in stores:
-        store.start()
-    for store in stores:
-        store.wait()
+    raw = functools.reduce(
+        lambda a, b: a + b, [share * raws[at][:, :256] for at, share in enumerate(shares)]
+    )
+    hand_out(raw, jnp.maximum(squares, 0.0), scale_ref, kv_ref, kv_held, sem)
 
 
 def take_share(share_ref, at):
@@ -186,7 +180,9 @@
     return jnp.sum(jnp.where(lane == at, share_ref[...], 0.0), axis=1, keepdims=True)
 
 
-def query_kernel(k, share_ref, *refs):
+def query_kernel(k, *refs):
+    if k > 0:
+        share_ref, refs = refs[0], refs[1:]
     parts, (w_ref, q_ref, acc) = refs[: k + 1], refs[k + 1 :]
 
     @pl.when(pl.program_id(0) == 0)
@@ -212,7 +208,7 @@
         functools.partial(query_kernel, len(parts) - 1),
         grid=(5,),
         out_shape=pltpu.VMEM((128, 640), BF16),
-        in_specs=[pl.BlockSpec((1, 128), lambda n: (0, 0))]
+        in_specs=[pl.BlockSpec((1, 128), lambda n: (0, 0))] * (len(parts) > 1)
         + [pl.BlockSpec((128, 1024), lambda n: (0, n))] * len(parts)
         + [pl.BlockSpec((1024, 640), lambda n: (n, 0))],
         out_specs=pl.BlockSpec((128, 640), lambda n: (0, 0)),
@@ -221,21 +217,18 @@
         cost_estimate=pl.CostEstimate(
             flops=2 * 128 * D * 640, bytes_accessed=8_000_000, transcendentals=0
         ),
-    )(share, *[pltpu.with_memory_space_constraint(part, pltpu.HBM) for part in (*parts, w_query)])
+    )(*([share] if len(parts) > 1 else []), *[pltpu.with_memory_space_constraint(part, pltpu.HBM) for part in (*parts, w_query)])
 
 
 def attend_kernel(
-    q_ref, scale_hbm, kv_ref, w_ref, own_ref, send_ref, w_held, scale_ref, attended, sem
+    q_ref, scale_ref, kv_ref, w_ref, own_ref, send_ref, w_held, attended, sem
 ):
-    small = pltpu.make_async_copy(scale_hbm, scale_ref, sem.at[1])
-    small.start()
-    load = pltpu.make_async_copy(w_ref, w_held, sem.at[0])
+    load = pltpu.make_async_copy(w_ref, w_held, sem)
     load.start()
     s = lax.axis_index("x") * 4 + lax.axis_index("z")
     row_at = s * 128 + row_offset(lax.broadcasted_iota(jnp.int32, (128, 1), 0))
     column = lax.broadcasted_iota(jnp.int32, (1, TOKENS), 1)
     allowed = row_at >= (column // 128) * 128 + row_offset(column % 128)
-    small.wait()
     factor = scale_ref[:, :1] * (SCORE_SCALE / math.log(2.0))
 
     def one_head(g, carry):
@@ -265,45 +258,26 @@
     lax.fori_loop(0, 4, one_part, 0)
 
 
-def home_copies(held, target, sem, start):
+def home_copies(held, outs, at, sem, start):
     y, c = lax.axis_index("y"), lax.axis_index("c")
     copies = []
     for by in range(4):
         for half in range(2):
             column = (((y + by) % 4) * 2 + (c + half) % 2) * 640
             columns = pl.ds(pl.multiple_of(column, 640), 640)
+            target = outs[half].at[at] if by == 0 else outs[1 + by].at[half, at]
             copies.append(
-                pltpu.make_async_copy(
-                    held.at[:, columns], target(by, half), sem.at[start + 2 * by + half]
-                )
+                pltpu.make_async_copy(held.at[:, columns], target, sem.at[start + 2 * by + half])
             )
     return copies
 
 
-def pack_kernel(*refs):
-    images, outs, (held, sem) = refs[:3], refs[3:7], refs[7:]
-    loads = [
-        pltpu.make_async_copy(image, held.at[at], sem.at[at]) for at, image in enumerate(images)
-    ]
-    for load in loads:
-        load.start()
-    copies = []
-    for at in range(3):
-        loads[at].wait()
-        fresh = home_copies(
-            held.at[at], lambda by, half: outs[by].at[half, at], sem, 3 + 8 * at
-        )
-        for copy in fresh:
-            copy.start()
-        copies += fresh
-    for copy in copies:
-        copy.wait()
-
-
 def finish_kernel(k, own_ref, a_ref, b_ref, d_ref, inj_ref, x_ref, gain_ref, gain_in_ref, *rest):
     older, rest = rest[:k], rest[k:]
+    if k in (1, 2):
+        rest = rest[5:]
     image_held, residual_held, dots_held, sem = rest[-4:]
-    image_out, residual_out = rest[:2]
+    image_out, residual_out, *home_out = rest[:7]
     inj, x = inj_ref[...].astype(F32), x_ref[...].astype(F32)
     summed = (x + inj) + (
         own_ref[...] + a_ref[...].astype(F32) + b_ref[...].astype(F32) + d_ref[...].astype(F32)
@@ -317,12 +291,11 @@
         pltpu.make_async_copy(image_held, image_out, sem.at[0]),
         pltpu.make_async_copy(residual_held, residual_out, sem.at[1]),
     ]
-    if k == ITERS - 1:
-        copies += home_copies(image_held, lambda by, half: rest[2 + by].at[half], sem, 2)
+    copies += home_copies(image_held, home_out, k % (ITERS - 1), sem, 2)
     for copy in copies:
         copy.start()
     if k < ITERS - 1:
-        rest[2][...] = ((image + inj) * gain_in_ref[...]).astype(BF16)
+        rest[7][...] = ((image + inj) * gain_in_ref[...]).astype(BF16)
     if k > 0:
         lane = lax.broadcasted_iota(jnp.int32, (1, 128), 1)
         dots = jnp.where(lane == k, total(residual * residual), 0.0)
@@ -331,7 +304,7 @@
         if k == 1:
             dots = dots + jnp.where(lane == 7, total(older[0][...] * older[0][...]), 0.0)
         dots_held[...] = jnp.broadcast_to(dots.reshape(1, 1, 128), (128, 1, 128))
-        table_out = rest[3] if k < ITERS - 1 else rest[6]
+        table_out = rest[8] if k < ITERS - 1 else rest[7]
         copies.append(pltpu.make_async_copy(dots_held, table_out, sem.at[10]))
         copies[-1].start()
     for copy in copies:
@@ -389,14 +362,19 @@
     shares = mix_shares(k, refs[:k])
     older, newest, (out_hbm, out_ref, sem) = refs[k : k + 5], refs[k + 5 : k + 10], refs[-3:]
     y, c = lax.axis_index("y"), lax.axis_index("c")
+
+    def piece(home, by, half, at):
+        if half == 1:
+            return home[4][by, at]
+        return home[0][at] if by == 0 else home[by][0, at]
+
     for by in range(4):
         for half in range(2):
             row = (((y - by + 4) % 4) * 2 + (c + half) % 2) * 16
             rows = pl.ds(pl.multiple_of(row, 16), 16)
-            old = older[by][0] if half == 0 else older[4][by]
-            mixed = shares[k] * (newest[by][0] if half == 0 else newest[4][by])
+            mixed = shares[k] * piece(newest, by, half, 0)
             for at in range(k):
-                mixed = mixed + shares[at] * old[at]
+                mixed = mixed + shares[at] * piece(older, by, half, at)
             out_ref[rows, :] = mixed
     store = pltpu.make_async_copy(out_ref, out_hbm, sem)
     store.start()
@@ -404,7 +382,7 @@
 
 
 def start_kernel(inj_hbm, warm_hbm, gain_hbm, payload_ref, *refs):
-    home_refs, (inj_ref, warm_ref, gain_ref, sem) = refs[:4], refs[4:]
+    home_refs, (inj_ref, warm_ref, gain_ref, sem) = refs[:5], refs[5:]
     loads = [
         pltpu.make_async_copy(gain_hbm, gain_ref, sem.at[2]),
         pltpu.make_async_copy(inj_hbm, inj_ref, sem.at[0]),
@@ -422,8 +400,11 @@
         for half in range(2):
             row = (((y + by) % 4) * 2 + (c + half) % 2) * 16
             rows = pl.ds(pl.multiple_of(row, 16), 16)
-            home_refs[by][half, 0] = inj_ref[rows, :]
-            home_refs[by][half, 1] = warm_ref[rows, :]
+            for at, source in enumerate((inj_ref, warm_ref)):
+                if by == 0:
+                    home_refs[half][at] = source[rows, :]
+                else:
+                    home_refs[1 + by][half, at] = source[rows, :]
 
 
 def settle_kernel(*refs):
@@ -433,15 +414,18 @@
         for half in range(2):
             column = (((y - by + 4) % 4) * 2 + (c + half) % 2) * 640
             columns = pl.ds(pl.multiple_of(column, 640), 640)
-            piece = refs[by][0] if half == 0 else refs[4][by]
-            inj_ref[:, columns] = piece[0]
-            warm_ref[:, columns] = piece[1]
+            for at, target in enumerate((inj_ref, warm_ref)):
+                if half == 1:
+                    target[:, columns] = refs[4][by, at]
+                else:
+                    target[:, columns] = refs[0][at] if by == 0 else refs[by][0, at]
 
 
 def move_home(pieces):
-    near = [pieces[0]] + [lax.ppermute(pieces[by], "y", shift(4, by)) for by in (1, 2, 3)]
-    joined = jnp.stack([piece[1] for piece in near])
-    return [*near, lax.ppermute(joined, "c", shift(2, 1))]
+    own, pair, *far = pieces
+    near = [lax.ppermute(piece, "y", shift(4, by + 1)) for by, piece in enumerate(far)]
+    joined = jnp.stack([pair] + [piece[1] for piece in near])
+    return [own, *near, lax.ppermute(joined, "c", shift(2, 1))]
 
 
 def on_device(injection, warm_start, gain_in, gain_out, w_query, w_key, w_value, w_out):
@@ -449,11 +433,12 @@
     tokens = pltpu.HBM((16, D), F32)
     wide = pltpu.VMEM((16, D), F32)
     narrow = pltpu.VMEM((16, D), BF16)
-    home_narrow = pltpu.VMEM((2, 2, 16, 640), BF16)
-    home_wide = pltpu.HBM((2, 16, 640), F32)
+    home_narrow = [pltpu.VMEM((2, 16, 640), BF16)] * 2 + [pltpu.VMEM((2, 2, 16, 640), BF16)] * 3
+    home_packed = [pltpu.HBM((3, 16, 640), F32)] * 2 + [pltpu.HBM((2, 3, 16, 640), F32)] * 3
+    home_last = [pltpu.VMEM((1, 16, 640), F32)] * 2 + [pltpu.HBM((2, 1, 16, 640), F32)] * 3
     payload, *home = call(
         start_kernel,
-        (pltpu.VMEM((128, 640), BF16), *[home_narrow] * 4),
+        (pltpu.VMEM((128, 640), BF16), *home_narrow),
         injection,
         warm_start,
         gain_in,
@@ -467,16 +452,17 @@
     )
     settled = []
     images, residuals, parts, tables, dots = [], [], [], [], None
-    raws = []
-    projected = (pltpu.HBM((128, D), BF16), pltpu.HBM((128, 384), F32))
-    project_scratch = [
-        pltpu.VMEM((128, D), BF16),
-        pltpu.VMEM((D, 2 * HEAD_DIM), BF16),
-        pltpu.VMEM((128, 384), F32),
-        pltpu.SemaphoreType.DMA((4,)),
-    ]
+    raws, share = [], None
+    rows_out = pltpu.HBM((128, D), BF16)
+    raw_out = pltpu.VMEM((128, 384), F32)
+    hand_outs = [pltpu.VMEM((128, 128), F32), pltpu.HBM((16, 128, 2 * HEAD_DIM), BF16)]
+    kv_scratch = pltpu.VMEM((128, 2 * HEAD_DIM), BF16)
+    project_scratch = [pltpu.VMEM((128, D), BF16), pltpu.VMEM((D, 2 * HEAD_DIM), BF16)]
+    many = pltpu.SemaphoreType.DMA((19,))
     for k in range(ITERS):
-        pieces = [payload] + [lax.ppermute(payload, "y", shift(4, by)) for by in (1, 2, 3)]
+        pieces = [payload]
+        for by in (1, 2, 3):
+            pieces.append(lax.ppermute(payload, "y", shift(4, by)))
         if dots is not None:
             tables.append(lax.all_to_all(dots, EVERY, split_axis=0, concat_axis=0, tiled=True))
         mine = jnp.stack(pieces) if k == 0 else jnp.concatenate(pieces, axis=0)
@@ -484,23 +470,23 @@
         if k == 1:
             parts, raws = [], []
         if k == 0:
-            rows, raw = call(
+            rows, scale, kv = call(
                 first_kernel,
-                projected,
+                [rows_out, *hand_outs],
                 w_key,
                 w_value,
                 gain_in,
                 *pieces,
                 specs=[HBM] * 2 + [VMEM] * 3,
                 vmem=8,
-                scratch=project_scratch,
+                scratch=[*project_scratch, kv_scratch, many],
                 flops=2 * 128 * D * 256,
                 touched=4_000_000,
             )
         else:
-            rows, raw = call(
+            rows, raw, *hand = call(
                 functools.partial(project_kernel, k - 1),
-                projected,
+                [rows_out, raw_out] + (hand_outs if k == 1 else []),
                 w_key,
                 w_value,
                 gain_in,
@@ -508,44 +494,31 @@
                 *pieces,
                 specs=[HBM] * 2 + [VMEM] + [HBM] * len(parts) + [VMEM] * 2,
                 vmem=10,
-                scratch=project_scratch
+                scratch=([kv_scratch] if k == 1 else [])
+                + project_scratch
                 + [
+                    many,
                     pltpu.VMEM((k - 1, 128, D) if k > 1 else (1, 8, 128), BF16),
                     pltpu.SemaphoreType.DMA((max(k - 1, 1), 8)),
                 ],
                 flops=2 * 128 * D * 256,
                 touched=4_000_000,
             )
+            raws.append(raw)
         parts.append(rows)
-        raws.append(raw)
-        share, scale, kv = call(
-            functools.partial(share_kernel, len(parts) - 1),
-            (
-                pltpu.VMEM((1, 128), F32),
-                pltpu.HBM((128, 128), F32),
-                pltpu.HBM((16, 128, 2 * HEAD_DIM), BF16),
-            ),
-            *tables,
-            *raws,
-            specs=[VMEM] * len(tables) + [HBM] * len(raws),
-            vmem=4,
-            scratch=[
-                pltpu.VMEM((len(raws), 128, 384), F32),
-                pltpu.VMEM((128, 128), F32),
-                pltpu.VMEM((128, 2 * HEAD_DIM), BF16),
-                pltpu.SemaphoreType.DMA((17,)),
-            ],
-        )
+        if k == 1:
+            scale, kv = hand
+        if k > 1:
+            share, scale, kv = call(
+                functools.partial(share_kernel, len(parts) - 1),
+                [pltpu.VMEM((1, 128), F32), *hand_outs],
+                *tables,
+                *raws,
+                vmem=4,
+                scratch=[kv_scratch, many],
+            )
         kv_all = lax.all_to_all(kv, SEQ, split_axis=0, concat_axis=0, tiled=True)
         q = query_dot(share, parts, w_query)
-        if k == ITERS - 1:
-            home = call(
-                pack_kernel,
-                [pltpu.HBM((2, 3, 16, 640), F32)] * 4,
-                *images,
-                specs=[HBM] * 3,
-                scratch=[pltpu.VMEM((3, 16, D), F32), pltpu.SemaphoreType.DMA((27,))],
-            )
         if k in (0, ITERS - 1):
             home = move_home(home)
             kv_all, home = lax.optimization_barrier((kv_all, home))
@@ -562,27 +535,27 @@
             scale,
             kv_all,
             w_out,
-            specs=[VMEM, HBM, VMEM, HBM],
+            specs=[VMEM, VMEM, VMEM, HBM],
             vmem=16,
             scratch=[
                 pltpu.VMEM((640, D), BF16),
-                pltpu.VMEM((128, 128), F32),
                 pltpu.VMEM((128, 640), BF16),
-                pltpu.SemaphoreType.DMA((2,)),
+                pltpu.SemaphoreType.DMA,
             ],
             flops=2 * 128 * 640 * (2 * TOKENS + D),
             touched=9_000_000,
         )
         pair = own + lax.ppermute(send, "c", shift(2, 1)).astype(F32)
-        arrived = [
-            lax.ppermute(pair[16 * by : 16 * by + 16].astype(BF16), "y", shift(4, -by))
-            for by in (1, 2, 3)
-        ]
-        shapes = [tokens, tokens] + ([home_wide] * 4 if k == ITERS - 1 else [])
+        arrived = []
+        for by in (1, 2, 3):
+            piece = pair[16 * by : 16 * by + 16].astype(BF16)
+            arrived.append(lax.ppermute(piece, "y", shift(4, -by)))
+        shapes = [tokens, tokens, *(home_packed if k < ITERS - 1 else home_last)]
         if k < ITERS - 1:
             shapes.append(narrow)
         if k > 0:
             shapes.append(pltpu.HBM((128, 1, 128), F32))
+        packed = list(home) if k in (1, 2) else []
         outs = call(
             functools.partial(finish_kernel, k),
             tuple(shapes),
@@ -593,6 +566,9 @@
             gain_out,
             gain_in,
             *residuals,
+            *packed,
+            specs=[VMEM] * (8 + len(residuals)) + [HBM] * len(packed),
+            aliases={8 + k + at: 2 + at for at in range(len(packed))},
             scratch=[
                 pltpu.VMEM((16, D), F32),
                 pltpu.VMEM((16, D), F32),
@@ -602,8 +578,8 @@
         )
         images.append(outs[0])
         residuals.append(outs[1])
-        home = outs[2:6]
-        payload = outs[2]
+        home = outs[2:7]
+        payload = outs[7]
         if k == 0:
             current = outs[0]
         else:

time: 319 us -> 311 us (0.975)
  Pallas kernels: 83.7 us -> 74.6 us
    pallas_call x22 -> x19, Pallas kernels: 60.5 us -> 51.5 us  [call(): pl.pallas_call(kernel, out_shape=outs, in_specs=specs, input_output_alias...]
  transfers between devices with their start and end apart: 50 -> 50, of which waited for: 39 -> 39; matrix products, arithmetic and copies ran while one was open for 1% -> 0% of each run, Pallas kernels for 11% -> 11%
where the time goes in v1:
time: 311 us; the launch traced here: 310 us
  waiting for transfers between devices  139 us (45%)
  starting transfers between devices  75.7 us (24%)
  Pallas kernels  74.6 us (24%)
  blocking collectives  16.8 us (5%)
    pallas_call x19, Pallas kernels, call(): pl.pallas_call(kernel, out_shape=outs, in_specs=specs, input_output_alias...  51.5 us
    ppermute x12, waiting for transfers between devices, on_device(): arrived.append(lax.ppermute(piece, 'y', shift(4, -by)))  39.5 us
    ppermute x12, waiting for transfers between devices, on_device(): pieces.append(lax.ppermute(payload, 'y', shift(4, by)))  32.2 us
    ppermute x9, waiting for transfers between devices, move_home(): lax.ppermute(piece, 'y', shift(4, by + 1))  24.9 us
    pallas_call x4, Pallas kernels, query_dot(): pl.pallas_call(functools.partial(query_kernel, len(parts) - 1), grid=(5,)...  23.1 us
    all_to_all x4, waiting for transfers between devices, on_device(): kv_all = lax.all_to_all(kv, SEQ, split_axis=0, concat_axis=0, tiled=True)  22 us
    all_to_all x4, starting transfers between devices, on_device(): kv_all = lax.all_to_all(kv, SEQ, split_axis=0, concat_axis=0, tiled=True)  18.7 us
    all_to_all x1, blocking collectives, on_device(): lax.all_to_all(dots, EVERY, split_axis=0, concat_axis=0, tiled=True)  16.8 us
  transfers between devices with their start and end apart: 50, of which 39 were waited for; matrix products, arithmetic and copies ran while one was open for 0% of the time, Pallas kernels for 11%

profile of v1, /device:TPU:1, one launch (start us, length us, event | category | flops | bytes accessed | tf_op | source)
XLA Modules:
  0.0 309.6 jit_solution(5835894846932032790)
XLA Ops:
  1.1 3.6 %collective-permute-start.2 = (bf16[128,640]{1,0:T(8,128)(2,1)S(1)}, bf16[128,640]{1,0:T(8,128)(2,1)S(1)}, u32[]{:S(2)}, u32[]{:S(2)}) collective-permute-start(bf16[128,640]{1,0:T(8,128)(2,1)S(1)} %get-tuple-element.82), channel_id=1, source_target_pairs={{0,6},{2,0},{4,2},{6,4},{1,7},{3,1},{5,3},{7,5},{8,14},{10,8},{12,... | collective-permute-start | bytes 491528 | tf_op jit(solution)/shard_map/ppermute | solution.py:465
  5.8 5.4 %collective-permute-done.2 = bf16[128,640]{1,0:T(8,128)(2,1)S(1)} collective-permute-done((bf16[128,640]{1,0:T(8,128)(2,1)S(1)}, bf16[128,640]{1,0:T(8,128)(2,1)S(1)}, u32[]{:S(2)}, u32[]{:S(2)}) %collective-permute-start.2) | collective-permute-done | bytes 163872 | tf_op jit(solution)/shard_map/ppermute | solution.py:465
  11.2 4.7 %collective-permute-done = bf16[128,640]{1,0:T(8,128)(2,1)S(1)} collective-permute-done((bf16[128,640]{1,0:T(8,128)(2,1)S(1)}, bf16[128,640]{1,0:T(8,128)(2,1)S(1)}, u32[]{:S(2)}, u32[]{:S(2)}) %collective-permute-start) | collective-permute-done | bytes 163872 | tf_op jit(solution)/shard_map/ppermute | solution.py:465
  18.3 3.9 %shard_map.83 = (bf16[128,5120]{1,0:T(8,128)(2,1)}, f32[128,128]{1,0:T(8,128)S(1)}, bf16[16,128,256]{2,1,0:T(8,128)(2,1)}) custom-call(bf16[5120,128]{1,0:T(8,128)(2,1)} %refs_0_.5, bf16[5120,128]{1,0:T(8,128)(2,1)} %refs_1_.9, f32[1,5120]{1,0:T(1,128)S(1)} %bitcast.10, bf16[4,128,640]{2,1,0:T(8,128)(2,1)S(1)} %pad_maximum_fusion.refs_0_, ...), custom_call_target="tpu_custom_call" | custom-call | flops 335544320 | bytes 4000000 | tf_op jit(solution)/shard_map/pallas_call | solution.py:43
  22.2 7.6 %all-to-all-start = ((bf16[16,128,256]{2,1,0:T(8,128)(2,1)}), bf16[16,128,256]{2,1,0:T(8,128)(2,1)S(1)}, u32[]{:S(2)}, u32[]{:S(2)}) async-start(bf16[16,128,256]{2,1,0:T(8,128)(2,1)} %get-tuple-element.85), calls=%async_computation | async-start | bytes 2097152 | tf_op jit(solution)/shard_map/all_to_all | solution.py:520
  33.2 2.1 collective-permute-done.5.refs_2_
  38.5 5.5 %shard_map.84.q_ref = bf16[128,640]{1,0:T(8,128)(2,1)S(1)} custom-call(bf16[128,5120]{1,0:T(8,128)(2,1)} %get-tuple-element.83.refs_0_, bf16[5120,640]{1,0:T(8,128)(2,1)} %refs_4_.1), custom_call_target="tpu_custom_call" | custom-call | flops 838860800 | bytes 8000000 | tf_op jit(solution)/shard_map/pallas_call | solution.py:207
  45.5 6.0 %shard_map.85 = (f32[64,5120]{1,0:T(8,128)S(1)}, bf16[64,5120]{1,0:T(8,128)(2,1)S(1)}) custom-call(bf16[128,640]{1,0:T(8,128)(2,1)S(1)} %shard_map.84.q_ref, f32[128,128]{1,0:T(8,128)S(1)} %get-tuple-element.84.scale_ref, bf16[16,128,256]{2,1,0:T(8,128)(2,1)S(1)} %all-to-all-done.kv_ref, bf16[640,5120]{1,0:T(8,128)(2,1)} %w_ref.7), custom_call_target="tpu_custom_call" | custom-call | flops 1509949440 | bytes 9000000 | tf_op jit(solution)/shard_map/pallas_call | solution.py:43
  51.4 3.2 %collective-permute-start.8 = (bf16[64,5120]{1,0:T(8,128)(2,1)S(1)}, bf16[64,5120]{1,0:T(8,128)(2,1)S(1)}, u32[]{:S(2)}, u32[]{:S(2)}) collective-permute-start(bf16[64,5120]{1,0:T(8,128)(2,1)S(1)} %get-tuple-element.93), channel_id=1, source_target_pairs={{0,1},{1,0},{2,3},{3,2},{4,5},{5,4},{6,7},{7,6},{8,9},{9,8},{10,11... | collective-permute-start | bytes 1966088 | tf_op jit(solution)/shard_map/ppermute | solution.py:548
  58.2 3.8 %collective-permute-done.9.a_ref = bf16[16,5120]{1,0:T(8,128)(2,1)S(1)} collective-permute-done((bf16[16,5120]{1,0:T(8,128)(2,1)S(1)}, bf16[16,5120]{1,0:T(8,128)(2,1)S(1)}, u32[]{:S(2)}, u32[]{:S(2)}) %collective-permute-start.9) | collective-permute-done | bytes 163872 | tf_op jit(solution)/shard_map/ppermute | solution.py:552
  63.6 4.5 %collective-permute-done.11.d_ref = bf16[16,5120]{1,0:T(8,128)(2,1)S(1)} collective-permute-done((bf16[16,5120]{1,0:T(8,128)(2,1)S(1)}, bf16[16,5120]{1,0:T(8,128)(2,1)S(1)}, u32[]{:S(2)}, u32[]{:S(2)}) %collective-permute-start.11) | collective-permute-done | bytes 163872 | tf_op jit(solution)/shard_map/ppermute | solution.py:552
  72.3 7.4 %collective-permute-done.12 = bf16[16,5120]{1,0:T(8,128)(2,1)S(1)} collective-permute-done((bf16[16,5120]{1,0:T(8,128)(2,1)S(1)}, bf16[16,5120]{1,0:T(8,128)(2,1)S(1)}, u32[]{:S(2)}, u32[]{:S(2)}) %collective-permute-start.12) | collective-permute-done | bytes 163872 | tf_op jit(solution)/shard_map/ppermute | solution.py:465
  83.3 3.4 %shard_map.88 = (bf16[128,5120]{1,0:T(8,128)(2,1)}, f32[128,384]{1,0:T(8,128)S(1)}, f32[128,128]{1,0:T(8,128)S(1)}, bf16[16,128,256]{2,1,0:T(8,128)(2,1)}) custom-call(bf16[5120,128]{1,0:T(8,128)(2,1)} %refs_0_.5, bf16[5120,128]{1,0:T(8,128)(2,1)} %refs_1_.9, f32[1,5120]{1,0:T(1,128)S(1)} %bitcast.12, ...), custom_call_target="tpu_custom_call" | custom-call | flops 335544320 | bytes 4000000 | tf_op jit(solution)/shard_map/pallas_call | solution.py:43
  86.8 3.7 %all-to-all-start.1 = ((bf16[16,128,256]{2,1,0:T(8,128)(2,1)}), bf16[16,128,256]{2,1,0:T(8,128)(2,1)S(1)}, u32[]{:S(2)}, u32[]{:S(2)}) async-start(bf16[16,128,256]{2,1,0:T(8,128)(2,1)} %get-tuple-element.104), calls=%async_computation.1 | async-start | bytes 2097152 | tf_op jit(solution)/shard_map/all_to_all | solution.py:520
  90.5 5.5 %shard_map.89.q_ref = bf16[128,640]{1,0:T(8,128)(2,1)S(1)} custom-call(bf16[128,5120]{1,0:T(8,128)(2,1)} %get-tuple-element.102.refs_0_.refs_3_.refs_1_, bf16[5120,640]{1,0:T(8,128)(2,1)} %refs_4_.1), custom_call_target="tpu_custom_call" | custom-call | flops 838860800 | bytes 8000000 | tf_op jit(solution)/shard_map/pallas_call | solution.py:207
  96.0 10.7 %all-to-all-done.1.kv_ref = bf16[16,128,256]{2,1,0:T(8,128)(2,1)S(1)} async-done(((bf16[16,128,256]{2,1,0:T(8,128)(2,1)}), bf16[16,128,256]{2,1,0:T(8,128)(2,1)S(1)}, u32[]{:S(2)}, u32[]{:S(2)}) %all-to-all-start.1) | async-done | bytes 1048608 | tf_op jit(solution)/shard_map/all_to_all | solution.py:520
  106.7 6.0 %shard_map.90 = (f32[64,5120]{1,0:T(8,128)S(1)}, bf16[64,5120]{1,0:T(8,128)(2,1)S(1)}) custom-call(bf16[128,640]{1,0:T(8,128)(2,1)S(1)} %shard_map.89.q_ref, f32[128,128]{1,0:T(8,128)S(1)} %get-tuple-element.103.scale_ref, bf16[16,128,256]{2,1,0:T(8,128)(2,1)S(1)} %all-to-all-done.1.kv_ref, bf16[640,5120]{1,0:T(8,128)(2,1)} %w_ref.7), custom_call_target="tpu_custom_call" | custom-call | flops 1509949440 | bytes 9000000 | tf_op jit(solution)/shard_map/pallas_call | solution.py:43
  112.6 2.6 collective-permute-start.16
  117.2 2.4 collective-permute-start.17
  120.2 2.9 collective-permute-done.17.a_ref
  123.2 3.1 collective-permute-done.18.b_ref
  126.2 3.9 %collective-permute-done.19.d_ref = bf16[16,5120]{1,0:T(8,128)(2,1)S(1)} collective-permute-done((bf16[16,5120]{1,0:T(8,128)(2,1)S(1)}, bf16[16,5120]{1,0:T(8,128)(2,1)S(1)}, u32[]{:S(2)}, u32[]{:S(2)}) %collective-permute-start.19) | collective-permute-done | bytes 163872 | tf_op jit(solution)/shard_map/ppermute | solution.py:552
  134.5 7.3 %collective-permute-done.20 = bf16[16,5120]{1,0:T(8,128)(2,1)S(1)} collective-permute-done((bf16[16,5120]{1,0:T(8,128)(2,1)S(1)}, bf16[16,5120]{1,0:T(8,128)(2,1)S(1)}, u32[]{:S(2)}, u32[]{:S(2)}) %collective-permute-start.20) | collective-permute-done | bytes 163872 | tf_op jit(solution)/shard_map/ppermute | solution.py:465
  143.8 5.0 %all-to-all-start.2 = ((f32[128,1,128]{2,1,0:T(1,128)}), f32[128,1,128]{2,1,0:T(1,128)S(1)}, u32[]{:S(2)}, u32[]{:S(2)}) async-start(f32[128,1,128]{2,1,0:T(1,128)} %get-tuple-element.114), calls=%async_computation.2 | async-start | bytes 131072 | tf_op jit(solution)/shard_map/all_to_all | solution.py:467
  148.8 3.6 %shard_map.92 = (bf16[128,5120]{1,0:T(8,128)(2,1)}, f32[128,384]{1,0:T(8,128)S(1)}) custom-call(bf16[5120,128]{1,0:T(8,128)(2,1)} %refs_0_.5, bf16[5120,128]{1,0:T(8,128)(2,1)} %refs_1_.9, f32[1,5120]{1,0:T(1,128)S(1)} %bitcast.14, bf16[128,5120]{1,0:T(8,128)(2,1)} %get-tuple-element.102.refs_0_.refs_3_.refs_1_, ...), custom_call_target="tpu_custom_call" | custom-call | flops 335544320 | bytes 4000000 | tf_op jit(solution)/shard_map/pallas_call | solution.py:43
  152.4 5.9 %all-to-all-done.2.refs_0_ = f32[128,1,128]{2,1,0:T(1,128)S(1)} async-done(((f32[128,1,128]{2,1,0:T(1,128)}), f32[128,1,128]{2,1,0:T(1,128)S(1)}, u32[]{:S(2)}, u32[]{:S(2)}) %all-to-all-start.2) | async-done | bytes 65568 | tf_op jit(solution)/shard_map/all_to_all | solution.py:467
  159.8 3.7 %all-to-all-start.3 = ((bf16[16,128,256]{2,1,0:T(8,128)(2,1)}), bf16[16,128,256]{2,1,0:T(8,128)(2,1)S(1)}, u32[]{:S(2)}, u32[]{:S(2)}) async-start(bf16[16,128,256]{2,1,0:T(8,128)(2,1)} %get-tuple-element.121), calls=%async_computation.3 | async-start | bytes 2097152 | tf_op jit(solution)/shard_map/all_to_all | solution.py:520
  163.5 5.9 %shard_map.94.q_ref = bf16[128,640]{1,0:T(8,128)(2,1)S(1)} custom-call(f32[1,128]{1,0:T(1,128)S(1)} %get-tuple-element.118.refs_0_.share_ref, bf16[128,5120]{1,0:T(8,128)(2,1)} %get-tuple-element.102.refs_0_.refs_3_.refs_1_, bf16[128,5120]{1,0:T(8,128)(2,1)} %get-tuple-element.119.refs_2_.refs_4_, bf16[5120,640]{1,0:T(8,128)(2,1)} %refs_4_.1), custom_call_target="tpu_custom_call" | custom-call | flops 838860800 | bytes 8000000 | tf_op jit(solution)/shard_map/pallas_call | solution.py:207
  169.4 9.8 %all-to-all-done.3.kv_ref = bf16[16,128,256]{2,1,0:T(8,128)(2,1)S(1)} async-done(((bf16[16,128,256]{2,1,0:T(8,128)(2,1)}), bf16[16,128,256]{2,1,0:T(8,128)(2,1)S(1)}, u32[]{:S(2)}, u32[]{:S(2)}) %all-to-all-start.3) | async-done | bytes 1048608 | tf_op jit(solution)/shard_map/all_to_all | solution.py:520
  179.1 6.0 %shard_map.95 = (f32[64,5120]{1,0:T(8,128)S(1)}, bf16[64,5120]{1,0:T(8,128)(2,1)S(1)}) custom-call(bf16[128,640]{1,0:T(8,128)(2,1)S(1)} %shard_map.94.q_ref, f32[128,128]{1,0:T(8,128)S(1)} %get-tuple-element.120.scale_ref, bf16[16,128,256]{2,1,0:T(8,128)(2,1)S(1)} %all-to-all-done.3.kv_ref, bf16[640,5120]{1,0:T(8,128)(2,1)} %w_ref.7), custom_call_target="tpu_custom_call" | custom-call | flops 1509949440 | bytes 9000000 | tf_op jit(solution)/shard_map/pallas_call | solution.py:43
  185.1 3.1 %collective-permute-start.24 = (bf16[64,5120]{1,0:T(8,128)(2,1)S(1)}, bf16[64,5120]{1,0:T(8,128)(2,1)S(1)}, u32[]{:S(2)}, u32[]{:S(2)}) collective-permute-start(bf16[64,5120]{1,0:T(8,128)(2,1)S(1)} %get-tuple-element.123), channel_id=1, source_target_pairs={{0,1},{1,0},{2,3},{3,2},{4,5},{5,4},{6,7},{7,6},{8,9},{9,8},{10,11... | collective-permute-start | bytes 1966088 | tf_op jit(solution)/shard_map/ppermute | solution.py:548
  192.5 3.1 collective-permute-done.25.a_ref
  195.6 2.3 collective-permute-done.26.b_ref
  197.9 4.5 %collective-permute-done.27.d_ref = bf16[16,5120]{1,0:T(8,128)(2,1)S(1)} collective-permute-done((bf16[16,5120]{1,0:T(8,128)(2,1)S(1)}, bf16[16,5120]{1,0:T(8,128)(2,1)S(1)}, u32[]{:S(2)}, u32[]{:S(2)}) %collective-permute-start.27) | collective-permute-done | bytes 163872 | tf_op jit(solution)/shard_map/ppermute | solution.py:552
  207.2 7.0 %collective-permute-done.28 = bf16[16,5120]{1,0:T(8,128)(2,1)S(1)} collective-permute-done((bf16[16,5120]{1,0:T(8,128)(2,1)S(1)}, bf16[16,5120]{1,0:T(8,128)(2,1)S(1)}, u32[]{:S(2)}, u32[]{:S(2)}) %collective-permute-start.28) | collective-permute-done | bytes 163872 | tf_op jit(solution)/shard_map/ppermute | solution.py:465
  216.2 5.1 %all-to-all-start.4 = ((f32[128,1,128]{2,1,0:T(1,128)}), f32[128,1,128]{2,1,0:T(1,128)S(1)}, u32[]{:S(2)}, u32[]{:S(2)}) async-start(f32[128,1,128]{2,1,0:T(1,128)} %get-tuple-element.131), calls=%async_computation.4 | async-start | bytes 131072 | tf_op jit(solution)/shard_map/all_to_all | solution.py:467
  221.3 5.7 %shard_map.98 = (bf16[128,5120]{1,0:T(8,128)(2,1)}, f32[128,384]{1,0:T(8,128)S(1)}) custom-call(bf16[5120,128]{1,0:T(8,128)(2,1)} %refs_0_.5, bf16[5120,128]{1,0:T(8,128)(2,1)} %refs_1_.9, f32[1,5120]{1,0:T(1,128)S(1)} %bitcast.16, bf16[128,5120]{1,0:T(8,128)(2,1)} %get-tuple-element.102.refs_0_.refs_3_.refs_1_, ...), custom_call_target="tpu_custom_call" | custom-call | flops 335544320 | bytes 4000000 | tf_op jit(solution)/shard_map/pallas_call | solution.py:43
  227.0 3.8 %all-to-all-done.4.refs_1_ = f32[128,1,128]{2,1,0:T(1,128)S(1)} async-done(((f32[128,1,128]{2,1,0:T(1,128)}), f32[128,1,128]{2,1,0:T(1,128)S(1)}, u32[]{:S(2)}, u32[]{:S(2)}) %all-to-all-start.4) | async-done | bytes 65568 | tf_op jit(solution)/shard_map/all_to_all | solution.py:467
  232.4 3.8 %all-to-all-start.5 = ((bf16[16,128,256]{2,1,0:T(8,128)(2,1)}), bf16[16,128,256]{2,1,0:T(8,128)(2,1)S(1)}, u32[]{:S(2)}, u32[]{:S(2)}) async-start(bf16[16,128,256]{2,1,0:T(8,128)(2,1)} %get-tuple-element.137), calls=%async_computation.5 | async-start | bytes 2097152 | tf_op jit(solution)/shard_map/all_to_all | solution.py:520
  236.2 2.3 collective-permute-start.34
  239.6 4.7 %collective-permute-done.34.refs_6_ = f32[2,3,16,640]{3,2,1,0:T(8,128)S(1)} collective-permute-done((f32[2,3,16,640]{3,2,1,0:T(8,128)}, f32[2,3,16,640]{3,2,1,0:T(8,128)S(1)}, u32[]{:S(2)}, u32[]{:S(2)}) %collective-permute-start.34) | collective-permute-done | bytes 245792 | tf_op jit(solution)/shard_map/ppermute | solution.py:426
  244.2 2.6 collective-permute-done.33.refs_5_
  246.8 6.5 %collective-permute-done.32.refs_4_ = f32[2,3,16,640]{3,2,1,0:T(8,128)S(1)} collective-permute-done((f32[2,3,16,640]{3,2,1,0:T(8,128)S(1)}, f32[2,3,16,640]{3,2,1,0:T(8,128)S(1)}, u32[]{:S(2)}, u32[]{:S(2)}) %collective-permute-start.32) | collective-permute-done | bytes 245792 | tf_op jit(solution)/shard_map/ppermute | solution.py:426
  254.7 6.2 %shard_map.100.q_ref = bf16[128,640]{1,0:T(8,128)(2,1)S(1)} custom-call(f32[1,128]{1,0:T(1,128)S(1)} %get-tuple-element.134.refs_0_.share_ref, bf16[128,5120]{1,0:T(8,128)(2,1)} %get-tuple-element.102.refs_0_.refs_3_.refs_1_, bf16[128,5120]{1,0:T(8,128)(2,1)} %get-tuple-element.119.refs_2_.refs_4_, bf16[128,5120]{1,0:T(8,128)(2,1)} %get-tuple-element.135.refs_3_, ...), custom_call_target="tpu_custom_call" | custom-call | flops 838860800 | bytes 8000000 | tf_op jit(solution)/shard_map/pallas_call | solution.py:207
  261.7 5.9 %shard_map.101 = (f32[64,5120]{1,0:T(8,128)S(1)}, bf16[64,5120]{1,0:T(8,128)(2,1)S(1)}) custom-call(bf16[128,640]{1,0:T(8,128)(2,1)S(1)} %shard_map.100.q_ref, f32[128,128]{1,0:T(8,128)S(1)} %get-tuple-element.136.scale_ref, bf16[16,128,256]{2,1,0:T(8,128)(2,1)S(1)} %all-to-all-done.5.kv_ref, bf16[640,5120]{1,0:T(8,128)(2,1)} %w_ref.7), custom_call_target="tpu_custom_call" | custom-call | flops 1509949440 | bytes 9000000 | tf_op jit(solution)/shard_map/pallas_call | solution.py:43
  271.8 3.9 %collective-permute-done.37.a_ref = bf16[16,5120]{1,0:T(8,128)(2,1)S(1)} collective-permute-done((bf16[16,5120]{1,0:T(8,128)(2,1)S(1)}, bf16[16,5120]{1,0:T(8,128)(2,1)S(1)}, u32[]{:S(2)}, u32[]{:S(2)}) %collective-permute-start.37) | collective-permute-done | bytes 163872 | tf_op jit(solution)/shard_map/ppermute | solution.py:552
  277.3 4.3 %collective-permute-done.39.d_ref = bf16[16,5120]{1,0:T(8,128)(2,1)S(1)} collective-permute-done((bf16[16,5120]{1,0:T(8,128)(2,1)S(1)}, bf16[16,5120]{1,0:T(8,128)(2,1)S(1)}, u32[]{:S(2)}, u32[]{:S(2)}) %collective-permute-start.39) | collective-permute-done | bytes 163872 | tf_op jit(solution)/shard_map/ppermute | solution.py:552
  291.5 16.8 %all_to_all.35.refs_2_ = f32[128,1,128]{2,1,0:T(1,128)S(1)} all-to-all(f32[128,1,128]{2,1,0:T(1,128)} %get-tuple-element.148), channel_id=1, replica_groups=mesh['x'=4,'z'=4,'y'=4,'c'=2] {'x','z','y','c'}, dimensions={0} | all-to-all | bytes 131072 | tf_op jit(solution)/shard_map/all_to_all | solution.py:588
  (147 shorter events, 68.3 us)
Async XLA Ops:
  1.1 10.1 %collective-permute-start.2 = (bf16[128,640]{1,0:T(8,128)(2,1)S(1)}, bf16[128,640]{1,0:T(8,128)(2,1)S(1)}, u32[]{:S(2)}, u32[]{:S(2)}) collective-permute-start(bf16[128,640]{1,0:T(8,128)(2,1)S(1)} %get-tuple-element.82), channel_id=1, source_target_pairs={{0,6},{2,0},{4,2},{6,4},{1,7},{3,1},{5,3},{7,5},{8,14},{10,8},{12,... | collective-permute-start | bytes 491528 | tf_op jit(solution)/shard_map/ppermute | solution.py:465
  4.7 6.4 %collective-permute-start.1 = (bf16[128,640]{1,0:T(8,128)(2,1)S(1)}, bf16[128,640]{1,0:T(8,128)(2,1)S(1)}, u32[]{:S(2)}, u32[]{:S(2)}) collective-permute-start(bf16[128,640]{1,0:T(8,128)(2,1)S(1)} %get-tuple-element.82), channel_id=1, source_target_pairs={{0,4},{2,6},{4,0},{6,2},{1,5},{3,7},{5,1},{7,3},{8,12},{10,14},{12... | collective-permute-start | bytes 491528 | tf_op jit(solution)/shard_map/ppermute | solution.py:465
  5.1 10.8 %collective-permute-start = (bf16[128,640]{1,0:T(8,128)(2,1)S(1)}, bf16[128,640]{1,0:T(8,128)(2,1)S(1)}, u32[]{:S(2)}, u32[]{:S(2)}) collective-permute-start(bf16[128,640]{1,0:T(8,128)(2,1)S(1)} %get-tuple-element.82), channel_id=1, source_target_pairs={{0,2},{2,4},{4,6},{6,0},{1,3},{3,5},{5,7},{7,1},{8,10},{10,12},{12... | collective-permute-start | bytes 491528 | tf_op jit(solution)/shard_map/ppermute | solution.py:465
  22.2 23.3 %all-to-all-start = ((bf16[16,128,256]{2,1,0:T(8,128)(2,1)}), bf16[16,128,256]{2,1,0:T(8,128)(2,1)S(1)}, u32[]{:S(2)}, u32[]{:S(2)}) async-start(bf16[16,128,256]{2,1,0:T(8,128)(2,1)} %get-tuple-element.85), calls=%async_computation | async-start | bytes 2097152 | tf_op jit(solution)/shard_map/all_to_all | solution.py:520
  29.8 3.4 %collective-permute-start.6 = (bf16[2,2,16,640]{3,2,1,0:T(8,128)(2,1)S(1)}, bf16[2,2,16,640]{3,2,1,0:T(8,128)(2,1)S(1)}, u32[]{:S(2)}, u32[]{:S(2)}) collective-permute-start(bf16[2,2,16,640]{3,2,1,0:T(8,128)(2,1)S(1)} %get-tuple-element.89), channel_id=1, source_target_pairs={{0,6},{2,0},{4,2},{6,4},{1,7},{3,1},{5,3},{7,5},{8,14},{10,8},{12,... | collective-permute-start | bytes 245768 | tf_op jit(solution)/shard_map/ppermute | solution.py:426
  30.2 5.1 %collective-permute-start.5 = (bf16[2,2,16,640]{3,2,1,0:T(8,128)(2,1)S(1)}, bf16[2,2,16,640]{3,2,1,0:T(8,128)(2,1)S(1)}, u32[]{:S(2)}, u32[]{:S(2)}) collective-permute-start(bf16[2,2,16,640]{3,2,1,0:T(8,128)(2,1)S(1)} %get-tuple-element.88), channel_id=1, source_target_pairs={{0,4},{2,6},{4,0},{6,2},{1,5},{3,7},{5,1},{7,3},{8,12},{10,14},{12... | collective-permute-start | bytes 245768 | tf_op jit(solution)/shard_map/ppermute | solution.py:426
  30.5 6.8 %collective-permute-start.4 = (bf16[2,2,16,640]{3,2,1,0:T(8,128)(2,1)S(1)}, bf16[2,2,16,640]{3,2,1,0:T(8,128)(2,1)S(1)}, u32[]{:S(2)}, u32[]{:S(2)}) collective-permute-start(bf16[2,2,16,640]{3,2,1,0:T(8,128)(2,1)S(1)} %get-tuple-element.87), channel_id=1, source_target_pairs={{0,2},{2,4},{4,6},{6,0},{1,3},{3,5},{5,7},{7,1},{8,10},{10,12},{12... | collective-permute-start | bytes 245768 | tf_op jit(solution)/shard_map/ppermute | solution.py:426
  37.4 6.6 %collective-permute-start.7 = (bf16[4,2,16,640]{3,2,1,0:T(8,128)(2,1)S(1)}, bf16[4,2,16,640]{3,2,1,0:T(8,128)(2,1)S(1)}, u32[]{:S(2)}, u32[]{:S(2)}) collective-permute-start(bf16[4,2,16,640]{3,2,1,0:T(8,128)(2,1)S(1)} %pad_maximum_fusion.2), channel_id=1, source_target_pairs={{0,1},{1,0},{2,3},{3,2},{4,5},{5,4},{6,7},{7,6},{8,9},{9,8},{10,11... | collective-permute-start | bytes 491528 | tf_op jit(solution)/shard_map/ppermute | solution.py:428
  51.4 4.9 %collective-permute-start.8 = (bf16[64,5120]{1,0:T(8,128)(2,1)S(1)}, bf16[64,5120]{1,0:T(8,128)(2,1)S(1)}, u32[]{:S(2)}, u32[]{:S(2)}) collective-permute-start(bf16[64,5120]{1,0:T(8,128)(2,1)S(1)} %get-tuple-element.93), channel_id=1, source_target_pairs={{0,1},{1,0},{2,3},{3,2},{4,5},{5,4},{6,7},{7,6},{8,9},{9,8},{10,11... | collective-permute-start | bytes 1966088 | tf_op jit(solution)/shard_map/ppermute | solution.py:548
  56.6 5.5 %collective-permute-start.9 = (bf16[16,5120]{1,0:T(8,128)(2,1)S(1)}, bf16[16,5120]{1,0:T(8,128)(2,1)S(1)}, u32[]{:S(2)}, u32[]{:S(2)}) collective-permute-start(bf16[16,5120]{1,0:T(8,128)(2,1)S(1)} %get-tuple-element.178), channel_id=1, source_target_pairs={{0,6},{2,0},{4,2},{6,4},{1,7},{3,1},{5,3},{7,5},{8,14},{10,8},{12,... | collective-permute-start | bytes 491528 | tf_op jit(solution)/shard_map/ppermute | solution.py:552
  57.0 6.6 %collective-permute-start.10 = (bf16[16,5120]{1,0:T(8,128)(2,1)S(1)}, bf16[16,5120]{1,0:T(8,128)(2,1)S(1)}, u32[]{:S(2)}, u32[]{:S(2)}) collective-permute-start(bf16[16,5120]{1,0:T(8,128)(2,1)S(1)} %get-tuple-element.177), channel_id=1, source_target_pairs={{0,4},{2,6},{4,0},{6,2},{1,5},{3,7},{5,1},{7,3},{8,12},{10,14},{12... | collective-permute-start | bytes 491528 | tf_op jit(solution)/shard_map/ppermute | solution.py:552
  57.3 10.8 %collective-permute-start.11 = (bf16[16,5120]{1,0:T(8,128)(2,1)S(1)}, bf16[16,5120]{1,0:T(8,128)(2,1)S(1)}, u32[]{:S(2)}, u32[]{:S(2)}) collective-permute-start(bf16[16,5120]{1,0:T(8,128)(2,1)S(1)} %get-tuple-element.176), channel_id=1, source_target_pairs={{0,2},{2,4},{4,6},{6,0},{1,3},{3,5},{5,7},{7,1},{8,10},{10,12},{12... | collective-permute-start | bytes 491528 | tf_op jit(solution)/shard_map/ppermute | solution.py:552
  69.4 10.3 %collective-permute-start.12 = (bf16[16,5120]{1,0:T(8,128)(2,1)S(1)}, bf16[16,5120]{1,0:T(8,128)(2,1)S(1)}, u32[]{:S(2)}, u32[]{:S(2)}) collective-permute-start(bf16[16,5120]{1,0:T(8,128)(2,1)S(1)} %get-tuple-element.101), channel_id=1, source_target_pairs={{0,2},{2,4},{4,6},{6,0},{1,3},{3,5},{5,7},{7,1},{8,10},{10,12},{12... | collective-permute-start | bytes 491528 | tf_op jit(solution)/shard_map/ppermute | solution.py:465
  69.5 10.2 %collective-permute-start.13 = (bf16[16,5120]{1,0:T(8,128)(2,1)S(1)}, bf16[16,5120]{1,0:T(8,128)(2,1)S(1)}, u32[]{:S(2)}, u32[]{:S(2)}) collective-permute-start(bf16[16,5120]{1,0:T(8,128)(2,1)S(1)} %get-tuple-element.101), channel_id=1, source_target_pairs={{0,4},{2,6},{4,0},{6,2},{1,5},{3,7},{5,1},{7,3},{8,12},{10,14},{12... | collective-permute-start | bytes 491528 | tf_op jit(solution)/shard_map/ppermute | solution.py:465
  70.6 9.4 %collective-permute-start.14 = (bf16[16,5120]{1,0:T(8,128)(2,1)S(1)}, bf16[16,5120]{1,0:T(8,128)(2,1)S(1)}, u32[]{:S(2)}, u32[]{:S(2)}) collective-permute-start(bf16[16,5120]{1,0:T(8,128)(2,1)S(1)} %get-tuple-element.101), channel_id=1, source_target_pairs={{0,6},{2,0},{4,2},{6,4},{1,7},{3,1},{5,3},{7,5},{8,14},{10,8},{12,... | collective-permute-start | bytes 491528 | tf_op jit(solution)/shard_map/ppermute | solution.py:465
  80.0 3.4 %collective-permute-start.15 = (bf16[64,5120]{1,0:T(8,128)(2,1)S(1)}, bf16[64,5120]{1,0:T(8,128)(2,1)S(1)}, u32[]{:S(2)}, u32[]{:S(2)}) collective-permute-start(bf16[64,5120]{1,0:T(8,128)(2,1)S(1)} %constant_dynamic-update-slice_fusion.refs_3_), channel_id=1, source_target_pairs={{0,1},{1,0},{2,3},{3,2},{4,5},{5,4},{6,7},{7,6},{8,9},{9,8},{10,11... | collective-permute-start | bytes 1966088 | tf_op jit(solution)/shard_map/ppermute | solution.py:469
  86.8 19.9 %all-to-all-start.1 = ((bf16[16,128,256]{2,1,0:T(8,128)(2,1)}), bf16[16,128,256]{2,1,0:T(8,128)(2,1)S(1)}, u32[]{:S(2)}, u32[]{:S(2)}) async-start(bf16[16,128,256]{2,1,0:T(8,128)(2,1)} %get-tuple-element.104), calls=%async_computation.1 | async-start | bytes 2097152 | tf_op jit(solution)/shard_map/all_to_all | solution.py:520
  112.6 4.3 %collective-permute-start.16 = (bf16[64,5120]{1,0:T(8,128)(2,1)S(1)}, bf16[64,5120]{1,0:T(8,128)(2,1)S(1)}, u32[]{:S(2)}, u32[]{:S(2)}) collective-permute-start(bf16[64,5120]{1,0:T(8,128)(2,1)S(1)} %get-tuple-element.106), channel_id=1, source_target_pairs={{0,1},{1,0},{2,3},{3,2},{4,5},{5,4},{6,7},{7,6},{8,9},{9,8},{10,11... | collective-permute-start | bytes 1966088 | tf_op jit(solution)/shard_map/ppermute | solution.py:548
  117.2 6.0 %collective-permute-start.17 = (bf16[16,5120]{1,0:T(8,128)(2,1)S(1)}, bf16[16,5120]{1,0:T(8,128)(2,1)S(1)}, u32[]{:S(2)}, u32[]{:S(2)}) collective-permute-start(bf16[16,5120]{1,0:T(8,128)(2,1)S(1)} %get-tuple-element.175), channel_id=1, source_target_pairs={{0,6},{2,0},{4,2},{6,4},{1,7},{3,1},{5,3},{7,5},{8,14},{10,8},{12,... | collective-permute-start | bytes 491528 | tf_op jit(solution)/shard_map/ppermute | solution.py:552
  119.5 6.7 %collective-permute-start.18 = (bf16[16,5120]{1,0:T(8,128)(2,1)S(1)}, bf16[16,5120]{1,0:T(8,128)(2,1)S(1)}, u32[]{:S(2)}, u32[]{:S(2)}) collective-permute-start(bf16[16,5120]{1,0:T(8,128)(2,1)S(1)} %get-tuple-element.174), channel_id=1, source_target_pairs={{0,4},{2,6},{4,0},{6,2},{1,5},{3,7},{5,1},{7,3},{8,12},{10,14},{12... | collective-permute-start | bytes 491528 | tf_op jit(solution)/shard_map/ppermute | solution.py:552
  119.5 10.6 %collective-permute-start.19 = (bf16[16,5120]{1,0:T(8,128)(2,1)S(1)}, bf16[16,5120]{1,0:T(8,128)(2,1)S(1)}, u32[]{:S(2)}, u32[]{:S(2)}) collective-permute-start(bf16[16,5120]{1,0:T(8,128)(2,1)S(1)} %get-tuple-element.173), channel_id=1, source_target_pairs={{0,2},{2,4},{4,6},{6,0},{1,3},{3,5},{5,7},{7,1},{8,10},{10,12},{12... | collective-permute-start | bytes 491528 | tf_op jit(solution)/shard_map/ppermute | solution.py:552
  131.6 10.2 %collective-permute-start.20 = (bf16[16,5120]{1,0:T(8,128)(2,1)S(1)}, bf16[16,5120]{1,0:T(8,128)(2,1)S(1)}, u32[]{:S(2)}, u32[]{:S(2)}) collective-permute-start(bf16[16,5120]{1,0:T(8,128)(2,1)S(1)} %get-tuple-element.116), channel_id=1, source_target_pairs={{0,2},{2,4},{4,6},{6,0},{1,3},{3,5},{5,7},{7,1},{8,10},{10,12},{12... | collective-permute-start | bytes 491528 | tf_op jit(solution)/shard_map/ppermute | solution.py:465
  131.7 10.1 %collective-permute-start.21 = (bf16[16,5120]{1,0:T(8,128)(2,1)S(1)}, bf16[16,5120]{1,0:T(8,128)(2,1)S(1)}, u32[]{:S(2)}, u32[]{:S(2)}) collective-permute-start(bf16[16,5120]{1,0:T(8,128)(2,1)S(1)} %get-tuple-element.116), channel_id=1, source_target_pairs={{0,4},{2,6},{4,0},{6,2},{1,5},{3,7},{5,1},{7,3},{8,12},{10,14},{12... | collective-permute-start | bytes 491528 | tf_op jit(solution)/shard_map/ppermute | solution.py:465
  132.9 9.0 %collective-permute-start.22 = (bf16[16,5120]{1,0:T(8,128)(2,1)S(1)}, bf16[16,5120]{1,0:T(8,128)(2,1)S(1)}, u32[]{:S(2)}, u32[]{:S(2)}) collective-permute-start(bf16[16,5120]{1,0:T(8,128)(2,1)S(1)} %get-tuple-element.116), channel_id=1, source_target_pairs={{0,6},{2,0},{4,2},{6,4},{1,7},{3,1},{5,3},{7,5},{8,14},{10,8},{12,... | collective-permute-start | bytes 491528 | tf_op jit(solution)/shard_map/ppermute | solution.py:465
  141.8 7.0 %collective-permute-start.23 = (bf16[64,5120]{1,0:T(8,128)(2,1)S(1)}, bf16[64,5120]{1,0:T(8,128)(2,1)S(1)}, u32[]{:S(2)}, u32[]{:S(2)}) collective-permute-start(bf16[64,5120]{1,0:T(8,128)(2,1)S(1)} %constant_dynamic-update-slice_fusion.4.refs_4_), channel_id=1, source_target_pairs={{0,1},{1,0},{2,3},{3,2},{4,5},{5,4},{6,7},{7,6},{8,9},{9,8},{10,11... | collective-permute-start | bytes 1966088 | tf_op jit(solution)/shard_map/ppermute | solution.py:469
  143.8 14.5 %all-to-all-start.2 = ((f32[128,1,128]{2,1,0:T(1,128)}), f32[128,1,128]{2,1,0:T(1,128)S(1)}, u32[]{:S(2)}, u32[]{:S(2)}) async-start(f32[128,1,128]{2,1,0:T(1,128)} %get-tuple-element.114), calls=%async_computation.2 | async-start | bytes 131072 | tf_op jit(solution)/shard_map/all_to_all | solution.py:467
  159.8 19.3 %all-to-all-start.3 = ((bf16[16,128,256]{2,1,0:T(8,128)(2,1)}), bf16[16,128,256]{2,1,0:T(8,128)(2,1)S(1)}, u32[]{:S(2)}, u32[]{:S(2)}) async-start(bf16[16,128,256]{2,1,0:T(8,128)(2,1)} %get-tuple-element.121), calls=%async_computation.3 | async-start | bytes 2097152 | tf_op jit(solution)/shard_map/all_to_all | solution.py:520
  185.1 4.8 %collective-permute-start.24 = (bf16[64,5120]{1,0:T(8,128)(2,1)S(1)}, bf16[64,5120]{1,0:T(8,128)(2,1)S(1)}, u32[]{:S(2)}, u32[]{:S(2)}) collective-permute-start(bf16[64,5120]{1,0:T(8,128)(2,1)S(1)} %get-tuple-element.123), channel_id=1, source_target_pairs={{0,1},{1,0},{2,3},{3,2},{4,5},{5,4},{6,7},{7,6},{8,9},{9,8},{10,11... | collective-permute-start | bytes 1966088 | tf_op jit(solution)/shard_map/ppermute | solution.py:548
  190.2 5.5 %collective-permute-start.25 = (bf16[16,5120]{1,0:T(8,128)(2,1)S(1)}, bf16[16,5120]{1,0:T(8,128)(2,1)S(1)}, u32[]{:S(2)}, u32[]{:S(2)}) collective-permute-start(bf16[16,5120]{1,0:T(8,128)(2,1)S(1)} %get-tuple-element.172), channel_id=1, source_target_pairs={{0,6},{2,0},{4,2},{6,4},{1,7},{3,1},{5,3},{7,5},{8,14},{10,8},{12,... | collective-permute-start | bytes 491528 | tf_op jit(solution)/shard_map/ppermute | solution.py:552
  191.3 6.6 %collective-permute-start.26 = (bf16[16,5120]{1,0:T(8,128)(2,1)S(1)}, bf16[16,5120]{1,0:T(8,128)(2,1)S(1)}, u32[]{:S(2)}, u32[]{:S(2)}) collective-permute-start(bf16[16,5120]{1,0:T(8,128)(2,1)S(1)} %get-tuple-element.171), channel_id=1, source_target_pairs={{0,4},{2,6},{4,0},{6,2},{1,5},{3,7},{5,1},{7,3},{8,12},{10,14},{12... | collective-permute-start | bytes 491528 | tf_op jit(solution)/shard_map/ppermute | solution.py:552
  192.4 10.1 %collective-permute-start.27 = (bf16[16,5120]{1,0:T(8,128)(2,1)S(1)}, bf16[16,5120]{1,0:T(8,128)(2,1)S(1)}, u32[]{:S(2)}, u32[]{:S(2)}) collective-permute-start(bf16[16,5120]{1,0:T(8,128)(2,1)S(1)} %get-tuple-element.170), channel_id=1, source_target_pairs={{0,2},{2,4},{4,6},{6,0},{1,3},{3,5},{5,7},{7,1},{8,10},{10,12},{12... | collective-permute-start | bytes 491528 | tf_op jit(solution)/shard_map/ppermute | solution.py:552
  203.9 10.3 %collective-permute-start.28 = (bf16[16,5120]{1,0:T(8,128)(2,1)S(1)}, bf16[16,5120]{1,0:T(8,128)(2,1)S(1)}, u32[]{:S(2)}, u32[]{:S(2)}) collective-permute-start(bf16[16,5120]{1,0:T(8,128)(2,1)S(1)} %get-tuple-element.132), channel_id=1, source_target_pairs={{0,2},{2,4},{4,6},{6,0},{1,3},{3,5},{5,7},{7,1},{8,10},{10,12},{12... | collective-permute-start | bytes 491528 | tf_op jit(solution)/shard_map/ppermute | solution.py:465
  204.0 10.2 %collective-permute-start.29 = (bf16[16,5120]{1,0:T(8,128)(2,1)S(1)}, bf16[16,5120]{1,0:T(8,128)(2,1)S(1)}, u32[]{:S(2)}, u32[]{:S(2)}) collective-permute-start(bf16[16,5120]{1,0:T(8,128)(2,1)S(1)} %get-tuple-element.132), channel_id=1, source_target_pairs={{0,4},{2,6},{4,0},{6,2},{1,5},{3,7},{5,1},{7,3},{8,12},{10,14},{12... | collective-permute-start | bytes 491528 | tf_op jit(solution)/shard_map/ppermute | solution.py:465
  205.2 9.3 %collective-permute-start.30 = (bf16[16,5120]{1,0:T(8,128)(2,1)S(1)}, bf16[16,5120]{1,0:T(8,128)(2,1)S(1)}, u32[]{:S(2)}, u32[]{:S(2)}) collective-permute-start(bf16[16,5120]{1,0:T(8,128)(2,1)S(1)} %get-tuple-element.132), channel_id=1, source_target_pairs={{0,6},{2,0},{4,2},{6,4},{1,7},{3,1},{5,3},{7,5},{8,14},{10,8},{12,... | collective-permute-start | bytes 491528 | tf_op jit(solution)/shard_map/ppermute | solution.py:465
  214.5 6.8 %collective-permute-start.31 = (bf16[64,5120]{1,0:T(8,128)(2,1)S(1)}, bf16[64,5120]{1,0:T(8,128)(2,1)}, u32[]{:S(2)}, u32[]{:S(2)}) collective-permute-start(bf16[64,5120]{1,0:T(8,128)(2,1)S(1)} %constant_dynamic-update-slice_fusion.8.refs_5_), channel_id=1, source_target_pairs={{0,1},{1,0},{2,3},{3,2},{4,5},{5,4},{6,7},{7,6},{8,9},{9,8},{10,11... | collective-permute-start | bytes 1966088 | tf_op jit(solution)/shard_map/ppermute | solution.py:469
  216.2 14.6 %all-to-all-start.4 = ((f32[128,1,128]{2,1,0:T(1,128)}), f32[128,1,128]{2,1,0:T(1,128)S(1)}, u32[]{:S(2)}, u32[]{:S(2)}) async-start(f32[128,1,128]{2,1,0:T(1,128)} %get-tuple-element.131), calls=%async_computation.4 | async-start | bytes 131072 | tf_op jit(solution)/shard_map/all_to_all | solution.py:467
  232.4 29.4 %all-to-all-start.5 = ((bf16[16,128,256]{2,1,0:T(8,128)(2,1)}), bf16[16,128,256]{2,1,0:T(8,128)(2,1)S(1)}, u32[]{:S(2)}, u32[]{:S(2)}) async-start(bf16[16,128,256]{2,1,0:T(8,128)(2,1)} %get-tuple-element.137), calls=%async_computation.5 | async-start | bytes 2097152 | tf_op jit(solution)/shard_map/all_to_all | solution.py:520
  236.2 8.1 %collective-permute-start.34 = (f32[2,3,16,640]{3,2,1,0:T(8,128)}, f32[2,3,16,640]{3,2,1,0:T(8,128)S(1)}, u32[]{:S(2)}, u32[]{:S(2)}) collective-permute-start(f32[2,3,16,640]{3,2,1,0:T(8,128)} %get-tuple-element.141), channel_id=1, source_target_pairs={{0,6},{2,0},{4,2},{6,4},{1,7},{3,1},{5,3},{7,5},{8,14},{10,8},{12,... | collective-permute-start | bytes 737288 | tf_op jit(solution)/shard_map/ppermute | solution.py:426
  238.5 8.3 %collective-permute-start.33 = (f32[2,3,16,640]{3,2,1,0:T(8,128)}, f32[2,3,16,640]{3,2,1,0:T(8,128)S(1)}, u32[]{:S(2)}, u32[]{:S(2)}) collective-permute-start(f32[2,3,16,640]{3,2,1,0:T(8,128)} %get-tuple-element.140), channel_id=1, source_target_pairs={{0,4},{2,6},{4,0},{6,2},{1,5},{3,7},{5,1},{7,3},{8,12},{10,14},{12... | collective-permute-start | bytes 737288 | tf_op jit(solution)/shard_map/ppermute | solution.py:426
  239.0 14.3 %collective-permute-start.32 = (f32[2,3,16,640]{3,2,1,0:T(8,128)S(1)}, f32[2,3,16,640]{3,2,1,0:T(8,128)S(1)}, u32[]{:S(2)}, u32[]{:S(2)}) collective-permute-start(f32[2,3,16,640]{3,2,1,0:T(8,128)S(1)} %copy-done.16), channel_id=1, source_target_pairs={{0,2},{2,4},{4,6},{6,0},{1,3},{3,5},{5,7},{7,1},{8,10},{10,12},{12... | collective-permute-start | bytes 737288 | tf_op jit(solution)/shard_map/ppermute | solution.py:426
  254.1 6.8 %collective-permute-start.35 = (f32[4,3,16,640]{3,2,1,0:T(8,128)S(1)}, f32[4,3,16,640]{3,2,1,0:T(8,128)S(1)}, u32[]{:S(2)}, u32[]{:S(2)}) collective-permute-start(f32[4,3,16,640]{3,2,1,0:T(8,128)S(1)} %pad_maximum_fusion.1), channel_id=1, source_target_pairs={{0,1},{1,0},{2,3},{3,2},{4,5},{5,4},{6,7},{7,6},{8,9},{9,8},{10,11... | collective-permute-start | bytes 1474568 | tf_op jit(solution)/shard_map/ppermute | solution.py:428
  270.0 5.7 %collective-permute-start.37 = (bf16[16,5120]{1,0:T(8,128)(2,1)S(1)}, bf16[16,5120]{1,0:T(8,128)(2,1)S(1)}, u32[]{:S(2)}, u32[]{:S(2)}) collective-permute-start(bf16[16,5120]{1,0:T(8,128)(2,1)S(1)} %get-tuple-element.169), channel_id=1, source_target_pairs={{0,6},{2,0},{4,2},{6,4},{1,7},{3,1},{5,3},{7,5},{8,14},{10,8},{12,... | collective-permute-start | bytes 491528 | tf_op jit(solution)/shard_map/ppermute | solution.py:552
  270.4 6.9 %collective-permute-start.38 = (bf16[16,5120]{1,0:T(8,128)(2,1)S(1)}, bf16[16,5120]{1,0:T(8,128)(2,1)S(1)}, u32[]{:S(2)}, u32[]{:S(2)}) collective-permute-start(bf16[16,5120]{1,0:T(8,128)(2,1)S(1)} %get-tuple-element.168), channel_id=1, source_target_pairs={{0,4},{2,6},{4,0},{6,2},{1,5},{3,7},{5,1},{7,3},{8,12},{10,14},{12... | collective-permute-start | bytes 491528 | tf_op jit(solution)/shard_map/ppermute | solution.py:552
  271.0 10.6 %collective-permute-start.39 = (bf16[16,5120]{1,0:T(8,128)(2,1)S(1)}, bf16[16,5120]{1,0:T(8,128)(2,1)S(1)}, u32[]{:S(2)}, u32[]{:S(2)}) collective-permute-start(bf16[16,5120]{1,0:T(8,128)(2,1)S(1)} %get-tuple-element.167), channel_id=1, source_target_pairs={{0,2},{2,4},{4,6},{6,0},{1,3},{3,5},{5,7},{7,1},{8,10},{10,12},{12... | collective-permute-start | bytes 491528 | tf_op jit(solution)/shard_map/ppermute | solution.py:552
  282.9 3.6 %collective-permute-start.42 = (f32[2,1,16,640]{3,2,1,0:T(8,128)}, f32[2,1,16,640]{3,2,1,0:T(8,128)S(1)}, u32[]{:S(2)}, u32[]{:S(2)}) collective-permute-start(f32[2,1,16,640]{3,2,1,0:T(8,128)} %get-tuple-element.157), channel_id=1, source_target_pairs={{0,6},{2,0},{4,2},{6,4},{1,7},{3,1},{5,3},{7,5},{8,14},{10,8},{12,... | collective-permute-start | bytes 245768 | tf_op jit(solution)/shard_map/ppermute | solution.py:426
  283.1 5.0 %collective-permute-start.41 = (f32[2,1,16,640]{3,2,1,0:T(8,128)}, f32[2,1,16,640]{3,2,1,0:T(8,128)S(1)}, u32[]{:S(2)}, u32[]{:S(2)}) collective-permute-start(f32[2,1,16,640]{3,2,1,0:T(8,128)} %get-tuple-element.156), channel_id=1, source_target_pairs={{0,4},{2,6},{4,0},{6,2},{1,5},{3,7},{5,1},{7,3},{8,12},{10,14},{12... | collective-permute-start | bytes 245768 | tf_op jit(solution)/shard_map/ppermute | solution.py:426
  283.6 6.1 %collective-permute-start.40 = (f32[2,1,16,640]{3,2,1,0:T(8,128)}, f32[2,1,16,640]{3,2,1,0:T(8,128)S(1)}, u32[]{:S(2)}, u32[]{:S(2)}) collective-permute-start(f32[2,1,16,640]{3,2,1,0:T(8,128)} %get-tuple-element.155), channel_id=1, source_target_pairs={{0,2},{2,4},{4,6},{6,0},{1,3},{3,5},{5,7},{7,1},{8,10},{10,12},{12... | collective-permute-start | bytes 245768 | tf_op jit(solution)/shard_map/ppermute | solution.py:426
  289.7 18.7 %collective-permute-start.43 = (f32[4,1,16,640]{3,2,1,0:T(8,128)S(1)}, f32[4,1,16,640]{3,2,1,0:T(8,128)S(1)}, u32[]{:S(2)}, u32[]{:S(2)}) collective-permute-start(f32[4,1,16,640]{3,2,1,0:T(8,128)S(1)} %pad_maximum_fusion.3), channel_id=1, source_target_pairs={{0,1},{1,0},{2,3},{3,2},{4,5},{5,4},{6,7},{7,6},{8,9},{9,8},{10,11... | collective-permute-start | bytes 491528 | tf_op jit(solution)/shard_map/ppermute | solution.py:428
  (19 other events, 234.9 us)

commit v2 on v1

--- a/solution.py
+++ b/solution.py
@@ -274,7 +274,7 @@
 
 def finish_kernel(k, own_ref, a_ref, b_ref, d_ref, inj_ref, x_ref, gain_ref, gain_in_ref, *rest):
     older, rest = rest[:k], rest[k:]
-    if k in (1, 2):
+    if k % 2 == 1:
         rest = rest[5:]
     image_held, residual_held, dots_held, sem = rest[-4:]
     image_out, residual_out, *home_out = rest[:7]
@@ -291,7 +291,7 @@
         pltpu.make_async_copy(image_held, image_out, sem.at[0]),
         pltpu.make_async_copy(residual_held, residual_out, sem.at[1]),
     ]
-    copies += home_copies(image_held, home_out, k % (ITERS - 1), sem, 2)
+    copies += home_copies(image_held, home_out, k % 2, sem, 2)
     for copy in copies:
         copy.start()
     if k < ITERS - 1:
@@ -372,9 +372,9 @@
         for half in range(2):
             row = (((y - by + 4) % 4) * 2 + (c + half) % 2) * 16
             rows = pl.ds(pl.multiple_of(row, 16), 16)
-            mixed = shares[k] * piece(newest, by, half, 0)
-            for at in range(k):
-                mixed = mixed + shares[at] * piece(older, by, half, at)
+            mixed = jnp.zeros((16, 640), F32)
+            for at in range(k + 1):
+                mixed = mixed + shares[at] * piece(older if at < 2 else newest, by, half, at % 2)
             out_ref[rows, :] = mixed
     store = pltpu.make_async_copy(out_ref, out_hbm, sem)
     store.start()
@@ -423,7 +423,9 @@
 
 def move_home(pieces):
     own, pair, *far = pieces
-    near = [lax.ppermute(piece, "y", shift(4, by + 1)) for by, piece in enumerate(far)]
+    near = []
+    for by, piece in enumerate(far):
+        near.append(lax.ppermute(piece, "y", shift(4, by + 1)))
     joined = jnp.stack([pair] + [piece[1] for piece in near])
     return [own, *near, lax.ppermute(joined, "c", shift(2, 1))]
 
@@ -434,8 +436,7 @@
     wide = pltpu.VMEM((16, D), F32)
     narrow = pltpu.VMEM((16, D), BF16)
     home_narrow = [pltpu.VMEM((2, 16, 640), BF16)] * 2 + [pltpu.VMEM((2, 2, 16, 640), BF16)] * 3
-    home_packed = [pltpu.HBM((3, 16, 640), F32)] * 2 + [pltpu.HBM((2, 3, 16, 640), F32)] * 3
-    home_last = [pltpu.VMEM((1, 16, 640), F32)] * 2 + [pltpu.HBM((2, 1, 16, 640), F32)] * 3
+    home_packed = [pltpu.HBM((2, 16, 640), F32)] * 2 + [pltpu.HBM((2, 2, 16, 640), F32)] * 3
     payload, *home = call(
         start_kernel,
         (pltpu.VMEM((128, 640), BF16), *home_narrow),
@@ -519,12 +520,12 @@
             )
         kv_all = lax.all_to_all(kv, SEQ, split_axis=0, concat_axis=0, tiled=True)
         q = query_dot(share, parts, w_query)
-        if k in (0, ITERS - 1):
+        if k in (0, 2):
             home = move_home(home)
             kv_all, home = lax.optimization_barrier((kv_all, home))
         if k == 0:
             inj, current = call(settle_kernel, (narrow, narrow), *home)
-        if k == ITERS - 1:
+        if k == 2:
             settled = home
         if k > 1:
             current = call(mix_kernel, wide, share, *images)
@@ -550,12 +551,12 @@
         for by in (1, 2, 3):
             piece = pair[16 * by : 16 * by + 16].astype(BF16)
             arrived.append(lax.ppermute(piece, "y", shift(4, -by)))
-        shapes = [tokens, tokens, *(home_packed if k < ITERS - 1 else home_last)]
+        shapes = [tokens, tokens, *home_packed]
         if k < ITERS - 1:
             shapes.append(narrow)
         if k > 0:
             shapes.append(pltpu.HBM((128, 1, 128), F32))
-        packed = list(home) if k in (1, 2) else []
+        packed = list(home) if k % 2 == 1 else []
         outs = call(
             functools.partial(finish_kernel, k),
             tuple(shapes),

time: 311 us -> 310 us (level)
  blocking collectives: 16.8 us -> 13.3 us
  starting transfers between devices: 75.7 us -> 78.9 us
    all_to_all x1, blocking collectives: 16.8 us -> 13.3 us  [on_device(): lax.all_to_all(dots, EVERY, split_axis=0, concat_axis=0, tiled=True)]
    all_to_all x2, starting transfers between devices: 10.1 us -> 13.5 us  [on_device(): lax.all_to_all(dots, EVERY, split_axis=0, concat_axis=0, tiled=True)]
where the time goes in v2:
time: 310 us; the launch traced here: 309 us
  waiting for transfers between devices  139 us (45%)
  starting transfers between devices  78.9 us (25%)
  Pallas kernels  74.6 us (24%)
  blocking collectives  13.3 us (4%)
    pallas_call x19, Pallas kernels, call(): pl.pallas_call(kernel, out_shape=outs, in_specs=specs, input_output_alias...  51.5 us
    ppermute x12, waiting for transfers between devices, on_device(): arrived.append(lax.ppermute(piece, 'y', shift(4, -by)))  39 us
    ppermute x12, waiting for transfers between devices, on_device(): pieces.append(lax.ppermute(payload, 'y', shift(4, by)))  32.2 us
    ppermute x9, waiting for transfers between devices, move_home(): near.append(lax.ppermute(piece, 'y', shift(4, by + 1)))  25.9 us
    pallas_call x4, Pallas kernels, query_dot(): pl.pallas_call(functools.partial(query_kernel, len(parts) - 1), grid=(5,)...  23.1 us
    all_to_all x4, waiting for transfers between devices, on_device(): kv_all = lax.all_to_all(kv, SEQ, split_axis=0, concat_axis=0, tiled=True)  21.6 us
    all_to_all x4, starting transfers between devices, on_device(): kv_all = lax.all_to_all(kv, SEQ, split_axis=0, concat_axis=0, tiled=True)  18.7 us
    ppermute x12, starting transfers between devices, on_device(): pieces.append(lax.ppermute(payload, 'y', shift(4, by)))  13.7 us
  transfers between devices with their start and end apart: 50, of which 39 were waited for; matrix products, arithmetic and copies ran while one was open for 0% of the time, Pallas kernels for 11%

profile of v2, /device:TPU:1, one launch (start us, length us, event | category | flops | bytes accessed | tf_op | source)
XLA Modules:
  0.0 308.6 jit_solution(941595136600240443)
XLA Ops:
  1.1 3.6 %collective-permute-start.2 = (bf16[128,640]{1,0:T(8,128)(2,1)S(1)}, bf16[128,640]{1,0:T(8,128)(2,1)S(1)}, u32[]{:S(2)}, u32[]{:S(2)}) collective-permute-start(bf16[128,640]{1,0:T(8,128)(2,1)S(1)} %get-tuple-element.82), channel_id=1, source_target_pairs={{0,6},{2,0},{4,2},{6,4},{1,7},{3,1},{5,3},{7,5},{8,14},{10,8},{12,... | collective-permute-start | bytes 491528 | tf_op jit(solution)/shard_map/ppermute | solution.py:466
  5.8 5.4 %collective-permute-done.2 = bf16[128,640]{1,0:T(8,128)(2,1)S(1)} collective-permute-done((bf16[128,640]{1,0:T(8,128)(2,1)S(1)}, bf16[128,640]{1,0:T(8,128)(2,1)S(1)}, u32[]{:S(2)}, u32[]{:S(2)}) %collective-permute-start.2) | collective-permute-done | bytes 163872 | tf_op jit(solution)/shard_map/ppermute | solution.py:466
  11.2 4.7 %collective-permute-done = bf16[128,640]{1,0:T(8,128)(2,1)S(1)} collective-permute-done((bf16[128,640]{1,0:T(8,128)(2,1)S(1)}, bf16[128,640]{1,0:T(8,128)(2,1)S(1)}, u32[]{:S(2)}, u32[]{:S(2)}) %collective-permute-start) | collective-permute-done | bytes 163872 | tf_op jit(solution)/shard_map/ppermute | solution.py:466
  18.3 3.9 %shard_map.83 = (bf16[128,5120]{1,0:T(8,128)(2,1)}, f32[128,128]{1,0:T(8,128)S(1)}, bf16[16,128,256]{2,1,0:T(8,128)(2,1)}) custom-call(bf16[5120,128]{1,0:T(8,128)(2,1)} %refs_0_.5, bf16[5120,128]{1,0:T(8,128)(2,1)} %refs_1_.9, f32[1,5120]{1,0:T(1,128)S(1)} %bitcast.10, bf16[4,128,640]{2,1,0:T(8,128)(2,1)S(1)} %pad_maximum_fusion.refs_0_, ...), custom_call_target="tpu_custom_call" | custom-call | flops 335544320 | bytes 4000000 | tf_op jit(solution)/shard_map/pallas_call | solution.py:43
  22.2 7.6 %all-to-all-start = ((bf16[16,128,256]{2,1,0:T(8,128)(2,1)}), bf16[16,128,256]{2,1,0:T(8,128)(2,1)S(1)}, u32[]{:S(2)}, u32[]{:S(2)}) async-start(bf16[16,128,256]{2,1,0:T(8,128)(2,1)} %get-tuple-element.85), calls=%async_computation | async-start | bytes 2097152 | tf_op jit(solution)/shard_map/all_to_all | solution.py:521
  38.5 5.5 %shard_map.84.q_ref = bf16[128,640]{1,0:T(8,128)(2,1)S(1)} custom-call(bf16[128,5120]{1,0:T(8,128)(2,1)} %get-tuple-element.83.refs_0_, bf16[5120,640]{1,0:T(8,128)(2,1)} %refs_4_.1), custom_call_target="tpu_custom_call" | custom-call | flops 838860800 | bytes 8000000 | tf_op jit(solution)/shard_map/pallas_call | solution.py:207
  45.5 6.0 %shard_map.85 = (f32[64,5120]{1,0:T(8,128)S(1)}, bf16[64,5120]{1,0:T(8,128)(2,1)S(1)}) custom-call(bf16[128,640]{1,0:T(8,128)(2,1)S(1)} %shard_map.84.q_ref, f32[128,128]{1,0:T(8,128)S(1)} %get-tuple-element.84.scale_ref, bf16[16,128,256]{2,1,0:T(8,128)(2,1)S(1)} %all-to-all-done.kv_ref, bf16[640,5120]{1,0:T(8,128)(2,1)} %w_ref.7), custom_call_target="tpu_custom_call" | custom-call | flops 1509949440 | bytes 9000000 | tf_op jit(solution)/shard_map/pallas_call | solution.py:43
  51.4 3.2 %collective-permute-start.8 = (bf16[64,5120]{1,0:T(8,128)(2,1)S(1)}, bf16[64,5120]{1,0:T(8,128)(2,1)S(1)}, u32[]{:S(2)}, u32[]{:S(2)}) collective-permute-start(bf16[64,5120]{1,0:T(8,128)(2,1)S(1)} %get-tuple-element.93), channel_id=1, source_target_pairs={{0,1},{1,0},{2,3},{3,2},{4,5},{5,4},{6,7},{7,6},{8,9},{9,8},{10,11... | collective-permute-start | bytes 1966088 | tf_op jit(solution)/shard_map/ppermute | solution.py:549
  58.2 3.8 %collective-permute-done.9.a_ref = bf16[16,5120]{1,0:T(8,128)(2,1)S(1)} collective-permute-done((bf16[16,5120]{1,0:T(8,128)(2,1)S(1)}, bf16[16,5120]{1,0:T(8,128)(2,1)S(1)}, u32[]{:S(2)}, u32[]{:S(2)}) %collective-permute-start.9) | collective-permute-done | bytes 163872 | tf_op jit(solution)/shard_map/ppermute | solution.py:553
  63.6 4.5 %collective-permute-done.11.d_ref = bf16[16,5120]{1,0:T(8,128)(2,1)S(1)} collective-permute-done((bf16[16,5120]{1,0:T(8,128)(2,1)S(1)}, bf16[16,5120]{1,0:T(8,128)(2,1)S(1)}, u32[]{:S(2)}, u32[]{:S(2)}) %collective-permute-start.11) | collective-permute-done | bytes 163872 | tf_op jit(solution)/shard_map/ppermute | solution.py:553
  72.3 7.4 %collective-permute-done.12 = bf16[16,5120]{1,0:T(8,128)(2,1)S(1)} collective-permute-done((bf16[16,5120]{1,0:T(8,128)(2,1)S(1)}, bf16[16,5120]{1,0:T(8,128)(2,1)S(1)}, u32[]{:S(2)}, u32[]{:S(2)}) %collective-permute-start.12) | collective-permute-done | bytes 163872 | tf_op jit(solution)/shard_map/ppermute | solution.py:466
  83.3 3.4 %shard_map.88 = (bf16[128,5120]{1,0:T(8,128)(2,1)}, f32[128,384]{1,0:T(8,128)S(1)}, f32[128,128]{1,0:T(8,128)S(1)}, bf16[16,128,256]{2,1,0:T(8,128)(2,1)}) custom-call(bf16[5120,128]{1,0:T(8,128)(2,1)} %refs_0_.5, bf16[5120,128]{1,0:T(8,128)(2,1)} %refs_1_.9, f32[1,5120]{1,0:T(1,128)S(1)} %bitcast.12, ...), custom_call_target="tpu_custom_call" | custom-call | flops 335544320 | bytes 4000000 | tf_op jit(solution)/shard_map/pallas_call | solution.py:43
  86.8 3.7 %all-to-all-start.1 = ((bf16[16,128,256]{2,1,0:T(8,128)(2,1)}), bf16[16,128,256]{2,1,0:T(8,128)(2,1)S(1)}, u32[]{:S(2)}, u32[]{:S(2)}) async-start(bf16[16,128,256]{2,1,0:T(8,128)(2,1)} %get-tuple-element.104), calls=%async_computation.1 | async-start | bytes 2097152 | tf_op jit(solution)/shard_map/all_to_all | solution.py:521
  90.5 5.5 %shard_map.89.q_ref = bf16[128,640]{1,0:T(8,128)(2,1)S(1)} custom-call(bf16[128,5120]{1,0:T(8,128)(2,1)} %get-tuple-element.102.refs_0_.refs_3_.refs_1_, bf16[5120,640]{1,0:T(8,128)(2,1)} %refs_4_.1), custom_call_target="tpu_custom_call" | custom-call | flops 838860800 | bytes 8000000 | tf_op jit(solution)/shard_map/pallas_call | solution.py:207
  96.0 10.6 %all-to-all-done.1.kv_ref = bf16[16,128,256]{2,1,0:T(8,128)(2,1)S(1)} async-done(((bf16[16,128,256]{2,1,0:T(8,128)(2,1)}), bf16[16,128,256]{2,1,0:T(8,128)(2,1)S(1)}, u32[]{:S(2)}, u32[]{:S(2)}) %all-to-all-start.1) | async-done | bytes 1048608 | tf_op jit(solution)/shard_map/all_to_all | solution.py:521
  106.6 6.0 %shard_map.90 = (f32[64,5120]{1,0:T(8,128)S(1)}, bf16[64,5120]{1,0:T(8,128)(2,1)S(1)}) custom-call(bf16[128,640]{1,0:T(8,128)(2,1)S(1)} %shard_map.89.q_ref, f32[128,128]{1,0:T(8,128)S(1)} %get-tuple-element.103.scale_ref, bf16[16,128,256]{2,1,0:T(8,128)(2,1)S(1)} %all-to-all-done.1.kv_ref, bf16[640,5120]{1,0:T(8,128)(2,1)} %w_ref.7), custom_call_target="tpu_custom_call" | custom-call | flops 1509949440 | bytes 9000000 | tf_op jit(solution)/shard_map/pallas_call | solution.py:43
  112.6 2.6 collective-permute-start.16
  117.1 2.4 collective-permute-start.17
  120.2 2.9 collective-permute-done.17.a_ref
  123.1 3.1 collective-permute-done.18.b_ref
  126.2 3.9 %collective-permute-done.19.d_ref = bf16[16,5120]{1,0:T(8,128)(2,1)S(1)} collective-permute-done((bf16[16,5120]{1,0:T(8,128)(2,1)S(1)}, bf16[16,5120]{1,0:T(8,128)(2,1)S(1)}, u32[]{:S(2)}, u32[]{:S(2)}) %collective-permute-start.19) | collective-permute-done | bytes 163872 | tf_op jit(solution)/shard_map/ppermute | solution.py:553
  134.5 7.3 %collective-permute-done.20 = bf16[16,5120]{1,0:T(8,128)(2,1)S(1)} collective-permute-done((bf16[16,5120]{1,0:T(8,128)(2,1)S(1)}, bf16[16,5120]{1,0:T(8,128)(2,1)S(1)}, u32[]{:S(2)}, u32[]{:S(2)}) %collective-permute-start.20) | collective-permute-done | bytes 163872 | tf_op jit(solution)/shard_map/ppermute | solution.py:466
  143.8 5.0 %all-to-all-start.2 = ((f32[128,1,128]{2,1,0:T(1,128)}), f32[128,1,128]{2,1,0:T(1,128)S(1)}, u32[]{:S(2)}, u32[]{:S(2)}) async-start(f32[128,1,128]{2,1,0:T(1,128)} %get-tuple-element.114), calls=%async_computation.2 | async-start | bytes 131072 | tf_op jit(solution)/shard_map/all_to_all | solution.py:468
  148.8 3.6 %shard_map.92 = (bf16[128,5120]{1,0:T(8,128)(2,1)}, f32[128,384]{1,0:T(8,128)S(1)}) custom-call(bf16[5120,128]{1,0:T(8,128)(2,1)} %refs_0_.5, bf16[5120,128]{1,0:T(8,128)(2,1)} %refs_1_.9, f32[1,5120]{1,0:T(1,128)S(1)} %bitcast.14, bf16[128,5120]{1,0:T(8,128)(2,1)} %get-tuple-element.102.refs_0_.refs_3_.refs_1_, ...), custom_call_target="tpu_custom_call" | custom-call | flops 335544320 | bytes 4000000 | tf_op jit(solution)/shard_map/pallas_call | solution.py:43
  152.4 5.9 %all-to-all-done.2.refs_0_ = f32[128,1,128]{2,1,0:T(1,128)S(1)} async-done(((f32[128,1,128]{2,1,0:T(1,128)}), f32[128,1,128]{2,1,0:T(1,128)S(1)}, u32[]{:S(2)}, u32[]{:S(2)}) %all-to-all-start.2) | async-done | bytes 65568 | tf_op jit(solution)/shard_map/all_to_all | solution.py:468
  159.8 3.8 %all-to-all-start.3 = ((bf16[16,128,256]{2,1,0:T(8,128)(2,1)}), bf16[16,128,256]{2,1,0:T(8,128)(2,1)S(1)}, u32[]{:S(2)}, u32[]{:S(2)}) async-start(bf16[16,128,256]{2,1,0:T(8,128)(2,1)} %get-tuple-element.121), calls=%async_computation.3 | async-start | bytes 2097152 | tf_op jit(solution)/shard_map/all_to_all | solution.py:521
  165.8 2.7 collective-permute-done.26.refs_6_
  168.5 2.6 collective-permute-done.25.refs_5_
  171.2 4.7 %collective-permute-done.24.refs_4_ = f32[2,2,16,640]{3,2,1,0:T(8,128)S(1)} collective-permute-done((f32[2,2,16,640]{3,2,1,0:T(8,128)S(1)}, f32[2,2,16,640]{3,2,1,0:T(8,128)S(1)}, u32[]{:S(2)}, u32[]{:S(2)}) %collective-permute-start.24) | collective-permute-done | bytes 163872 | tf_op jit(solution)/shard_map/ppermute | solution.py:428
  176.5 5.9 %shard_map.94.q_ref = bf16[128,640]{1,0:T(8,128)(2,1)S(1)} custom-call(f32[1,128]{1,0:T(1,128)S(1)} %get-tuple-element.118.refs_0_.share_ref, bf16[128,5120]{1,0:T(8,128)(2,1)} %get-tuple-element.102.refs_0_.refs_3_.refs_1_, bf16[128,5120]{1,0:T(8,128)(2,1)} %get-tuple-element.119.refs_2_.refs_4_, bf16[5120,640]{1,0:T(8,128)(2,1)} %refs_4_.1), custom_call_target="tpu_custom_call" | custom-call | flops 838860800 | bytes 8000000 | tf_op jit(solution)/shard_map/pallas_call | solution.py:207
  182.5 5.9 %shard_map.95 = (f32[64,5120]{1,0:T(8,128)S(1)}, bf16[64,5120]{1,0:T(8,128)(2,1)S(1)}) custom-call(bf16[128,640]{1,0:T(8,128)(2,1)S(1)} %shard_map.94.q_ref, f32[128,128]{1,0:T(8,128)S(1)} %get-tuple-element.120.scale_ref, bf16[16,128,256]{2,1,0:T(8,128)(2,1)S(1)} %all-to-all-done.3.kv_ref, bf16[640,5120]{1,0:T(8,128)(2,1)} %w_ref.7), custom_call_target="tpu_custom_call" | custom-call | flops 1509949440 | bytes 9000000 | tf_op jit(solution)/shard_map/pallas_call | solution.py:43
  193.1 3.3 %collective-permute-done.29.a_ref = bf16[16,5120]{1,0:T(8,128)(2,1)S(1)} collective-permute-done((bf16[16,5120]{1,0:T(8,128)(2,1)S(1)}, bf16[16,5120]{1,0:T(8,128)(2,1)S(1)}, u32[]{:S(2)}, u32[]{:S(2)}) %collective-permute-start.29) | collective-permute-done | bytes 163872 | tf_op jit(solution)/shard_map/ppermute | solution.py:553
  198.0 4.5 %collective-permute-done.31.d_ref = bf16[16,5120]{1,0:T(8,128)(2,1)S(1)} collective-permute-done((bf16[16,5120]{1,0:T(8,128)(2,1)S(1)}, bf16[16,5120]{1,0:T(8,128)(2,1)S(1)}, u32[]{:S(2)}, u32[]{:S(2)}) %collective-permute-start.31) | collective-permute-done | bytes 163872 | tf_op jit(solution)/shard_map/ppermute | solution.py:553
  207.3 7.0 %collective-permute-done.32 = bf16[16,5120]{1,0:T(8,128)(2,1)S(1)} collective-permute-done((bf16[16,5120]{1,0:T(8,128)(2,1)S(1)}, bf16[16,5120]{1,0:T(8,128)(2,1)S(1)}, u32[]{:S(2)}, u32[]{:S(2)}) %collective-permute-start.32) | collective-permute-done | bytes 163872 | tf_op jit(solution)/shard_map/ppermute | solution.py:466
  216.2 8.5 %all-to-all-start.4 = ((f32[128,1,128]{2,1,0:T(1,128)}), f32[128,1,128]{2,1,0:T(1,128)S(1)}, u32[]{:S(2)}, u32[]{:S(2)}) async-start(f32[128,1,128]{2,1,0:T(1,128)} %get-tuple-element.132), calls=%async_computation.4 | async-start | bytes 131072 | tf_op jit(solution)/shard_map/all_to_all | solution.py:468
  224.7 5.7 %shard_map.98 = (bf16[128,5120]{1,0:T(8,128)(2,1)}, f32[128,384]{1,0:T(8,128)S(1)}) custom-call(bf16[5120,128]{1,0:T(8,128)(2,1)} %refs_0_.5, bf16[5120,128]{1,0:T(8,128)(2,1)} %refs_1_.9, f32[1,5120]{1,0:T(1,128)S(1)} %bitcast.16, bf16[128,5120]{1,0:T(8,128)(2,1)} %get-tuple-element.102.refs_0_.refs_3_.refs_1_, ...), custom_call_target="tpu_custom_call" | custom-call | flops 335544320 | bytes 4000000 | tf_op jit(solution)/shard_map/pallas_call | solution.py:43
  230.4 3.8 %all-to-all-done.4.refs_1_ = f32[128,1,128]{2,1,0:T(1,128)S(1)} async-done(((f32[128,1,128]{2,1,0:T(1,128)}), f32[128,1,128]{2,1,0:T(1,128)S(1)}, u32[]{:S(2)}, u32[]{:S(2)}) %all-to-all-start.4) | async-done | bytes 65568 | tf_op jit(solution)/shard_map/all_to_all | solution.py:468
  235.8 3.7 %all-to-all-start.5 = ((bf16[16,128,256]{2,1,0:T(8,128)(2,1)}), bf16[16,128,256]{2,1,0:T(8,128)(2,1)S(1)}, u32[]{:S(2)}, u32[]{:S(2)}) async-start(bf16[16,128,256]{2,1,0:T(8,128)(2,1)} %get-tuple-element.138), calls=%async_computation.5 | async-start | bytes 2097152 | tf_op jit(solution)/shard_map/all_to_all | solution.py:521
  239.4 6.2 %shard_map.100.q_ref = bf16[128,640]{1,0:T(8,128)(2,1)S(1)} custom-call(f32[1,128]{1,0:T(1,128)S(1)} %get-tuple-element.135.refs_0_.share_ref, bf16[128,5120]{1,0:T(8,128)(2,1)} %get-tuple-element.102.refs_0_.refs_3_.refs_1_, bf16[128,5120]{1,0:T(8,128)(2,1)} %get-tuple-element.119.refs_2_.refs_4_, bf16[128,5120]{1,0:T(8,128)(2,1)} %get-tuple-element.136.refs_3_, ...), custom_call_target="tpu_custom_call" | custom-call | flops 838860800 | bytes 8000000 | tf_op jit(solution)/shard_map/pallas_call | solution.py:207
  245.7 9.4 %all-to-all-done.5.kv_ref = bf16[16,128,256]{2,1,0:T(8,128)(2,1)S(1)} async-done(((bf16[16,128,256]{2,1,0:T(8,128)(2,1)}), bf16[16,128,256]{2,1,0:T(8,128)(2,1)S(1)}, u32[]{:S(2)}, u32[]{:S(2)}) %all-to-all-start.5) | async-done | bytes 1048608 | tf_op jit(solution)/shard_map/all_to_all | solution.py:521
  255.1 5.9 %shard_map.101 = (f32[64,5120]{1,0:T(8,128)S(1)}, bf16[64,5120]{1,0:T(8,128)(2,1)S(1)}) custom-call(bf16[128,640]{1,0:T(8,128)(2,1)S(1)} %shard_map.100.q_ref, f32[128,128]{1,0:T(8,128)S(1)} %get-tuple-element.137.scale_ref, bf16[16,128,256]{2,1,0:T(8,128)(2,1)S(1)} %all-to-all-done.5.kv_ref, bf16[640,5120]{1,0:T(8,128)(2,1)} %w_ref.7), custom_call_target="tpu_custom_call" | custom-call | flops 1509949440 | bytes 9000000 | tf_op jit(solution)/shard_map/pallas_call | solution.py:43
  261.0 3.1 %collective-permute-start.36 = (bf16[64,5120]{1,0:T(8,128)(2,1)S(1)}, bf16[64,5120]{1,0:T(8,128)(2,1)S(1)}, u32[]{:S(2)}, u32[]{:S(2)}) collective-permute-start(bf16[64,5120]{1,0:T(8,128)(2,1)S(1)} %get-tuple-element.140), channel_id=1, source_target_pairs={{0,1},{1,0},{2,3},{3,2},{4,5},{5,4},{6,7},{7,6},{8,9},{9,8},{10,11... | collective-permute-start | bytes 1966088 | tf_op jit(solution)/shard_map/ppermute | solution.py:549
  269.7 2.5 collective-permute-done.37.a_ref
  272.2 2.9 collective-permute-done.38.b_ref
  275.1 4.5 %collective-permute-done.39.d_ref = bf16[16,5120]{1,0:T(8,128)(2,1)S(1)} collective-permute-done((bf16[16,5120]{1,0:T(8,128)(2,1)S(1)}, bf16[16,5120]{1,0:T(8,128)(2,1)S(1)}, u32[]{:S(2)}, u32[]{:S(2)}) %collective-permute-start.39) | collective-permute-done | bytes 163872 | tf_op jit(solution)/shard_map/ppermute | solution.py:553
  282.6 4.0 %collective-permute-done.42.refs_11_ = f32[2,2,16,640]{3,2,1,0:T(8,128)S(1)} collective-permute-done((f32[2,2,16,640]{3,2,1,0:T(8,128)}, f32[2,2,16,640]{3,2,1,0:T(8,128)S(1)}, u32[]{:S(2)}, u32[]{:S(2)}) %collective-permute-start.42) | collective-permute-done | bytes 163872 | tf_op jit(solution)/shard_map/ppermute | solution.py:428
  287.7 4.9 %collective-permute-done.40.refs_9_ = f32[2,2,16,640]{3,2,1,0:T(8,128)S(1)} collective-permute-done((f32[2,2,16,640]{3,2,1,0:T(8,128)}, f32[2,2,16,640]{3,2,1,0:T(8,128)S(1)}, u32[]{:S(2)}, u32[]{:S(2)}) %collective-permute-start.40) | collective-permute-done | bytes 163872 | tf_op jit(solution)/shard_map/ppermute | solution.py:428
  294.0 13.3 %all_to_all.35.refs_2_ = f32[128,1,128]{2,1,0:T(1,128)S(1)} all-to-all(f32[128,1,128]{2,1,0:T(1,128)} %get-tuple-element.148), channel_id=1, replica_groups=mesh['x'=4,'z'=4,'y'=4,'c'=2] {'x','z','y','c'}, dimensions={0} | all-to-all | bytes 131072 | tf_op jit(solution)/shard_map/all_to_all | solution.py:589
  (149 shorter events, 67.6 us)
Async XLA Ops:
  1.1 10.1 %collective-permute-start.2 = (bf16[128,640]{1,0:T(8,128)(2,1)S(1)}, bf16[128,640]{1,0:T(8,128)(2,1)S(1)}, u32[]{:S(2)}, u32[]{:S(2)}) collective-permute-start(bf16[128,640]{1,0:T(8,128)(2,1)S(1)} %get-tuple-element.82), channel_id=1, source_target_pairs={{0,6},{2,0},{4,2},{6,4},{1,7},{3,1},{5,3},{7,5},{8,14},{10,8},{12,... | collective-permute-start | bytes 491528 | tf_op jit(solution)/shard_map/ppermute | solution.py:466
  4.7 6.4 %collective-permute-start.1 = (bf16[128,640]{1,0:T(8,128)(2,1)S(1)}, bf16[128,640]{1,0:T(8,128)(2,1)S(1)}, u32[]{:S(2)}, u32[]{:S(2)}) collective-permute-start(bf16[128,640]{1,0:T(8,128)(2,1)S(1)} %get-tuple-element.82), channel_id=1, source_target_pairs={{0,4},{2,6},{4,0},{6,2},{1,5},{3,7},{5,1},{7,3},{8,12},{10,14},{12... | collective-permute-start | bytes 491528 | tf_op jit(solution)/shard_map/ppermute | solution.py:466
  5.1 10.8 %collective-permute-start = (bf16[128,640]{1,0:T(8,128)(2,1)S(1)}, bf16[128,640]{1,0:T(8,128)(2,1)S(1)}, u32[]{:S(2)}, u32[]{:S(2)}) collective-permute-start(bf16[128,640]{1,0:T(8,128)(2,1)S(1)} %get-tuple-element.82), channel_id=1, source_target_pairs={{0,2},{2,4},{4,6},{6,0},{1,3},{3,5},{5,7},{7,1},{8,10},{10,12},{12... | collective-permute-start | bytes 491528 | tf_op jit(solution)/shard_map/ppermute | solution.py:466
  22.2 23.3 %all-to-all-start = ((bf16[16,128,256]{2,1,0:T(8,128)(2,1)}), bf16[16,128,256]{2,1,0:T(8,128)(2,1)S(1)}, u32[]{:S(2)}, u32[]{:S(2)}) async-start(bf16[16,128,256]{2,1,0:T(8,128)(2,1)} %get-tuple-element.85), calls=%async_computation | async-start | bytes 2097152 | tf_op jit(solution)/shard_map/all_to_all | solution.py:521
  29.8 3.4 %collective-permute-start.6 = (bf16[2,2,16,640]{3,2,1,0:T(8,128)(2,1)S(1)}, bf16[2,2,16,640]{3,2,1,0:T(8,128)(2,1)S(1)}, u32[]{:S(2)}, u32[]{:S(2)}) collective-permute-start(bf16[2,2,16,640]{3,2,1,0:T(8,128)(2,1)S(1)} %get-tuple-element.89), channel_id=1, source_target_pairs={{0,6},{2,0},{4,2},{6,4},{1,7},{3,1},{5,3},{7,5},{8,14},{10,8},{12,... | collective-permute-start | bytes 245768 | tf_op jit(solution)/shard_map/ppermute | solution.py:428
  30.2 5.1 %collective-permute-start.5 = (bf16[2,2,16,640]{3,2,1,0:T(8,128)(2,1)S(1)}, bf16[2,2,16,640]{3,2,1,0:T(8,128)(2,1)S(1)}, u32[]{:S(2)}, u32[]{:S(2)}) collective-permute-start(bf16[2,2,16,640]{3,2,1,0:T(8,128)(2,1)S(1)} %get-tuple-element.88), channel_id=1, source_target_pairs={{0,4},{2,6},{4,0},{6,2},{1,5},{3,7},{5,1},{7,3},{8,12},{10,14},{12... | collective-permute-start | bytes 245768 | tf_op jit(solution)/shard_map/ppermute | solution.py:428
  30.5 6.8 %collective-permute-start.4 = (bf16[2,2,16,640]{3,2,1,0:T(8,128)(2,1)S(1)}, bf16[2,2,16,640]{3,2,1,0:T(8,128)(2,1)S(1)}, u32[]{:S(2)}, u32[]{:S(2)}) collective-permute-start(bf16[2,2,16,640]{3,2,1,0:T(8,128)(2,1)S(1)} %get-tuple-element.87), channel_id=1, source_target_pairs={{0,2},{2,4},{4,6},{6,0},{1,3},{3,5},{5,7},{7,1},{8,10},{10,12},{12... | collective-permute-start | bytes 245768 | tf_op jit(solution)/shard_map/ppermute | solution.py:428
  37.3 6.6 %collective-permute-start.7 = (bf16[4,2,16,640]{3,2,1,0:T(8,128)(2,1)S(1)}, bf16[4,2,16,640]{3,2,1,0:T(8,128)(2,1)S(1)}, u32[]{:S(2)}, u32[]{:S(2)}) collective-permute-start(bf16[4,2,16,640]{3,2,1,0:T(8,128)(2,1)S(1)} %pad_maximum_fusion.3), channel_id=1, source_target_pairs={{0,1},{1,0},{2,3},{3,2},{4,5},{5,4},{6,7},{7,6},{8,9},{9,8},{10,11... | collective-permute-start | bytes 491528 | tf_op jit(solution)/shard_map/ppermute | solution.py:430
  51.4 4.9 %collective-permute-start.8 = (bf16[64,5120]{1,0:T(8,128)(2,1)S(1)}, bf16[64,5120]{1,0:T(8,128)(2,1)S(1)}, u32[]{:S(2)}, u32[]{:S(2)}) collective-permute-start(bf16[64,5120]{1,0:T(8,128)(2,1)S(1)} %get-tuple-element.93), channel_id=1, source_target_pairs={{0,1},{1,0},{2,3},{3,2},{4,5},{5,4},{6,7},{7,6},{8,9},{9,8},{10,11... | collective-permute-start | bytes 1966088 | tf_op jit(solution)/shard_map/ppermute | solution.py:549
  56.6 5.5 %collective-permute-start.9 = (bf16[16,5120]{1,0:T(8,128)(2,1)S(1)}, bf16[16,5120]{1,0:T(8,128)(2,1)S(1)}, u32[]{:S(2)}, u32[]{:S(2)}) collective-permute-start(bf16[16,5120]{1,0:T(8,128)(2,1)S(1)} %get-tuple-element.178), channel_id=1, source_target_pairs={{0,6},{2,0},{4,2},{6,4},{1,7},{3,1},{5,3},{7,5},{8,14},{10,8},{12,... | collective-permute-start | bytes 491528 | tf_op jit(solution)/shard_map/ppermute | solution.py:553
  57.0 6.6 %collective-permute-start.10 = (bf16[16,5120]{1,0:T(8,128)(2,1)S(1)}, bf16[16,5120]{1,0:T(8,128)(2,1)S(1)}, u32[]{:S(2)}, u32[]{:S(2)}) collective-permute-start(bf16[16,5120]{1,0:T(8,128)(2,1)S(1)} %get-tuple-element.177), channel_id=1, source_target_pairs={{0,4},{2,6},{4,0},{6,2},{1,5},{3,7},{5,1},{7,3},{8,12},{10,14},{12... | collective-permute-start | bytes 491528 | tf_op jit(solution)/shard_map/ppermute | solution.py:553
  57.3 10.8 %collective-permute-start.11 = (bf16[16,5120]{1,0:T(8,128)(2,1)S(1)}, bf16[16,5120]{1,0:T(8,128)(2,1)S(1)}, u32[]{:S(2)}, u32[]{:S(2)}) collective-permute-start(bf16[16,5120]{1,0:T(8,128)(2,1)S(1)} %get-tuple-element.176), channel_id=1, source_target_pairs={{0,2},{2,4},{4,6},{6,0},{1,3},{3,5},{5,7},{7,1},{8,10},{10,12},{12... | collective-permute-start | bytes 491528 | tf_op jit(solution)/shard_map/ppermute | solution.py:553
  69.4 10.3 %collective-permute-start.12 = (bf16[16,5120]{1,0:T(8,128)(2,1)S(1)}, bf16[16,5120]{1,0:T(8,128)(2,1)S(1)}, u32[]{:S(2)}, u32[]{:S(2)}) collective-permute-start(bf16[16,5120]{1,0:T(8,128)(2,1)S(1)} %get-tuple-element.101), channel_id=1, source_target_pairs={{0,2},{2,4},{4,6},{6,0},{1,3},{3,5},{5,7},{7,1},{8,10},{10,12},{12... | collective-permute-start | bytes 491528 | tf_op jit(solution)/shard_map/ppermute | solution.py:466
  69.5 10.2 %collective-permute-start.13 = (bf16[16,5120]{1,0:T(8,128)(2,1)S(1)}, bf16[16,5120]{1,0:T(8,128)(2,1)S(1)}, u32[]{:S(2)}, u32[]{:S(2)}) collective-permute-start(bf16[16,5120]{1,0:T(8,128)(2,1)S(1)} %get-tuple-element.101), channel_id=1, source_target_pairs={{0,4},{2,6},{4,0},{6,2},{1,5},{3,7},{5,1},{7,3},{8,12},{10,14},{12... | collective-permute-start | bytes 491528 | tf_op jit(solution)/shard_map/ppermute | solution.py:466
  70.6 9.4 %collective-permute-start.14 = (bf16[16,5120]{1,0:T(8,128)(2,1)S(1)}, bf16[16,5120]{1,0:T(8,128)(2,1)S(1)}, u32[]{:S(2)}, u32[]{:S(2)}) collective-permute-start(bf16[16,5120]{1,0:T(8,128)(2,1)S(1)} %get-tuple-element.101), channel_id=1, source_target_pairs={{0,6},{2,0},{4,2},{6,4},{1,7},{3,1},{5,3},{7,5},{8,14},{10,8},{12,... | collective-permute-start | bytes 491528 | tf_op jit(solution)/shard_map/ppermute | solution.py:466
  80.0 3.4 %collective-permute-start.15 = (bf16[64,5120]{1,0:T(8,128)(2,1)S(1)}, bf16[64,5120]{1,0:T(8,128)(2,1)S(1)}, u32[]{:S(2)}, u32[]{:S(2)}) collective-permute-start(bf16[64,5120]{1,0:T(8,128)(2,1)S(1)} %constant_dynamic-update-slice_fusion.refs_3_), channel_id=1, source_target_pairs={{0,1},{1,0},{2,3},{3,2},{4,5},{5,4},{6,7},{7,6},{8,9},{9,8},{10,11... | collective-permute-start | bytes 1966088 | tf_op jit(solution)/shard_map/ppermute | solution.py:470
  86.8 19.8 %all-to-all-start.1 = ((bf16[16,128,256]{2,1,0:T(8,128)(2,1)}), bf16[16,128,256]{2,1,0:T(8,128)(2,1)S(1)}, u32[]{:S(2)}, u32[]{:S(2)}) async-start(bf16[16,128,256]{2,1,0:T(8,128)(2,1)} %get-tuple-element.104), calls=%async_computation.1 | async-start | bytes 2097152 | tf_op jit(solution)/shard_map/all_to_all | solution.py:521
  112.6 4.3 %collective-permute-start.16 = (bf16[64,5120]{1,0:T(8,128)(2,1)S(1)}, bf16[64,5120]{1,0:T(8,128)(2,1)S(1)}, u32[]{:S(2)}, u32[]{:S(2)}) collective-permute-start(bf16[64,5120]{1,0:T(8,128)(2,1)S(1)} %get-tuple-element.106), channel_id=1, source_target_pairs={{0,1},{1,0},{2,3},{3,2},{4,5},{5,4},{6,7},{7,6},{8,9},{9,8},{10,11... | collective-permute-start | bytes 1966088 | tf_op jit(solution)/shard_map/ppermute | solution.py:549
  117.1 6.0 %collective-permute-start.17 = (bf16[16,5120]{1,0:T(8,128)(2,1)S(1)}, bf16[16,5120]{1,0:T(8,128)(2,1)S(1)}, u32[]{:S(2)}, u32[]{:S(2)}) collective-permute-start(bf16[16,5120]{1,0:T(8,128)(2,1)S(1)} %get-tuple-element.175), channel_id=1, source_target_pairs={{0,6},{2,0},{4,2},{6,4},{1,7},{3,1},{5,3},{7,5},{8,14},{10,8},{12,... | collective-permute-start | bytes 491528 | tf_op jit(solution)/shard_map/ppermute | solution.py:553
  119.5 6.7 %collective-permute-start.18 = (bf16[16,5120]{1,0:T(8,128)(2,1)S(1)}, bf16[16,5120]{1,0:T(8,128)(2,1)S(1)}, u32[]{:S(2)}, u32[]{:S(2)}) collective-permute-start(bf16[16,5120]{1,0:T(8,128)(2,1)S(1)} %get-tuple-element.174), channel_id=1, source_target_pairs={{0,4},{2,6},{4,0},{6,2},{1,5},{3,7},{5,1},{7,3},{8,12},{10,14},{12... | collective-permute-start | bytes 491528 | tf_op jit(solution)/shard_map/ppermute | solution.py:553
  119.5 10.6 %collective-permute-start.19 = (bf16[16,5120]{1,0:T(8,128)(2,1)S(1)}, bf16[16,5120]{1,0:T(8,128)(2,1)S(1)}, u32[]{:S(2)}, u32[]{:S(2)}) collective-permute-start(bf16[16,5120]{1,0:T(8,128)(2,1)S(1)} %get-tuple-element.173), channel_id=1, source_target_pairs={{0,2},{2,4},{4,6},{6,0},{1,3},{3,5},{5,7},{7,1},{8,10},{10,12},{12... | collective-permute-start | bytes 491528 | tf_op jit(solution)/shard_map/ppermute | solution.py:553
  131.6 10.2 %collective-permute-start.20 = (bf16[16,5120]{1,0:T(8,128)(2,1)S(1)}, bf16[16,5120]{1,0:T(8,128)(2,1)S(1)}, u32[]{:S(2)}, u32[]{:S(2)}) collective-permute-start(bf16[16,5120]{1,0:T(8,128)(2,1)S(1)} %get-tuple-element.116), channel_id=1, source_target_pairs={{0,2},{2,4},{4,6},{6,0},{1,3},{3,5},{5,7},{7,1},{8,10},{10,12},{12... | collective-permute-start | bytes 491528 | tf_op jit(solution)/shard_map/ppermute | solution.py:466
  131.7 10.1 %collective-permute-start.21 = (bf16[16,5120]{1,0:T(8,128)(2,1)S(1)}, bf16[16,5120]{1,0:T(8,128)(2,1)S(1)}, u32[]{:S(2)}, u32[]{:S(2)}) collective-permute-start(bf16[16,5120]{1,0:T(8,128)(2,1)S(1)} %get-tuple-element.116), channel_id=1, source_target_pairs={{0,4},{2,6},{4,0},{6,2},{1,5},{3,7},{5,1},{7,3},{8,12},{10,14},{12... | collective-permute-start | bytes 491528 | tf_op jit(solution)/shard_map/ppermute | solution.py:466
  132.8 9.0 %collective-permute-start.22 = (bf16[16,5120]{1,0:T(8,128)(2,1)S(1)}, bf16[16,5120]{1,0:T(8,128)(2,1)S(1)}, u32[]{:S(2)}, u32[]{:S(2)}) collective-permute-start(bf16[16,5120]{1,0:T(8,128)(2,1)S(1)} %get-tuple-element.116), channel_id=1, source_target_pairs={{0,6},{2,0},{4,2},{6,4},{1,7},{3,1},{5,3},{7,5},{8,14},{10,8},{12,... | collective-permute-start | bytes 491528 | tf_op jit(solution)/shard_map/ppermute | solution.py:466
  141.8 7.0 %collective-permute-start.23 = (bf16[64,5120]{1,0:T(8,128)(2,1)S(1)}, bf16[64,5120]{1,0:T(8,128)(2,1)S(1)}, u32[]{:S(2)}, u32[]{:S(2)}) collective-permute-start(bf16[64,5120]{1,0:T(8,128)(2,1)S(1)} %constant_dynamic-update-slice_fusion.4.refs_4_), channel_id=1, source_target_pairs={{0,1},{1,0},{2,3},{3,2},{4,5},{5,4},{6,7},{7,6},{8,9},{9,8},{10,11... | collective-permute-start | bytes 1966088 | tf_op jit(solution)/shard_map/ppermute | solution.py:470
  143.8 14.5 %all-to-all-start.2 = ((f32[128,1,128]{2,1,0:T(1,128)}), f32[128,1,128]{2,1,0:T(1,128)S(1)}, u32[]{:S(2)}, u32[]{:S(2)}) async-start(f32[128,1,128]{2,1,0:T(1,128)} %get-tuple-element.114), calls=%async_computation.2 | async-start | bytes 131072 | tf_op jit(solution)/shard_map/all_to_all | solution.py:468
  159.8 22.7 %all-to-all-start.3 = ((bf16[16,128,256]{2,1,0:T(8,128)(2,1)}), bf16[16,128,256]{2,1,0:T(8,128)(2,1)S(1)}, u32[]{:S(2)}, u32[]{:S(2)}) async-start(bf16[16,128,256]{2,1,0:T(8,128)(2,1)} %get-tuple-element.121), calls=%async_computation.3 | async-start | bytes 2097152 | tf_op jit(solution)/shard_map/all_to_all | solution.py:521
  163.6 4.9 %collective-permute-start.26 = (f32[2,2,16,640]{3,2,1,0:T(8,128)S(1)}, f32[2,2,16,640]{3,2,1,0:T(8,128)S(1)}, u32[]{:S(2)}, u32[]{:S(2)}) collective-permute-start(f32[2,2,16,640]{3,2,1,0:T(8,128)S(1)} %copy-done.17), channel_id=1, source_target_pairs={{0,6},{2,0},{4,2},{6,4},{1,7},{3,1},{5,3},{7,5},{8,14},{10,8},{12,... | collective-permute-start | bytes 491528 | tf_op jit(solution)/shard_map/ppermute | solution.py:428
  164.8 6.4 %collective-permute-start.25 = (f32[2,2,16,640]{3,2,1,0:T(8,128)S(1)}, f32[2,2,16,640]{3,2,1,0:T(8,128)S(1)}, u32[]{:S(2)}, u32[]{:S(2)}) collective-permute-start(f32[2,2,16,640]{3,2,1,0:T(8,128)S(1)} %copy-done.16), channel_id=1, source_target_pairs={{0,4},{2,6},{4,0},{6,2},{1,5},{3,7},{5,1},{7,3},{8,12},{10,14},{12... | collective-permute-start | bytes 491528 | tf_op jit(solution)/shard_map/ppermute | solution.py:428
  165.8 10.0 %collective-permute-start.24 = (f32[2,2,16,640]{3,2,1,0:T(8,128)S(1)}, f32[2,2,16,640]{3,2,1,0:T(8,128)S(1)}, u32[]{:S(2)}, u32[]{:S(2)}) collective-permute-start(f32[2,2,16,640]{3,2,1,0:T(8,128)S(1)} %copy-done.15), channel_id=1, source_target_pairs={{0,2},{2,4},{4,6},{6,0},{1,3},{3,5},{5,7},{7,1},{8,10},{10,12},{12... | collective-permute-start | bytes 491528 | tf_op jit(solution)/shard_map/ppermute | solution.py:428
  175.9 6.6 %collective-permute-start.27 = (f32[4,2,16,640]{3,2,1,0:T(8,128)S(1)}, f32[4,2,16,640]{3,2,1,0:T(8,128)S(1)}, u32[]{:S(2)}, u32[]{:S(2)}) collective-permute-start(f32[4,2,16,640]{3,2,1,0:T(8,128)S(1)} %pad_maximum_fusion.1), channel_id=1, source_target_pairs={{0,1},{1,0},{2,3},{3,2},{4,5},{5,4},{6,7},{7,6},{8,9},{9,8},{10,11... | collective-permute-start | bytes 983048 | tf_op jit(solution)/shard_map/ppermute | solution.py:430
  190.9 5.5 %collective-permute-start.29 = (bf16[16,5120]{1,0:T(8,128)(2,1)S(1)}, bf16[16,5120]{1,0:T(8,128)(2,1)S(1)}, u32[]{:S(2)}, u32[]{:S(2)}) collective-permute-start(bf16[16,5120]{1,0:T(8,128)(2,1)S(1)} %get-tuple-element.172), channel_id=1, source_target_pairs={{0,6},{2,0},{4,2},{6,4},{1,7},{3,1},{5,3},{7,5},{8,14},{10,8},{12,... | collective-permute-start | bytes 491528 | tf_op jit(solution)/shard_map/ppermute | solution.py:553
  191.4 6.6 %collective-permute-start.30 = (bf16[16,5120]{1,0:T(8,128)(2,1)S(1)}, bf16[16,5120]{1,0:T(8,128)(2,1)S(1)}, u32[]{:S(2)}, u32[]{:S(2)}) collective-permute-start(bf16[16,5120]{1,0:T(8,128)(2,1)S(1)} %get-tuple-element.171), channel_id=1, source_target_pairs={{0,4},{2,6},{4,0},{6,2},{1,5},{3,7},{5,1},{7,3},{8,12},{10,14},{12... | collective-permute-start | bytes 491528 | tf_op jit(solution)/shard_map/ppermute | solution.py:553
  192.4 10.1 %collective-permute-start.31 = (bf16[16,5120]{1,0:T(8,128)(2,1)S(1)}, bf16[16,5120]{1,0:T(8,128)(2,1)S(1)}, u32[]{:S(2)}, u32[]{:S(2)}) collective-permute-start(bf16[16,5120]{1,0:T(8,128)(2,1)S(1)} %get-tuple-element.170), channel_id=1, source_target_pairs={{0,2},{2,4},{4,6},{6,0},{1,3},{3,5},{5,7},{7,1},{8,10},{10,12},{12... | collective-permute-start | bytes 491528 | tf_op jit(solution)/shard_map/ppermute | solution.py:553
  204.0 10.3 %collective-permute-start.32 = (bf16[16,5120]{1,0:T(8,128)(2,1)S(1)}, bf16[16,5120]{1,0:T(8,128)(2,1)S(1)}, u32[]{:S(2)}, u32[]{:S(2)}) collective-permute-start(bf16[16,5120]{1,0:T(8,128)(2,1)S(1)} %get-tuple-element.133), channel_id=1, source_target_pairs={{0,2},{2,4},{4,6},{6,0},{1,3},{3,5},{5,7},{7,1},{8,10},{10,12},{12... | collective-permute-start | bytes 491528 | tf_op jit(solution)/shard_map/ppermute | solution.py:466
  204.1 10.2 %collective-permute-start.33 = (bf16[16,5120]{1,0:T(8,128)(2,1)S(1)}, bf16[16,5120]{1,0:T(8,128)(2,1)S(1)}, u32[]{:S(2)}, u32[]{:S(2)}) collective-permute-start(bf16[16,5120]{1,0:T(8,128)(2,1)S(1)} %get-tuple-element.133), channel_id=1, source_target_pairs={{0,4},{2,6},{4,0},{6,2},{1,5},{3,7},{5,1},{7,3},{8,12},{10,14},{12... | collective-permute-start | bytes 491528 | tf_op jit(solution)/shard_map/ppermute | solution.py:466
  205.2 9.3 %collective-permute-start.34 = (bf16[16,5120]{1,0:T(8,128)(2,1)S(1)}, bf16[16,5120]{1,0:T(8,128)(2,1)S(1)}, u32[]{:S(2)}, u32[]{:S(2)}) collective-permute-start(bf16[16,5120]{1,0:T(8,128)(2,1)S(1)} %get-tuple-element.133), channel_id=1, source_target_pairs={{0,6},{2,0},{4,2},{6,4},{1,7},{3,1},{5,3},{7,5},{8,14},{10,8},{12,... | collective-permute-start | bytes 491528 | tf_op jit(solution)/shard_map/ppermute | solution.py:466
  214.6 10.1 %collective-permute-start.35 = (bf16[64,5120]{1,0:T(8,128)(2,1)S(1)}, bf16[64,5120]{1,0:T(8,128)(2,1)}, u32[]{:S(2)}, u32[]{:S(2)}) collective-permute-start(bf16[64,5120]{1,0:T(8,128)(2,1)S(1)} %constant_dynamic-update-slice_fusion.8.refs_5_), channel_id=1, source_target_pairs={{0,1},{1,0},{2,3},{3,2},{4,5},{5,4},{6,7},{7,6},{8,9},{9,8},{10,11... | collective-permute-start | bytes 1966088 | tf_op jit(solution)/shard_map/ppermute | solution.py:470
  216.2 18.0 %all-to-all-start.4 = ((f32[128,1,128]{2,1,0:T(1,128)}), f32[128,1,128]{2,1,0:T(1,128)S(1)}, u32[]{:S(2)}, u32[]{:S(2)}) async-start(f32[128,1,128]{2,1,0:T(1,128)} %get-tuple-element.132), calls=%async_computation.4 | async-start | bytes 131072 | tf_op jit(solution)/shard_map/all_to_all | solution.py:468
  235.8 19.3 %all-to-all-start.5 = ((bf16[16,128,256]{2,1,0:T(8,128)(2,1)}), bf16[16,128,256]{2,1,0:T(8,128)(2,1)S(1)}, u32[]{:S(2)}, u32[]{:S(2)}) async-start(bf16[16,128,256]{2,1,0:T(8,128)(2,1)} %get-tuple-element.138), calls=%async_computation.5 | async-start | bytes 2097152 | tf_op jit(solution)/shard_map/all_to_all | solution.py:521
  261.0 4.8 %collective-permute-start.36 = (bf16[64,5120]{1,0:T(8,128)(2,1)S(1)}, bf16[64,5120]{1,0:T(8,128)(2,1)S(1)}, u32[]{:S(2)}, u32[]{:S(2)}) collective-permute-start(bf16[64,5120]{1,0:T(8,128)(2,1)S(1)} %get-tuple-element.140), channel_id=1, source_target_pairs={{0,1},{1,0},{2,3},{3,2},{4,5},{5,4},{6,7},{7,6},{8,9},{9,8},{10,11... | collective-permute-start | bytes 1966088 | tf_op jit(solution)/shard_map/ppermute | solution.py:549
  266.1 6.1 %collective-permute-start.37 = (bf16[16,5120]{1,0:T(8,128)(2,1)S(1)}, bf16[16,5120]{1,0:T(8,128)(2,1)S(1)}, u32[]{:S(2)}, u32[]{:S(2)}) collective-permute-start(bf16[16,5120]{1,0:T(8,128)(2,1)S(1)} %get-tuple-element.169), channel_id=1, source_target_pairs={{0,6},{2,0},{4,2},{6,4},{1,7},{3,1},{5,3},{7,5},{8,14},{10,8},{12,... | collective-permute-start | bytes 491528 | tf_op jit(solution)/shard_map/ppermute | solution.py:553
  268.4 6.6 %collective-permute-start.38 = (bf16[16,5120]{1,0:T(8,128)(2,1)S(1)}, bf16[16,5120]{1,0:T(8,128)(2,1)S(1)}, u32[]{:S(2)}, u32[]{:S(2)}) collective-permute-start(bf16[16,5120]{1,0:T(8,128)(2,1)S(1)} %get-tuple-element.168), channel_id=1, source_target_pairs={{0,4},{2,6},{4,0},{6,2},{1,5},{3,7},{5,1},{7,3},{8,12},{10,14},{12... | collective-permute-start | bytes 491528 | tf_op jit(solution)/shard_map/ppermute | solution.py:553
  268.9 10.7 %collective-permute-start.39 = (bf16[16,5120]{1,0:T(8,128)(2,1)S(1)}, bf16[16,5120]{1,0:T(8,128)(2,1)S(1)}, u32[]{:S(2)}, u32[]{:S(2)}) collective-permute-start(bf16[16,5120]{1,0:T(8,128)(2,1)S(1)} %get-tuple-element.167), channel_id=1, source_target_pairs={{0,2},{2,4},{4,6},{6,0},{1,3},{3,5},{5,7},{7,1},{8,10},{10,12},{12... | collective-permute-start | bytes 491528 | tf_op jit(solution)/shard_map/ppermute | solution.py:553
  281.0 5.5 %collective-permute-start.42 = (f32[2,2,16,640]{3,2,1,0:T(8,128)}, f32[2,2,16,640]{3,2,1,0:T(8,128)S(1)}, u32[]{:S(2)}, u32[]{:S(2)}) collective-permute-start(f32[2,2,16,640]{3,2,1,0:T(8,128)} %get-tuple-element.157), channel_id=1, source_target_pairs={{0,6},{2,0},{4,2},{6,4},{1,7},{3,1},{5,3},{7,5},{8,14},{10,8},{12,... | collective-permute-start | bytes 491528 | tf_op jit(solution)/shard_map/ppermute | solution.py:428
  281.1 6.5 %collective-permute-start.41 = (f32[2,2,16,640]{3,2,1,0:T(8,128)}, f32[2,2,16,640]{3,2,1,0:T(8,128)S(1)}, u32[]{:S(2)}, u32[]{:S(2)}) collective-permute-start(f32[2,2,16,640]{3,2,1,0:T(8,128)} %get-tuple-element.156), channel_id=1, source_target_pairs={{0,4},{2,6},{4,0},{6,2},{1,5},{3,7},{5,1},{7,3},{8,12},{10,14},{12... | collective-permute-start | bytes 491528 | tf_op jit(solution)/shard_map/ppermute | solution.py:428
  281.6 10.9 %collective-permute-start.40 = (f32[2,2,16,640]{3,2,1,0:T(8,128)}, f32[2,2,16,640]{3,2,1,0:T(8,128)S(1)}, u32[]{:S(2)}, u32[]{:S(2)}) collective-permute-start(f32[2,2,16,640]{3,2,1,0:T(8,128)} %get-tuple-element.155), channel_id=1, source_target_pairs={{0,2},{2,4},{4,6},{6,0},{1,3},{3,5},{5,7},{7,1},{8,10},{10,12},{12... | collective-permute-start | bytes 491528 | tf_op jit(solution)/shard_map/ppermute | solution.py:428
  293.5 13.9 %collective-permute-start.43 = (f32[4,2,16,640]{3,2,1,0:T(8,128)S(1)}, f32[4,2,16,640]{3,2,1,0:T(8,128)S(1)}, u32[]{:S(2)}, u32[]{:S(2)}) collective-permute-start(f32[4,2,16,640]{3,2,1,0:T(8,128)S(1)} %pad_maximum_fusion.2), channel_id=1, source_target_pairs={{0,1},{1,0},{2,3},{3,2},{4,5},{5,4},{6,7},{7,6},{8,9},{9,8},{10,11... | collective-permute-start | bytes 983048 | tf_op jit(solution)/shard_map/ppermute | solution.py:430
  (20 other events, 256.7 us)

commit v3 on v2

--- a/solution.py
+++ b/solution.py
@@ -227,8 +227,8 @@
     load.start()
     s = lax.axis_index("x") * 4 + lax.axis_index("z")
     row_at = s * 128 + row_offset(lax.broadcasted_iota(jnp.int32, (128, 1), 0))
-    column = lax.broadcasted_iota(jnp.int32, (1, TOKENS), 1)
-    allowed = row_at >= (column // 128) * 128 + row_offset(column % 128)
+    column_at = row_offset(lax.broadcasted_iota(jnp.int32, (1, 128), 1))
+    allowed = row_at >= jnp.concatenate([128 * n + column_at for n in range(16)], axis=1)
     factor = scale_ref[:, :1] * (SCORE_SCALE / math.log(2.0))
 
     def one_head(g, carry):
@@ -274,10 +274,6 @@
 
 def finish_kernel(k, own_ref, a_ref, b_ref, d_ref, inj_ref, x_ref, gain_ref, gain_in_ref, *rest):
     older, rest = rest[:k], rest[k:]
-    if k % 2 == 1:
-        rest = rest[5:]
-    image_held, residual_held, dots_held, sem = rest[-4:]
-    image_out, residual_out, *home_out = rest[:7]
     inj, x = inj_ref[...].astype(F32), x_ref[...].astype(F32)
     summed = (x + inj) + (
         own_ref[...] + a_ref[...].astype(F32) + b_ref[...].astype(F32) + d_ref[...].astype(F32)
@@ -285,18 +281,28 @@
     scale = lax.rsqrt(jnp.sum(summed * summed, axis=1, keepdims=True) / D + EPS)
     image = summed * scale * gain_ref[...]
     residual = image - x
-    image_held[...] = image
-    residual_held[...] = residual
-    copies = [
-        pltpu.make_async_copy(image_held, image_out, sem.at[0]),
-        pltpu.make_async_copy(residual_held, residual_out, sem.at[1]),
-    ]
-    copies += home_copies(image_held, home_out, k % 2, sem, 2)
-    for copy in copies:
-        copy.start()
-    if k < ITERS - 1:
-        rest[7][...] = ((image + inj) * gain_in_ref[...]).astype(BF16)
+    copies = []
+    if k >= 2:
+        rest, (image_ref, residual_ref, sem) = rest[:-3], rest[-3:]
+        rest = rest[5:] if k == ITERS - 1 else rest
+        image_ref[...] = image
+        copies = home_copies(image_ref, rest[:5], k % 2, sem, 3)
+        rest = rest[5:]
+        if k == 2:
+            residual_ref[...] = residual
+            copies.append(pltpu.make_async_copy(image_ref, rest[0], sem.at[1]))
+            copies.append(pltpu.make_async_copy(residual_ref, rest[1], sem.at[2]))
+            rest[2][...] = ((image + inj) * gain_in_ref[...]).astype(BF16)
+            rest = rest[3:]
+        for copy in copies:
+            copy.start()
+    else:
+        rest[0][...] = image
+        rest[1][...] = ((image + inj) * gain_in_ref[...]).astype(BF16)
+        rest = rest[2:]
     if k > 0:
+        table_out, dots_held = rest[0], rest[1]
+        table_sem = sem.at[0] if k >= 2 else rest[2]
         lane = lax.broadcasted_iota(jnp.int32, (1, 128), 1)
         dots = jnp.where(lane == k, total(residual * residual), 0.0)
         for at, other in enumerate(older):
@@ -304,9 +310,22 @@
         if k == 1:
             dots = dots + jnp.where(lane == 7, total(older[0][...] * older[0][...]), 0.0)
         dots_held[...] = jnp.broadcast_to(dots.reshape(1, 1, 128), (128, 1, 128))
-        table_out = rest[8] if k < ITERS - 1 else rest[7]
-        copies.append(pltpu.make_async_copy(dots_held, table_out, sem.at[10]))
+        copies.append(pltpu.make_async_copy(dots_held, table_out, table_sem))
         copies[-1].start()
+    for copy in copies:
+        copy.wait()
+
+
+def store_kernel(k, image_ref, x_ref, *rest):
+    rest = rest[5:] if k % 2 == 1 else rest
+    (image_out, residual_out), home_out, (residual_ref, sem) = rest[:2], rest[2:7], rest[7:]
+    copies = [pltpu.make_async_copy(image_ref, image_out, sem.at[0])]
+    copies += home_copies(image_ref, home_out, k % 2, sem, 2)
+    for copy in copies:
+        copy.start()
+    residual_ref[...] = image_ref[...] - x_ref[...].astype(F32)
+    copies.append(pltpu.make_async_copy(residual_ref, residual_out, sem.at[1]))
+    copies[-1].start()
     for copy in copies:
         copy.wait()
 
@@ -551,12 +570,17 @@
         for by in (1, 2, 3):
             piece = pair[16 * by : 16 * by + 16].astype(BF16)
             arrived.append(lax.ppermute(piece, "y", shift(4, -by)))
-        shapes = [tokens, tokens, *home_packed]
-        if k < ITERS - 1:
-            shapes.append(narrow)
+        last = k == ITERS - 1
+        shapes = [*home_packed, *([] if last else [tokens, tokens, narrow])] if k >= 2 else [wide, narrow]
+        scratch = []
         if k > 0:
             shapes.append(pltpu.HBM((128, 1, 128), F32))
-        packed = list(home) if k % 2 == 1 else []
+            scratch.append(pltpu.VMEM((128, 1, 128), F32))
+        if k == 1:
+            scratch.append(pltpu.SemaphoreType.DMA)
+        if k >= 2:
+            scratch += [pltpu.VMEM((16, D), F32)] * 2 + [pltpu.SemaphoreType.DMA((11,))]
+        packed = list(home) if last else []
         outs = call(
             functools.partial(finish_kernel, k),
             tuple(shapes),
@@ -569,22 +593,35 @@
             *residuals,
             *packed,
             specs=[VMEM] * (8 + len(residuals)) + [HBM] * len(packed),
-            aliases={8 + k + at: 2 + at for at in range(len(packed))},
-            scratch=[
-                pltpu.VMEM((16, D), F32),
-                pltpu.VMEM((16, D), F32),
-                pltpu.VMEM((128, 1, 128), F32),
-                pltpu.SemaphoreType.DMA((11,)),
-            ],
+            aliases={8 + k + at: at for at in range(len(packed))},
+            scratch=scratch,
         )
-        images.append(outs[0])
-        residuals.append(outs[1])
-        home = outs[2:7]
-        payload = outs[7]
-        if k == 0:
-            current = outs[0]
-        else:
-            dots = outs[-1]
+        dots = outs[-1] if k > 0 else None
+        if k >= 2:
+            home = outs[:5]
+        if k == 2:
+            image, residual, payload = outs[5:8]
+            images.append(image)
+            residuals.append(residual)
+        if k < 2:
+            image, payload = outs[:2]
+        if k < 2:
+            packed = list(home) if k % 2 == 1 else []
+            outs = call(
+                functools.partial(store_kernel, k),
+                (tokens, tokens, *home_packed),
+                image,
+                current,
+                *packed,
+                specs=[VMEM] * 2 + [HBM] * len(packed),
+                aliases={2 + at: 2 + at for at in range(len(packed))},
+                scratch=[pltpu.VMEM((16, D), F32), pltpu.SemaphoreType.DMA((10,))],
+            )
+            images.append(outs[0])
+            residuals.append(outs[1])
+            home = outs[2:7]
+            if k == 0:
+                current = outs[0]
     settled = settled + move_home(home)
     tables.append(lax.all_to_all(dots, EVERY, split_axis=0, concat_axis=0, tiled=True))
     return call(

time: 310 us -> 311 us (level)
    pallas_call x19 -> x21, Pallas kernels: 51.5 us -> 51.6 us  [call(): pl.pallas_call(kernel, out_shape=outs, in_specs=specs, input_output_alias...]
where the time goes in v3:
time: 311 us; the launch traced here: 310 us
  waiting for transfers between devices  138 us (44%)
  starting transfers between devices  78.2 us (25%)
  Pallas kernels  74.7 us (24%)
  blocking collectives  13.2 us (4%)
    pallas_call x21, Pallas kernels, call(): pl.pallas_call(kernel, out_shape=outs, in_specs=specs, input_output_alias...  51.6 us
    ppermute x12, waiting for transfers between devices, on_device(): arrived.append(lax.ppermute(piece, 'y', shift(4, -by)))  37.7 us
    ppermute x12, waiting for transfers between devices, on_device(): pieces.append(lax.ppermute(payload, 'y', shift(4, by)))  32.2 us
    ppermute x9, waiting for transfers between devices, move_home(): near.append(lax.ppermute(piece, 'y', shift(4, by + 1)))  26.1 us
    pallas_call x4, Pallas kernels, query_dot(): pl.pallas_call(functools.partial(query_kernel, len(parts) - 1), grid=(5,)...  23.1 us
    all_to_all x4, waiting for transfers between devices, on_device(): kv_all = lax.all_to_all(kv, SEQ, split_axis=0, concat_axis=0, tiled=True)  21.6 us
    all_to_all x4, starting transfers between devices, on_device(): kv_all = lax.all_to_all(kv, SEQ, split_axis=0, concat_axis=0, tiled=True)  18.6 us
    ppermute x12, starting transfers between devices, on_device(): pieces.append(lax.ppermute(payload, 'y', shift(4, by)))  13.7 us
  transfers between devices with their start and end apart: 50, of which 39 were waited for; matrix products, arithmetic and copies ran while one was open for 0% of the time, Pallas kernels for 11%

profile of v3, /device:TPU:1, one launch (start us, length us, event | category | flops | bytes accessed | tf_op | source)
XLA Modules:
  0.0 310.2 jit_solution(8406594877449446384)
XLA Ops:
  1.1 3.6 %collective-permute-start.2 = (bf16[128,640]{1,0:T(8,128)(2,1)S(1)}, bf16[128,640]{1,0:T(8,128)(2,1)S(1)}, u32[]{:S(2)}, u32[]{:S(2)}) collective-permute-start(bf16[128,640]{1,0:T(8,128)(2,1)S(1)} %get-tuple-element.84), channel_id=1, source_target_pairs={{0,6},{2,0},{4,2},{6,4},{1,7},{3,1},{5,3},{7,5},{8,14},{10,8},{12,... | collective-permute-start | bytes 491528 | tf_op jit(solution)/shard_map/ppermute | solution.py:485
  5.8 5.4 %collective-permute-done.2 = bf16[128,640]{1,0:T(8,128)(2,1)S(1)} collective-permute-done((bf16[128,640]{1,0:T(8,128)(2,1)S(1)}, bf16[128,640]{1,0:T(8,128)(2,1)S(1)}, u32[]{:S(2)}, u32[]{:S(2)}) %collective-permute-start.2) | collective-permute-done | bytes 163872 | tf_op jit(solution)/shard_map/ppermute | solution.py:485
  11.2 4.7 %collective-permute-done = bf16[128,640]{1,0:T(8,128)(2,1)S(1)} collective-permute-done((bf16[128,640]{1,0:T(8,128)(2,1)S(1)}, bf16[128,640]{1,0:T(8,128)(2,1)S(1)}, u32[]{:S(2)}, u32[]{:S(2)}) %collective-permute-start) | collective-permute-done | bytes 163872 | tf_op jit(solution)/shard_map/ppermute | solution.py:485
  18.3 3.9 %shard_map.83 = (bf16[128,5120]{1,0:T(8,128)(2,1)}, f32[128,128]{1,0:T(8,128)S(1)}, bf16[16,128,256]{2,1,0:T(8,128)(2,1)}) custom-call(bf16[5120,128]{1,0:T(8,128)(2,1)} %refs_0_.5, bf16[5120,128]{1,0:T(8,128)(2,1)} %refs_1_.9, f32[1,5120]{1,0:T(1,128)S(1)} %bitcast.10, bf16[4,128,640]{2,1,0:T(8,128)(2,1)S(1)} %pad_maximum_fusion.refs_0_, ...), custom_call_target="tpu_custom_call" | custom-call | flops 335544320 | bytes 4000000 | tf_op jit(solution)/shard_map/pallas_call | solution.py:43
  22.2 7.6 %all-to-all-start = ((bf16[16,128,256]{2,1,0:T(8,128)(2,1)}), bf16[16,128,256]{2,1,0:T(8,128)(2,1)S(1)}, u32[]{:S(2)}, u32[]{:S(2)}) async-start(bf16[16,128,256]{2,1,0:T(8,128)(2,1)} %get-tuple-element.87), calls=%async_computation | async-start | bytes 2097152 | tf_op jit(solution)/shard_map/all_to_all | solution.py:540
  38.5 5.5 %shard_map.84.q_ref = bf16[128,640]{1,0:T(8,128)(2,1)S(1)} custom-call(bf16[128,5120]{1,0:T(8,128)(2,1)} %get-tuple-element.85.refs_0_, bf16[5120,640]{1,0:T(8,128)(2,1)} %refs_4_.1), custom_call_target="tpu_custom_call" | custom-call | flops 838860800 | bytes 8000000 | tf_op jit(solution)/shard_map/pallas_call | solution.py:207
  45.5 5.8 %shard_map.85 = (f32[64,5120]{1,0:T(8,128)S(1)}, bf16[64,5120]{1,0:T(8,128)(2,1)S(1)}) custom-call(bf16[128,640]{1,0:T(8,128)(2,1)S(1)} %shard_map.84.q_ref, f32[128,128]{1,0:T(8,128)S(1)} %get-tuple-element.86.scale_ref, bf16[16,128,256]{2,1,0:T(8,128)(2,1)S(1)} %all-to-all-done.kv_ref, bf16[640,5120]{1,0:T(8,128)(2,1)} %w_ref.7), custom_call_target="tpu_custom_call" | custom-call | flops 1509949440 | bytes 9000000 | tf_op jit(solution)/shard_map/pallas_call | solution.py:43
  51.3 3.2 %collective-permute-start.8 = (bf16[64,5120]{1,0:T(8,128)(2,1)S(1)}, bf16[64,5120]{1,0:T(8,128)(2,1)S(1)}, u32[]{:S(2)}, u32[]{:S(2)}) collective-permute-start(bf16[64,5120]{1,0:T(8,128)(2,1)S(1)} %get-tuple-element.95), channel_id=1, source_target_pairs={{0,1},{1,0},{2,3},{3,2},{4,5},{5,4},{6,7},{7,6},{8,9},{9,8},{10,11... | collective-permute-start | bytes 1966088 | tf_op jit(solution)/shard_map/ppermute | solution.py:568
  58.1 3.8 %collective-permute-done.9.a_ref = bf16[16,5120]{1,0:T(8,128)(2,1)S(1)} collective-permute-done((bf16[16,5120]{1,0:T(8,128)(2,1)S(1)}, bf16[16,5120]{1,0:T(8,128)(2,1)S(1)}, u32[]{:S(2)}, u32[]{:S(2)}) %collective-permute-start.9) | collective-permute-done | bytes 163872 | tf_op jit(solution)/shard_map/ppermute | solution.py:572
  63.5 4.5 %collective-permute-done.11.d_ref = bf16[16,5120]{1,0:T(8,128)(2,1)S(1)} collective-permute-done((bf16[16,5120]{1,0:T(8,128)(2,1)S(1)}, bf16[16,5120]{1,0:T(8,128)(2,1)S(1)}, u32[]{:S(2)}, u32[]{:S(2)}) %collective-permute-start.11) | collective-permute-done | bytes 163872 | tf_op jit(solution)/shard_map/ppermute | solution.py:572
  71.2 7.4 %collective-permute-done.12 = bf16[16,5120]{1,0:T(8,128)(2,1)S(1)} collective-permute-done((bf16[16,5120]{1,0:T(8,128)(2,1)S(1)}, bf16[16,5120]{1,0:T(8,128)(2,1)S(1)}, u32[]{:S(2)}, u32[]{:S(2)}) %collective-permute-start.12) | collective-permute-done | bytes 163872 | tf_op jit(solution)/shard_map/ppermute | solution.py:485
  82.2 3.4 %shard_map.88 = (bf16[128,5120]{1,0:T(8,128)(2,1)}, f32[128,384]{1,0:T(8,128)S(1)}, f32[128,128]{1,0:T(8,128)S(1)}, bf16[16,128,256]{2,1,0:T(8,128)(2,1)}) custom-call(bf16[5120,128]{1,0:T(8,128)(2,1)} %refs_0_.5, bf16[5120,128]{1,0:T(8,128)(2,1)} %refs_1_.9, f32[1,5120]{1,0:T(1,128)S(1)} %bitcast.12, ...), custom_call_target="tpu_custom_call" | custom-call | flops 335544320 | bytes 4000000 | tf_op jit(solution)/shard_map/pallas_call | solution.py:43
  85.7 3.7 %all-to-all-start.1 = ((bf16[16,128,256]{2,1,0:T(8,128)(2,1)}), bf16[16,128,256]{2,1,0:T(8,128)(2,1)S(1)}, u32[]{:S(2)}, u32[]{:S(2)}) async-start(bf16[16,128,256]{2,1,0:T(8,128)(2,1)} %get-tuple-element.106), calls=%async_computation.1 | async-start | bytes 2097152 | tf_op jit(solution)/shard_map/all_to_all | solution.py:540
  89.3 5.5 %shard_map.89.q_ref = bf16[128,640]{1,0:T(8,128)(2,1)S(1)} custom-call(bf16[128,5120]{1,0:T(8,128)(2,1)} %get-tuple-element.104.refs_0_.refs_3_.refs_1_, bf16[5120,640]{1,0:T(8,128)(2,1)} %refs_4_.1), custom_call_target="tpu_custom_call" | custom-call | flops 838860800 | bytes 8000000 | tf_op jit(solution)/shard_map/pallas_call | solution.py:207
  94.8 10.6 %all-to-all-done.1.kv_ref = bf16[16,128,256]{2,1,0:T(8,128)(2,1)S(1)} async-done(((bf16[16,128,256]{2,1,0:T(8,128)(2,1)}), bf16[16,128,256]{2,1,0:T(8,128)(2,1)S(1)}, u32[]{:S(2)}, u32[]{:S(2)}) %all-to-all-start.1) | async-done | bytes 1048608 | tf_op jit(solution)/shard_map/all_to_all | solution.py:540
  105.5 5.8 %shard_map.90 = (f32[64,5120]{1,0:T(8,128)S(1)}, bf16[64,5120]{1,0:T(8,128)(2,1)S(1)}) custom-call(bf16[128,640]{1,0:T(8,128)(2,1)S(1)} %shard_map.89.q_ref, f32[128,128]{1,0:T(8,128)S(1)} %get-tuple-element.105.scale_ref, bf16[16,128,256]{2,1,0:T(8,128)(2,1)S(1)} %all-to-all-done.1.kv_ref, bf16[640,5120]{1,0:T(8,128)(2,1)} %w_ref.7), custom_call_target="tpu_custom_call" | custom-call | flops 1509949440 | bytes 9000000 | tf_op jit(solution)/shard_map/pallas_call | solution.py:43
  111.3 2.6 collective-permute-start.16
  115.9 2.2 collective-permute-start.17
  121.7 3.1 collective-permute-done.18.b_ref
  124.8 3.9 %collective-permute-done.19.d_ref = bf16[16,5120]{1,0:T(8,128)(2,1)S(1)} collective-permute-done((bf16[16,5120]{1,0:T(8,128)(2,1)S(1)}, bf16[16,5120]{1,0:T(8,128)(2,1)S(1)}, u32[]{:S(2)}, u32[]{:S(2)}) %collective-permute-start.19) | collective-permute-done | bytes 163872 | tf_op jit(solution)/shard_map/ppermute | solution.py:572
  134.7 7.3 %collective-permute-done.20 = bf16[16,5120]{1,0:T(8,128)(2,1)S(1)} collective-permute-done((bf16[16,5120]{1,0:T(8,128)(2,1)S(1)}, bf16[16,5120]{1,0:T(8,128)(2,1)S(1)}, u32[]{:S(2)}, u32[]{:S(2)}) %collective-permute-start.20) | collective-permute-done | bytes 163872 | tf_op jit(solution)/shard_map/ppermute | solution.py:485
  144.0 5.0 %all-to-all-start.2 = ((f32[128,1,128]{2,1,0:T(1,128)}), f32[128,1,128]{2,1,0:T(1,128)S(1)}, u32[]{:S(2)}, u32[]{:S(2)}) async-start(f32[128,1,128]{2,1,0:T(1,128)} %get-tuple-element.112), calls=%async_computation.2 | async-start | bytes 131072 | tf_op jit(solution)/shard_map/all_to_all | solution.py:487
  149.0 3.6 %shard_map.93 = (bf16[128,5120]{1,0:T(8,128)(2,1)}, f32[128,384]{1,0:T(8,128)S(1)}) custom-call(bf16[5120,128]{1,0:T(8,128)(2,1)} %refs_0_.5, bf16[5120,128]{1,0:T(8,128)(2,1)} %refs_1_.9, f32[1,5120]{1,0:T(1,128)S(1)} %bitcast.14, bf16[128,5120]{1,0:T(8,128)(2,1)} %get-tuple-element.104.refs_0_.refs_3_.refs_1_, ...), custom_call_target="tpu_custom_call" | custom-call | flops 335544320 | bytes 4000000 | tf_op jit(solution)/shard_map/pallas_call | solution.py:43
  152.6 5.9 %all-to-all-done.2.refs_0_ = f32[128,1,128]{2,1,0:T(1,128)S(1)} async-done(((f32[128,1,128]{2,1,0:T(1,128)}), f32[128,1,128]{2,1,0:T(1,128)S(1)}, u32[]{:S(2)}, u32[]{:S(2)}) %all-to-all-start.2) | async-done | bytes 65568 | tf_op jit(solution)/shard_map/all_to_all | solution.py:487
  159.9 3.7 %all-to-all-start.3 = ((bf16[16,128,256]{2,1,0:T(8,128)(2,1)}), bf16[16,128,256]{2,1,0:T(8,128)(2,1)S(1)}, u32[]{:S(2)}, u32[]{:S(2)}) async-start(bf16[16,128,256]{2,1,0:T(8,128)(2,1)} %get-tuple-element.119), calls=%async_computation.3 | async-start | bytes 2097152 | tf_op jit(solution)/shard_map/all_to_all | solution.py:540
  166.9 3.0 collective-permute-done.26.refs_6_
  169.9 2.6 collective-permute-done.25.refs_5_
  172.4 4.6 %collective-permute-done.24.refs_4_ = f32[2,2,16,640]{3,2,1,0:T(8,128)S(1)} collective-permute-done((f32[2,2,16,640]{3,2,1,0:T(8,128)}, f32[2,2,16,640]{3,2,1,0:T(8,128)S(1)}, u32[]{:S(2)}, u32[]{:S(2)}) %collective-permute-start.24) | collective-permute-done | bytes 163872 | tf_op jit(solution)/shard_map/ppermute | solution.py:447
  178.8 5.9 %shard_map.95.q_ref = bf16[128,640]{1,0:T(8,128)(2,1)S(1)} custom-call(f32[1,128]{1,0:T(1,128)S(1)} %get-tuple-element.116.refs_0_.share_ref, bf16[128,5120]{1,0:T(8,128)(2,1)} %get-tuple-element.104.refs_0_.refs_3_.refs_1_, bf16[128,5120]{1,0:T(8,128)(2,1)} %get-tuple-element.117.refs_2_.refs_4_, bf16[5120,640]{1,0:T(8,128)(2,1)} %refs_4_.1), custom_call_target="tpu_custom_call" | custom-call | flops 838860800 | bytes 8000000 | tf_op jit(solution)/shard_map/pallas_call | solution.py:207
  184.7 5.8 %shard_map.97 = (f32[64,5120]{1,0:T(8,128)S(1)}, bf16[64,5120]{1,0:T(8,128)(2,1)S(1)}) custom-call(bf16[128,640]{1,0:T(8,128)(2,1)S(1)} %shard_map.95.q_ref, f32[128,128]{1,0:T(8,128)S(1)} %get-tuple-element.118.scale_ref, bf16[16,128,256]{2,1,0:T(8,128)(2,1)S(1)} %all-to-all-done.3.kv_ref, bf16[640,5120]{1,0:T(8,128)(2,1)} %w_ref.7), custom_call_target="tpu_custom_call" | custom-call | flops 1509949440 | bytes 9000000 | tf_op jit(solution)/shard_map/pallas_call | solution.py:43
  195.0 3.6 %collective-permute-done.29.a_ref = bf16[16,5120]{1,0:T(8,128)(2,1)S(1)} collective-permute-done((bf16[16,5120]{1,0:T(8,128)(2,1)S(1)}, bf16[16,5120]{1,0:T(8,128)(2,1)S(1)}, u32[]{:S(2)}, u32[]{:S(2)}) %collective-permute-start.29) | collective-permute-done | bytes 163872 | tf_op jit(solution)/shard_map/ppermute | solution.py:572
  200.2 4.2 %collective-permute-done.31.d_ref = bf16[16,5120]{1,0:T(8,128)(2,1)S(1)} collective-permute-done((bf16[16,5120]{1,0:T(8,128)(2,1)S(1)}, bf16[16,5120]{1,0:T(8,128)(2,1)S(1)}, u32[]{:S(2)}, u32[]{:S(2)}) %collective-permute-start.31) | collective-permute-done | bytes 163872 | tf_op jit(solution)/shard_map/ppermute | solution.py:572
  209.1 6.9 %collective-permute-done.32 = bf16[16,5120]{1,0:T(8,128)(2,1)S(1)} collective-permute-done((bf16[16,5120]{1,0:T(8,128)(2,1)S(1)}, bf16[16,5120]{1,0:T(8,128)(2,1)S(1)}, u32[]{:S(2)}, u32[]{:S(2)}) %collective-permute-start.32) | collective-permute-done | bytes 163872 | tf_op jit(solution)/shard_map/ppermute | solution.py:485
  218.1 8.5 %all-to-all-start.4 = ((f32[128,1,128]{2,1,0:T(1,128)}), f32[128,1,128]{2,1,0:T(1,128)S(1)}, u32[]{:S(2)}, u32[]{:S(2)}) async-start(f32[128,1,128]{2,1,0:T(1,128)} %get-tuple-element.136), calls=%async_computation.4 | async-start | bytes 131072 | tf_op jit(solution)/shard_map/all_to_all | solution.py:487
  226.7 5.7 %shard_map.100 = (bf16[128,5120]{1,0:T(8,128)(2,1)}, f32[128,384]{1,0:T(8,128)S(1)}) custom-call(bf16[5120,128]{1,0:T(8,128)(2,1)} %refs_0_.5, bf16[5120,128]{1,0:T(8,128)(2,1)} %refs_1_.9, f32[1,5120]{1,0:T(1,128)S(1)} %bitcast.16, bf16[128,5120]{1,0:T(8,128)(2,1)} %get-tuple-element.104.refs_0_.refs_3_.refs_1_, ...), custom_call_target="tpu_custom_call" | custom-call | flops 335544320 | bytes 4000000 | tf_op jit(solution)/shard_map/pallas_call | solution.py:43
  232.4 3.8 %all-to-all-done.4.refs_1_ = f32[128,1,128]{2,1,0:T(1,128)S(1)} async-done(((f32[128,1,128]{2,1,0:T(1,128)}), f32[128,1,128]{2,1,0:T(1,128)S(1)}, u32[]{:S(2)}, u32[]{:S(2)}) %all-to-all-start.4) | async-done | bytes 65568 | tf_op jit(solution)/shard_map/all_to_all | solution.py:487
  237.8 3.7 %all-to-all-start.5 = ((bf16[16,128,256]{2,1,0:T(8,128)(2,1)}), bf16[16,128,256]{2,1,0:T(8,128)(2,1)S(1)}, u32[]{:S(2)}, u32[]{:S(2)}) async-start(bf16[16,128,256]{2,1,0:T(8,128)(2,1)} %get-tuple-element.142), calls=%async_computation.5 | async-start | bytes 2097152 | tf_op jit(solution)/shard_map/all_to_all | solution.py:540
  241.4 6.2 %shard_map.102.q_ref = bf16[128,640]{1,0:T(8,128)(2,1)S(1)} custom-call(f32[1,128]{1,0:T(1,128)S(1)} %get-tuple-element.139.refs_0_.share_ref, bf16[128,5120]{1,0:T(8,128)(2,1)} %get-tuple-element.104.refs_0_.refs_3_.refs_1_, bf16[128,5120]{1,0:T(8,128)(2,1)} %get-tuple-element.117.refs_2_.refs_4_, bf16[128,5120]{1,0:T(8,128)(2,1)} %get-tuple-element.140.refs_3_, ...), custom_call_target="tpu_custom_call" | custom-call | flops 838860800 | bytes 8000000 | tf_op jit(solution)/shard_map/pallas_call | solution.py:207
  247.7 9.4 %all-to-all-done.5.kv_ref = bf16[16,128,256]{2,1,0:T(8,128)(2,1)S(1)} async-done(((bf16[16,128,256]{2,1,0:T(8,128)(2,1)}), bf16[16,128,256]{2,1,0:T(8,128)(2,1)S(1)}, u32[]{:S(2)}, u32[]{:S(2)}) %all-to-all-start.5) | async-done | bytes 1048608 | tf_op jit(solution)/shard_map/all_to_all | solution.py:540
  257.1 5.8 %shard_map.103 = (f32[64,5120]{1,0:T(8,128)S(1)}, bf16[64,5120]{1,0:T(8,128)(2,1)S(1)}) custom-call(bf16[128,640]{1,0:T(8,128)(2,1)S(1)} %shard_map.102.q_ref, f32[128,128]{1,0:T(8,128)S(1)} %get-tuple-element.141.scale_ref, bf16[16,128,256]{2,1,0:T(8,128)(2,1)S(1)} %all-to-all-done.5.kv_ref, bf16[640,5120]{1,0:T(8,128)(2,1)} %w_ref.7), custom_call_target="tpu_custom_call" | custom-call | flops 1509949440 | bytes 9000000 | tf_op jit(solution)/shard_map/pallas_call | solution.py:43
  262.9 3.1 collective-permute-start.36
  267.9 2.4 collective-permute-start.37
  271.6 2.5 collective-permute-done.37.a_ref
  274.1 2.9 collective-permute-done.38.b_ref
  276.9 4.5 %collective-permute-done.39.d_ref = bf16[16,5120]{1,0:T(8,128)(2,1)S(1)} collective-permute-done((bf16[16,5120]{1,0:T(8,128)(2,1)S(1)}, bf16[16,5120]{1,0:T(8,128)(2,1)S(1)}, u32[]{:S(2)}, u32[]{:S(2)}) %collective-permute-start.39) | collective-permute-done | bytes 163872 | tf_op jit(solution)/shard_map/ppermute | solution.py:572
  284.2 4.0 %collective-permute-done.42.refs_11_ = f32[2,2,16,640]{3,2,1,0:T(8,128)S(1)} collective-permute-done((f32[2,2,16,640]{3,2,1,0:T(8,128)}, f32[2,2,16,640]{3,2,1,0:T(8,128)S(1)}, u32[]{:S(2)}, u32[]{:S(2)}) %collective-permute-start.42) | collective-permute-done | bytes 163872 | tf_op jit(solution)/shard_map/ppermute | solution.py:447
  289.3 4.9 %collective-permute-done.40.refs_9_ = f32[2,2,16,640]{3,2,1,0:T(8,128)S(1)} collective-permute-done((f32[2,2,16,640]{3,2,1,0:T(8,128)}, f32[2,2,16,640]{3,2,1,0:T(8,128)S(1)}, u32[]{:S(2)}, u32[]{:S(2)}) %collective-permute-start.40) | collective-permute-done | bytes 163872 | tf_op jit(solution)/shard_map/ppermute | solution.py:447
  295.7 13.2 %all_to_all.35.refs_2_ = f32[128,1,128]{2,1,0:T(1,128)S(1)} all-to-all(f32[128,1,128]{2,1,0:T(1,128)} %get-tuple-element.152), channel_id=1, replica_groups=mesh['x'=4,'z'=4,'y'=4,'c'=2] {'x','z','y','c'}, dimensions={0} | all-to-all | bytes 131072 | tf_op jit(solution)/shard_map/all_to_all | solution.py:626
  (147 shorter events, 70.4 us)
Async XLA Ops:
  1.1 10.1 %collective-permute-start.2 = (bf16[128,640]{1,0:T(8,128)(2,1)S(1)}, bf16[128,640]{1,0:T(8,128)(2,1)S(1)}, u32[]{:S(2)}, u32[]{:S(2)}) collective-permute-start(bf16[128,640]{1,0:T(8,128)(2,1)S(1)} %get-tuple-element.84), channel_id=1, source_target_pairs={{0,6},{2,0},{4,2},{6,4},{1,7},{3,1},{5,3},{7,5},{8,14},{10,8},{12,... | collective-permute-start | bytes 491528 | tf_op jit(solution)/shard_map/ppermute | solution.py:485
  4.7 6.4 %collective-permute-start.1 = (bf16[128,640]{1,0:T(8,128)(2,1)S(1)}, bf16[128,640]{1,0:T(8,128)(2,1)S(1)}, u32[]{:S(2)}, u32[]{:S(2)}) collective-permute-start(bf16[128,640]{1,0:T(8,128)(2,1)S(1)} %get-tuple-element.84), channel_id=1, source_target_pairs={{0,4},{2,6},{4,0},{6,2},{1,5},{3,7},{5,1},{7,3},{8,12},{10,14},{12... | collective-permute-start | bytes 491528 | tf_op jit(solution)/shard_map/ppermute | solution.py:485
  5.1 10.8 %collective-permute-start = (bf16[128,640]{1,0:T(8,128)(2,1)S(1)}, bf16[128,640]{1,0:T(8,128)(2,1)S(1)}, u32[]{:S(2)}, u32[]{:S(2)}) collective-permute-start(bf16[128,640]{1,0:T(8,128)(2,1)S(1)} %get-tuple-element.84), channel_id=1, source_target_pairs={{0,2},{2,4},{4,6},{6,0},{1,3},{3,5},{5,7},{7,1},{8,10},{10,12},{12... | collective-permute-start | bytes 491528 | tf_op jit(solution)/shard_map/ppermute | solution.py:485
  22.2 23.3 %all-to-all-start = ((bf16[16,128,256]{2,1,0:T(8,128)(2,1)}), bf16[16,128,256]{2,1,0:T(8,128)(2,1)S(1)}, u32[]{:S(2)}, u32[]{:S(2)}) async-start(bf16[16,128,256]{2,1,0:T(8,128)(2,1)} %get-tuple-element.87), calls=%async_computation | async-start | bytes 2097152 | tf_op jit(solution)/shard_map/all_to_all | solution.py:540
  29.8 3.4 %collective-permute-start.6 = (bf16[2,2,16,640]{3,2,1,0:T(8,128)(2,1)S(1)}, bf16[2,2,16,640]{3,2,1,0:T(8,128)(2,1)S(1)}, u32[]{:S(2)}, u32[]{:S(2)}) collective-permute-start(bf16[2,2,16,640]{3,2,1,0:T(8,128)(2,1)S(1)} %get-tuple-element.91), channel_id=1, source_target_pairs={{0,6},{2,0},{4,2},{6,4},{1,7},{3,1},{5,3},{7,5},{8,14},{10,8},{12,... | collective-permute-start | bytes 245768 | tf_op jit(solution)/shard_map/ppermute | solution.py:447
  30.2 5.1 %collective-permute-start.5 = (bf16[2,2,16,640]{3,2,1,0:T(8,128)(2,1)S(1)}, bf16[2,2,16,640]{3,2,1,0:T(8,128)(2,1)S(1)}, u32[]{:S(2)}, u32[]{:S(2)}) collective-permute-start(bf16[2,2,16,640]{3,2,1,0:T(8,128)(2,1)S(1)} %get-tuple-element.90), channel_id=1, source_target_pairs={{0,4},{2,6},{4,0},{6,2},{1,5},{3,7},{5,1},{7,3},{8,12},{10,14},{12... | collective-permute-start | bytes 245768 | tf_op jit(solution)/shard_map/ppermute | solution.py:447
  30.5 6.8 %collective-permute-start.4 = (bf16[2,2,16,640]{3,2,1,0:T(8,128)(2,1)S(1)}, bf16[2,2,16,640]{3,2,1,0:T(8,128)(2,1)S(1)}, u32[]{:S(2)}, u32[]{:S(2)}) collective-permute-start(bf16[2,2,16,640]{3,2,1,0:T(8,128)(2,1)S(1)} %get-tuple-element.89), channel_id=1, source_target_pairs={{0,2},{2,4},{4,6},{6,0},{1,3},{3,5},{5,7},{7,1},{8,10},{10,12},{12... | collective-permute-start | bytes 245768 | tf_op jit(solution)/shard_map/ppermute | solution.py:447
  37.3 6.6 %collective-permute-start.7 = (bf16[4,2,16,640]{3,2,1,0:T(8,128)(2,1)S(1)}, bf16[4,2,16,640]{3,2,1,0:T(8,128)(2,1)S(1)}, u32[]{:S(2)}, u32[]{:S(2)}) collective-permute-start(bf16[4,2,16,640]{3,2,1,0:T(8,128)(2,1)S(1)} %pad_maximum_fusion.3), channel_id=1, source_target_pairs={{0,1},{1,0},{2,3},{3,2},{4,5},{5,4},{6,7},{7,6},{8,9},{9,8},{10,11... | collective-permute-start | bytes 491528 | tf_op jit(solution)/shard_map/ppermute | solution.py:449
  51.3 4.9 %collective-permute-start.8 = (bf16[64,5120]{1,0:T(8,128)(2,1)S(1)}, bf16[64,5120]{1,0:T(8,128)(2,1)S(1)}, u32[]{:S(2)}, u32[]{:S(2)}) collective-permute-start(bf16[64,5120]{1,0:T(8,128)(2,1)S(1)} %get-tuple-element.95), channel_id=1, source_target_pairs={{0,1},{1,0},{2,3},{3,2},{4,5},{5,4},{6,7},{7,6},{8,9},{9,8},{10,11... | collective-permute-start | bytes 1966088 | tf_op jit(solution)/shard_map/ppermute | solution.py:568
  56.4 5.5 %collective-permute-start.9 = (bf16[16,5120]{1,0:T(8,128)(2,1)S(1)}, bf16[16,5120]{1,0:T(8,128)(2,1)S(1)}, u32[]{:S(2)}, u32[]{:S(2)}) collective-permute-start(bf16[16,5120]{1,0:T(8,128)(2,1)S(1)} %get-tuple-element.182), channel_id=1, source_target_pairs={{0,6},{2,0},{4,2},{6,4},{1,7},{3,1},{5,3},{7,5},{8,14},{10,8},{12,... | collective-permute-start | bytes 491528 | tf_op jit(solution)/shard_map/ppermute | solution.py:572
  56.8 6.6 %collective-permute-start.10 = (bf16[16,5120]{1,0:T(8,128)(2,1)S(1)}, bf16[16,5120]{1,0:T(8,128)(2,1)S(1)}, u32[]{:S(2)}, u32[]{:S(2)}) collective-permute-start(bf16[16,5120]{1,0:T(8,128)(2,1)S(1)} %get-tuple-element.181), channel_id=1, source_target_pairs={{0,4},{2,6},{4,0},{6,2},{1,5},{3,7},{5,1},{7,3},{8,12},{10,14},{12... | collective-permute-start | bytes 491528 | tf_op jit(solution)/shard_map/ppermute | solution.py:572
  57.1 10.8 %collective-permute-start.11 = (bf16[16,5120]{1,0:T(8,128)(2,1)S(1)}, bf16[16,5120]{1,0:T(8,128)(2,1)S(1)}, u32[]{:S(2)}, u32[]{:S(2)}) collective-permute-start(bf16[16,5120]{1,0:T(8,128)(2,1)S(1)} %get-tuple-element.180), channel_id=1, source_target_pairs={{0,2},{2,4},{4,6},{6,0},{1,3},{3,5},{5,7},{7,1},{8,10},{10,12},{12... | collective-permute-start | bytes 491528 | tf_op jit(solution)/shard_map/ppermute | solution.py:572
  68.3 10.3 %collective-permute-start.12 = (bf16[16,5120]{1,0:T(8,128)(2,1)S(1)}, bf16[16,5120]{1,0:T(8,128)(2,1)S(1)}, u32[]{:S(2)}, u32[]{:S(2)}) collective-permute-start(bf16[16,5120]{1,0:T(8,128)(2,1)S(1)} %get-tuple-element.103), channel_id=1, source_target_pairs={{0,2},{2,4},{4,6},{6,0},{1,3},{3,5},{5,7},{7,1},{8,10},{10,12},{12... | collective-permute-start | bytes 491528 | tf_op jit(solution)/shard_map/ppermute | solution.py:485
  68.4 10.2 %collective-permute-start.13 = (bf16[16,5120]{1,0:T(8,128)(2,1)S(1)}, bf16[16,5120]{1,0:T(8,128)(2,1)S(1)}, u32[]{:S(2)}, u32[]{:S(2)}) collective-permute-start(bf16[16,5120]{1,0:T(8,128)(2,1)S(1)} %get-tuple-element.103), channel_id=1, source_target_pairs={{0,4},{2,6},{4,0},{6,2},{1,5},{3,7},{5,1},{7,3},{8,12},{10,14},{12... | collective-permute-start | bytes 491528 | tf_op jit(solution)/shard_map/ppermute | solution.py:485
  69.5 9.4 %collective-permute-start.14 = (bf16[16,5120]{1,0:T(8,128)(2,1)S(1)}, bf16[16,5120]{1,0:T(8,128)(2,1)S(1)}, u32[]{:S(2)}, u32[]{:S(2)}) collective-permute-start(bf16[16,5120]{1,0:T(8,128)(2,1)S(1)} %get-tuple-element.103), channel_id=1, source_target_pairs={{0,6},{2,0},{4,2},{6,4},{1,7},{3,1},{5,3},{7,5},{8,14},{10,8},{12,... | collective-permute-start | bytes 491528 | tf_op jit(solution)/shard_map/ppermute | solution.py:485
  78.8 3.4 %collective-permute-start.15 = (bf16[64,5120]{1,0:T(8,128)(2,1)S(1)}, bf16[64,5120]{1,0:T(8,128)(2,1)S(1)}, u32[]{:S(2)}, u32[]{:S(2)}) collective-permute-start(bf16[64,5120]{1,0:T(8,128)(2,1)S(1)} %constant_dynamic-update-slice_fusion.refs_3_), channel_id=1, source_target_pairs={{0,1},{1,0},{2,3},{3,2},{4,5},{5,4},{6,7},{7,6},{8,9},{9,8},{10,11... | collective-permute-start | bytes 1966088 | tf_op jit(solution)/shard_map/ppermute | solution.py:489
  85.7 19.8 %all-to-all-start.1 = ((bf16[16,128,256]{2,1,0:T(8,128)(2,1)}), bf16[16,128,256]{2,1,0:T(8,128)(2,1)S(1)}, u32[]{:S(2)}, u32[]{:S(2)}) async-start(bf16[16,128,256]{2,1,0:T(8,128)(2,1)} %get-tuple-element.106), calls=%async_computation.1 | async-start | bytes 2097152 | tf_op jit(solution)/shard_map/all_to_all | solution.py:540
  111.3 4.3 %collective-permute-start.16 = (bf16[64,5120]{1,0:T(8,128)(2,1)S(1)}, bf16[64,5120]{1,0:T(8,128)(2,1)S(1)}, u32[]{:S(2)}, u32[]{:S(2)}) collective-permute-start(bf16[64,5120]{1,0:T(8,128)(2,1)S(1)} %get-tuple-element.108), channel_id=1, source_target_pairs={{0,1},{1,0},{2,3},{3,2},{4,5},{5,4},{6,7},{7,6},{8,9},{9,8},{10,11... | collective-permute-start | bytes 1966088 | tf_op jit(solution)/shard_map/ppermute | solution.py:568
  115.9 5.8 %collective-permute-start.17 = (bf16[16,5120]{1,0:T(8,128)(2,1)S(1)}, bf16[16,5120]{1,0:T(8,128)(2,1)S(1)}, u32[]{:S(2)}, u32[]{:S(2)}) collective-permute-start(bf16[16,5120]{1,0:T(8,128)(2,1)S(1)} %get-tuple-element.179), channel_id=1, source_target_pairs={{0,6},{2,0},{4,2},{6,4},{1,7},{3,1},{5,3},{7,5},{8,14},{10,8},{12,... | collective-permute-start | bytes 491528 | tf_op jit(solution)/shard_map/ppermute | solution.py:572
  118.1 6.7 %collective-permute-start.18 = (bf16[16,5120]{1,0:T(8,128)(2,1)S(1)}, bf16[16,5120]{1,0:T(8,128)(2,1)S(1)}, u32[]{:S(2)}, u32[]{:S(2)}) collective-permute-start(bf16[16,5120]{1,0:T(8,128)(2,1)S(1)} %get-tuple-element.178), channel_id=1, source_target_pairs={{0,4},{2,6},{4,0},{6,2},{1,5},{3,7},{5,1},{7,3},{8,12},{10,14},{12... | collective-permute-start | bytes 491528 | tf_op jit(solution)/shard_map/ppermute | solution.py:572
  118.1 10.6 %collective-permute-start.19 = (bf16[16,5120]{1,0:T(8,128)(2,1)S(1)}, bf16[16,5120]{1,0:T(8,128)(2,1)S(1)}, u32[]{:S(2)}, u32[]{:S(2)}) collective-permute-start(bf16[16,5120]{1,0:T(8,128)(2,1)S(1)} %get-tuple-element.177), channel_id=1, source_target_pairs={{0,2},{2,4},{4,6},{6,0},{1,3},{3,5},{5,7},{7,1},{8,10},{10,12},{12... | collective-permute-start | bytes 491528 | tf_op jit(solution)/shard_map/ppermute | solution.py:572
  131.7 10.2 %collective-permute-start.20 = (bf16[16,5120]{1,0:T(8,128)(2,1)S(1)}, bf16[16,5120]{1,0:T(8,128)(2,1)S(1)}, u32[]{:S(2)}, u32[]{:S(2)}) collective-permute-start(bf16[16,5120]{1,0:T(8,128)(2,1)S(1)} %get-tuple-element.114), channel_id=1, source_target_pairs={{0,2},{2,4},{4,6},{6,0},{1,3},{3,5},{5,7},{7,1},{8,10},{10,12},{12... | collective-permute-start | bytes 491528 | tf_op jit(solution)/shard_map/ppermute | solution.py:485
  131.8 10.1 %collective-permute-start.21 = (bf16[16,5120]{1,0:T(8,128)(2,1)S(1)}, bf16[16,5120]{1,0:T(8,128)(2,1)S(1)}, u32[]{:S(2)}, u32[]{:S(2)}) collective-permute-start(bf16[16,5120]{1,0:T(8,128)(2,1)S(1)} %get-tuple-element.114), channel_id=1, source_target_pairs={{0,4},{2,6},{4,0},{6,2},{1,5},{3,7},{5,1},{7,3},{8,12},{10,14},{12... | collective-permute-start | bytes 491528 | tf_op jit(solution)/shard_map/ppermute | solution.py:485
  133.0 9.0 %collective-permute-start.22 = (bf16[16,5120]{1,0:T(8,128)(2,1)S(1)}, bf16[16,5120]{1,0:T(8,128)(2,1)S(1)}, u32[]{:S(2)}, u32[]{:S(2)}) collective-permute-start(bf16[16,5120]{1,0:T(8,128)(2,1)S(1)} %get-tuple-element.114), channel_id=1, source_target_pairs={{0,6},{2,0},{4,2},{6,4},{1,7},{3,1},{5,3},{7,5},{8,14},{10,8},{12,... | collective-permute-start | bytes 491528 | tf_op jit(solution)/shard_map/ppermute | solution.py:485
  142.0 7.0 %collective-permute-start.23 = (bf16[64,5120]{1,0:T(8,128)(2,1)S(1)}, bf16[64,5120]{1,0:T(8,128)(2,1)S(1)}, u32[]{:S(2)}, u32[]{:S(2)}) collective-permute-start(bf16[64,5120]{1,0:T(8,128)(2,1)S(1)} %constant_dynamic-update-slice_fusion.4.refs_4_), channel_id=1, source_target_pairs={{0,1},{1,0},{2,3},{3,2},{4,5},{5,4},{6,7},{7,6},{8,9},{9,8},{10,11... | collective-permute-start | bytes 1966088 | tf_op jit(solution)/shard_map/ppermute | solution.py:489
  144.0 14.5 %all-to-all-start.2 = ((f32[128,1,128]{2,1,0:T(1,128)}), f32[128,1,128]{2,1,0:T(1,128)S(1)}, u32[]{:S(2)}, u32[]{:S(2)}) async-start(f32[128,1,128]{2,1,0:T(1,128)} %get-tuple-element.112), calls=%async_computation.2 | async-start | bytes 131072 | tf_op jit(solution)/shard_map/all_to_all | solution.py:487
  159.9 24.7 %all-to-all-start.3 = ((bf16[16,128,256]{2,1,0:T(8,128)(2,1)}), bf16[16,128,256]{2,1,0:T(8,128)(2,1)S(1)}, u32[]{:S(2)}, u32[]{:S(2)}) async-start(bf16[16,128,256]{2,1,0:T(8,128)(2,1)} %get-tuple-element.119), calls=%async_computation.3 | async-start | bytes 2097152 | tf_op jit(solution)/shard_map/all_to_all | solution.py:540
  164.7 5.2 %collective-permute-start.26 = (f32[2,2,16,640]{3,2,1,0:T(8,128)}, f32[2,2,16,640]{3,2,1,0:T(8,128)S(1)}, u32[]{:S(2)}, u32[]{:S(2)}) collective-permute-start(f32[2,2,16,640]{3,2,1,0:T(8,128)} %get-tuple-element.129), channel_id=1, source_target_pairs={{0,6},{2,0},{4,2},{6,4},{1,7},{3,1},{5,3},{7,5},{8,14},{10,8},{12,... | collective-permute-start | bytes 491528 | tf_op jit(solution)/shard_map/ppermute | solution.py:447
  165.8 6.6 %collective-permute-start.25 = (f32[2,2,16,640]{3,2,1,0:T(8,128)}, f32[2,2,16,640]{3,2,1,0:T(8,128)S(1)}, u32[]{:S(2)}, u32[]{:S(2)}) collective-permute-start(f32[2,2,16,640]{3,2,1,0:T(8,128)} %get-tuple-element.128), channel_id=1, source_target_pairs={{0,4},{2,6},{4,0},{6,2},{1,5},{3,7},{5,1},{7,3},{8,12},{10,14},{12... | collective-permute-start | bytes 491528 | tf_op jit(solution)/shard_map/ppermute | solution.py:447
  166.9 10.2 %collective-permute-start.24 = (f32[2,2,16,640]{3,2,1,0:T(8,128)}, f32[2,2,16,640]{3,2,1,0:T(8,128)S(1)}, u32[]{:S(2)}, u32[]{:S(2)}) collective-permute-start(f32[2,2,16,640]{3,2,1,0:T(8,128)} %get-tuple-element.127), channel_id=1, source_target_pairs={{0,2},{2,4},{4,6},{6,0},{1,3},{3,5},{5,7},{7,1},{8,10},{10,12},{12... | collective-permute-start | bytes 491528 | tf_op jit(solution)/shard_map/ppermute | solution.py:447
  178.1 6.6 %collective-permute-start.27 = (f32[4,2,16,640]{3,2,1,0:T(8,128)S(1)}, f32[4,2,16,640]{3,2,1,0:T(8,128)S(1)}, u32[]{:S(2)}, u32[]{:S(2)}) collective-permute-start(f32[4,2,16,640]{3,2,1,0:T(8,128)S(1)} %pad_maximum_fusion.1), channel_id=1, source_target_pairs={{0,1},{1,0},{2,3},{3,2},{4,5},{5,4},{6,7},{7,6},{8,9},{9,8},{10,11... | collective-permute-start | bytes 983048 | tf_op jit(solution)/shard_map/ppermute | solution.py:449
  192.9 5.7 %collective-permute-start.29 = (bf16[16,5120]{1,0:T(8,128)(2,1)S(1)}, bf16[16,5120]{1,0:T(8,128)(2,1)S(1)}, u32[]{:S(2)}, u32[]{:S(2)}) collective-permute-start(bf16[16,5120]{1,0:T(8,128)(2,1)S(1)} %get-tuple-element.176), channel_id=1, source_target_pairs={{0,6},{2,0},{4,2},{6,4},{1,7},{3,1},{5,3},{7,5},{8,14},{10,8},{12,... | collective-permute-start | bytes 491528 | tf_op jit(solution)/shard_map/ppermute | solution.py:572
  193.3 6.9 %collective-permute-start.30 = (bf16[16,5120]{1,0:T(8,128)(2,1)S(1)}, bf16[16,5120]{1,0:T(8,128)(2,1)S(1)}, u32[]{:S(2)}, u32[]{:S(2)}) collective-permute-start(bf16[16,5120]{1,0:T(8,128)(2,1)S(1)} %get-tuple-element.175), channel_id=1, source_target_pairs={{0,4},{2,6},{4,0},{6,2},{1,5},{3,7},{5,1},{7,3},{8,12},{10,14},{12... | collective-permute-start | bytes 491528 | tf_op jit(solution)/shard_map/ppermute | solution.py:572
  194.3 10.1 %collective-permute-start.31 = (bf16[16,5120]{1,0:T(8,128)(2,1)S(1)}, bf16[16,5120]{1,0:T(8,128)(2,1)S(1)}, u32[]{:S(2)}, u32[]{:S(2)}) collective-permute-start(bf16[16,5120]{1,0:T(8,128)(2,1)S(1)} %get-tuple-element.174), channel_id=1, source_target_pairs={{0,2},{2,4},{4,6},{6,0},{1,3},{3,5},{5,7},{7,1},{8,10},{10,12},{12... | collective-permute-start | bytes 491528 | tf_op jit(solution)/shard_map/ppermute | solution.py:572
  205.9 10.2 %collective-permute-start.32 = (bf16[16,5120]{1,0:T(8,128)(2,1)S(1)}, bf16[16,5120]{1,0:T(8,128)(2,1)S(1)}, u32[]{:S(2)}, u32[]{:S(2)}) collective-permute-start(bf16[16,5120]{1,0:T(8,128)(2,1)S(1)} %get-tuple-element.137), channel_id=1, source_target_pairs={{0,2},{2,4},{4,6},{6,0},{1,3},{3,5},{5,7},{7,1},{8,10},{10,12},{12... | collective-permute-start | bytes 491528 | tf_op jit(solution)/shard_map/ppermute | solution.py:485
  206.0 10.1 %collective-permute-start.33 = (bf16[16,5120]{1,0:T(8,128)(2,1)S(1)}, bf16[16,5120]{1,0:T(8,128)(2,1)S(1)}, u32[]{:S(2)}, u32[]{:S(2)}) collective-permute-start(bf16[16,5120]{1,0:T(8,128)(2,1)S(1)} %get-tuple-element.137), channel_id=1, source_target_pairs={{0,4},{2,6},{4,0},{6,2},{1,5},{3,7},{5,1},{7,3},{8,12},{10,14},{12... | collective-permute-start | bytes 491528 | tf_op jit(solution)/shard_map/ppermute | solution.py:485
  207.4 9.1 %collective-permute-start.34 = (bf16[16,5120]{1,0:T(8,128)(2,1)S(1)}, bf16[16,5120]{1,0:T(8,128)(2,1)S(1)}, u32[]{:S(2)}, u32[]{:S(2)}) collective-permute-start(bf16[16,5120]{1,0:T(8,128)(2,1)S(1)} %get-tuple-element.137), channel_id=1, source_target_pairs={{0,6},{2,0},{4,2},{6,4},{1,7},{3,1},{5,3},{7,5},{8,14},{10,8},{12,... | collective-permute-start | bytes 491528 | tf_op jit(solution)/shard_map/ppermute | solution.py:485
  216.5 10.2 %collective-permute-start.35 = (bf16[64,5120]{1,0:T(8,128)(2,1)S(1)}, bf16[64,5120]{1,0:T(8,128)(2,1)}, u32[]{:S(2)}, u32[]{:S(2)}) collective-permute-start(bf16[64,5120]{1,0:T(8,128)(2,1)S(1)} %constant_dynamic-update-slice_fusion.8.refs_5_), channel_id=1, source_target_pairs={{0,1},{1,0},{2,3},{3,2},{4,5},{5,4},{6,7},{7,6},{8,9},{9,8},{10,11... | collective-permute-start | bytes 1966088 | tf_op jit(solution)/shard_map/ppermute | solution.py:489
  218.1 18.1 %all-to-all-start.4 = ((f32[128,1,128]{2,1,0:T(1,128)}), f32[128,1,128]{2,1,0:T(1,128)S(1)}, u32[]{:S(2)}, u32[]{:S(2)}) async-start(f32[128,1,128]{2,1,0:T(1,128)} %get-tuple-element.136), calls=%async_computation.4 | async-start | bytes 131072 | tf_op jit(solution)/shard_map/all_to_all | solution.py:487
  237.8 19.3 %all-to-all-start.5 = ((bf16[16,128,256]{2,1,0:T(8,128)(2,1)}), bf16[16,128,256]{2,1,0:T(8,128)(2,1)S(1)}, u32[]{:S(2)}, u32[]{:S(2)}) async-start(bf16[16,128,256]{2,1,0:T(8,128)(2,1)} %get-tuple-element.142), calls=%async_computation.5 | async-start | bytes 2097152 | tf_op jit(solution)/shard_map/all_to_all | solution.py:540
  262.9 4.8 %collective-permute-start.36 = (bf16[64,5120]{1,0:T(8,128)(2,1)S(1)}, bf16[64,5120]{1,0:T(8,128)(2,1)S(1)}, u32[]{:S(2)}, u32[]{:S(2)}) collective-permute-start(bf16[64,5120]{1,0:T(8,128)(2,1)S(1)} %get-tuple-element.144), channel_id=1, source_target_pairs={{0,1},{1,0},{2,3},{3,2},{4,5},{5,4},{6,7},{7,6},{8,9},{9,8},{10,11... | collective-permute-start | bytes 1966088 | tf_op jit(solution)/shard_map/ppermute | solution.py:568
  267.9 6.1 %collective-permute-start.37 = (bf16[16,5120]{1,0:T(8,128)(2,1)S(1)}, bf16[16,5120]{1,0:T(8,128)(2,1)S(1)}, u32[]{:S(2)}, u32[]{:S(2)}) collective-permute-start(bf16[16,5120]{1,0:T(8,128)(2,1)S(1)} %get-tuple-element.173), channel_id=1, source_target_pairs={{0,6},{2,0},{4,2},{6,4},{1,7},{3,1},{5,3},{7,5},{8,14},{10,8},{12,... | collective-permute-start | bytes 491528 | tf_op jit(solution)/shard_map/ppermute | solution.py:572
  270.3 6.6 %collective-permute-start.38 = (bf16[16,5120]{1,0:T(8,128)(2,1)S(1)}, bf16[16,5120]{1,0:T(8,128)(2,1)S(1)}, u32[]{:S(2)}, u32[]{:S(2)}) collective-permute-start(bf16[16,5120]{1,0:T(8,128)(2,1)S(1)} %get-tuple-element.172), channel_id=1, source_target_pairs={{0,4},{2,6},{4,0},{6,2},{1,5},{3,7},{5,1},{7,3},{8,12},{10,14},{12... | collective-permute-start | bytes 491528 | tf_op jit(solution)/shard_map/ppermute | solution.py:572
  270.7 10.7 %collective-permute-start.39 = (bf16[16,5120]{1,0:T(8,128)(2,1)S(1)}, bf16[16,5120]{1,0:T(8,128)(2,1)S(1)}, u32[]{:S(2)}, u32[]{:S(2)}) collective-permute-start(bf16[16,5120]{1,0:T(8,128)(2,1)S(1)} %get-tuple-element.171), channel_id=1, source_target_pairs={{0,2},{2,4},{4,6},{6,0},{1,3},{3,5},{5,7},{7,1},{8,10},{10,12},{12... | collective-permute-start | bytes 491528 | tf_op jit(solution)/shard_map/ppermute | solution.py:572
  282.7 5.5 %collective-permute-start.42 = (f32[2,2,16,640]{3,2,1,0:T(8,128)}, f32[2,2,16,640]{3,2,1,0:T(8,128)S(1)}, u32[]{:S(2)}, u32[]{:S(2)}) collective-permute-start(f32[2,2,16,640]{3,2,1,0:T(8,128)} %get-tuple-element.161), channel_id=1, source_target_pairs={{0,6},{2,0},{4,2},{6,4},{1,7},{3,1},{5,3},{7,5},{8,14},{10,8},{12,... | collective-permute-start | bytes 491528 | tf_op jit(solution)/shard_map/ppermute | solution.py:447
  282.8 6.5 %collective-permute-start.41 = (f32[2,2,16,640]{3,2,1,0:T(8,128)}, f32[2,2,16,640]{3,2,1,0:T(8,128)S(1)}, u32[]{:S(2)}, u32[]{:S(2)}) collective-permute-start(f32[2,2,16,640]{3,2,1,0:T(8,128)} %get-tuple-element.160), channel_id=1, source_target_pairs={{0,4},{2,6},{4,0},{6,2},{1,5},{3,7},{5,1},{7,3},{8,12},{10,14},{12... | collective-permute-start | bytes 491528 | tf_op jit(solution)/shard_map/ppermute | solution.py:447
  283.3 10.9 %collective-permute-start.40 = (f32[2,2,16,640]{3,2,1,0:T(8,128)}, f32[2,2,16,640]{3,2,1,0:T(8,128)S(1)}, u32[]{:S(2)}, u32[]{:S(2)}) collective-permute-start(f32[2,2,16,640]{3,2,1,0:T(8,128)} %get-tuple-element.159), channel_id=1, source_target_pairs={{0,2},{2,4},{4,6},{6,0},{1,3},{3,5},{5,7},{7,1},{8,10},{10,12},{12... | collective-permute-start | bytes 491528 | tf_op jit(solution)/shard_map/ppermute | solution.py:447
  295.1 13.8 %collective-permute-start.43 = (f32[4,2,16,640]{3,2,1,0:T(8,128)S(1)}, f32[4,2,16,640]{3,2,1,0:T(8,128)S(1)}, u32[]{:S(2)}, u32[]{:S(2)}) collective-permute-start(f32[4,2,16,640]{3,2,1,0:T(8,128)S(1)} %pad_maximum_fusion.2), channel_id=1, source_target_pairs={{0,1},{1,0},{2,3},{3,2},{4,5},{5,4},{6,7},{7,6},{8,9},{9,8},{10,11... | collective-permute-start | bytes 983048 | tf_op jit(solution)/shard_map/ppermute | solution.py:449
  (18 other events, 202.4 us)

commit v4 on v3

--- a/solution.py
+++ b/solution.py
@@ -72,9 +72,13 @@
     return copies
 
 
-def first_kernel(wk_ref, wv_ref, gain_ref, *refs):
-    pieces, (rows_out, scale_ref, kv_ref, rows_ref, held, kv_held, sem) = refs[:2], refs[2:]
-    loads = load_keys(wk_ref, wv_ref, held, sem)
+def fetch_kernel(wk_ref, wv_ref, payload_ref, held, sem):
+    for load in load_keys(wk_ref, wv_ref, held, sem):
+        load.wait()
+
+
+def first_kernel(w_ref, gain_ref, *refs):
+    pieces, (rows_out, scale_ref, kv_ref, rows_ref, kv_held, sem) = refs[:2], refs[2:]
     y, c = lax.axis_index("y"), lax.axis_index("c")
     for half in range(2):
         for block in range(4):
@@ -92,9 +96,7 @@
         return squares + jnp.sum(part * part, axis=1, keepdims=True)
 
     squares = lax.fori_loop(0, 8, one_part, jnp.zeros((128, 1), F32))
-    for load in loads:
-        load.wait()
-    raw = jnp.dot(rows_ref[...], held[...], preferred_element_type=F32)
+    raw = jnp.dot(rows_ref[...], w_ref[...], preferred_element_type=F32)
     hand_out(raw, squares, scale_ref, kv_ref, kv_held, sem)
     keep.wait()
 
@@ -111,16 +113,18 @@
 
 
 def project_kernel(k, *refs):
-    (wk_ref, wv_ref, gain_ref), refs = refs[:3], refs[3:]
+    weights, refs = (refs[:2], refs[2:]) if k > 0 else (refs[:1], refs[1:])
+    gain_ref, refs = refs[0], refs[1:]
     older_hbm, pieces = refs[:k], refs[k : k + 2]
-    rows_out, raw_ref, *hand, rows_ref, held, sem, older_ref, older_sem = refs[k + 2 :]
+    rows_out, raw_ref, *hand, rows_ref, sem, older_ref, older_sem = refs[k + 2 :]
+    held = hand[-1] if k > 0 else weights[0]
     for n in range(8):
         for at in range(k):
             columns = slice(640 * n, 640 * n + 640)
             pltpu.make_async_copy(
                 older_hbm[at].at[:, columns], older_ref.at[at, :, columns], older_sem.at[at, n]
             ).start()
-    loads = load_keys(wk_ref, wv_ref, held, sem)
+    loads = load_keys(*weights, held, sem) if k > 0 else []
 
     def one_part(n, sums):
         at = pl.ds(pl.multiple_of(n * 640, 640), 640)
@@ -255,7 +259,7 @@
         send_ref[:, at] = part[64:].astype(BF16)
         return carry
 
-    lax.fori_loop(0, 4, one_part, 0)
+    lax.fori_loop(0, 4, one_part, 0, unroll=2)
 
 
 def home_copies(held, outs, at, sem, start):
@@ -477,7 +481,8 @@
     raw_out = pltpu.VMEM((128, 384), F32)
     hand_outs = [pltpu.VMEM((128, 128), F32), pltpu.HBM((16, 128, 2 * HEAD_DIM), BF16)]
     kv_scratch = pltpu.VMEM((128, 2 * HEAD_DIM), BF16)
-    project_scratch = [pltpu.VMEM((128, D), BF16), pltpu.VMEM((D, 2 * HEAD_DIM), BF16)]
+    rows_scratch = pltpu.VMEM((128, D), BF16)
+    key_scratch = pltpu.VMEM((D, 2 * HEAD_DIM), BF16)
     many = pltpu.SemaphoreType.DMA((19,))
     for k in range(ITERS):
         pieces = [payload]
@@ -485,6 +490,17 @@
             pieces.append(lax.ppermute(payload, "y", shift(4, by)))
         if dots is not None:
             tables.append(lax.all_to_all(dots, EVERY, split_axis=0, concat_axis=0, tiled=True))
+        if k < 2:
+            fetched = call(
+                fetch_kernel,
+                pltpu.VMEM((D, 2 * HEAD_DIM), BF16),
+                w_key,
+                w_value,
+                payload,
+                specs=[HBM, HBM, VMEM],
+                vmem=2,
+                scratch=[pltpu.SemaphoreType.DMA((2,))],
+            )
         mine = jnp.stack(pieces) if k == 0 else jnp.concatenate(pieces, axis=0)
         pieces = [mine, lax.ppermute(mine, "c", shift(2, 1))]
         if k == 1:
@@ -493,13 +509,11 @@
             rows, scale, kv = call(
                 first_kernel,
                 [rows_out, *hand_outs],
-                w_key,
-                w_value,
+                fetched,
                 gain_in,
                 *pieces,
-                specs=[HBM] * 2 + [VMEM] * 3,
                 vmem=8,
-                scratch=[*project_scratch, kv_scratch, many],
+                scratch=[rows_scratch, kv_scratch, many],
                 flops=2 * 128 * D * 256,
                 touched=4_000_000,
             )
@@ -507,16 +521,18 @@
             rows, raw, *hand = call(
                 functools.partial(project_kernel, k - 1),
                 [rows_out, raw_out] + (hand_outs if k == 1 else []),
-                w_key,
-                w_value,
+                *([fetched] if k == 1 else [w_key, w_value]),
                 gain_in,
                 *parts,
                 *pieces,
-                specs=[HBM] * 2 + [VMEM] + [HBM] * len(parts) + [VMEM] * 2,
+                specs=([VMEM] if k == 1 else [HBM] * 2)
+                + [VMEM]
+                + [HBM] * len(parts)
+                + [VMEM] * 2,
                 vmem=10,
-                scratch=([kv_scratch] if k == 1 else [])
-                + project_scratch
+                scratch=[kv_scratch if k == 1 else key_scratch]
                 + [
+                    rows_scratch,
                     many,
                     pltpu.VMEM((k - 1, 128, D) if k > 1 else (1, 8, 128), BF16),
                     pltpu.SemaphoreType.DMA((max(k - 1, 1), 8)),

time: 311 us -> 309 us (level)
    ppermute x4, waiting for transfers between devices: 3.45 us -> 0.01 us  [on_device(): pieces = [mine, lax.ppermute(mine, 'c', shift(2, 1))]]
    pallas_call x21 -> x23, Pallas kernels: 51.6 us -> 52.1 us  [call(): pl.pallas_call(kernel, out_shape=outs, in_specs=specs, input_output_alias...]
  transfers between devices with their start and end apart: 50 -> 50, of which waited for: 39 -> 37; matrix products, arithmetic and copies ran while one was open for 0% -> 0% of each run, Pallas kernels for 11% -> 12%
where the time goes in v4:
time: 309 us; the launch traced here: 308 us
  waiting for transfers between devices  135 us (44%)
  starting transfers between devices  77.8 us (25%)
  Pallas kernels  75.2 us (24%)
  blocking collectives  13.2 us (4%)
    pallas_call x23, Pallas kernels, call(): pl.pallas_call(kernel, out_shape=outs, in_specs=specs, input_output_alias...  52.1 us
    ppermute x12, waiting for transfers between devices, on_device(): arrived.append(lax.ppermute(piece, 'y', shift(4, -by)))  37.9 us
    ppermute x12, waiting for transfers between devices, on_device(): pieces.append(lax.ppermute(payload, 'y', shift(4, by)))  32.2 us
    ppermute x9, waiting for transfers between devices, move_home(): near.append(lax.ppermute(piece, 'y', shift(4, by + 1)))  26.2 us
    pallas_call x4, Pallas kernels, query_dot(): pl.pallas_call(functools.partial(query_kernel, len(parts) - 1), grid=(5,)...  23.1 us
    all_to_all x4, waiting for transfers between devices, on_device(): kv_all = lax.all_to_all(kv, SEQ, split_axis=0, concat_axis=0, tiled=True)  22 us
    all_to_all x4, starting transfers between devices, on_device(): kv_all = lax.all_to_all(kv, SEQ, split_axis=0, concat_axis=0, tiled=True)  18.6 us
    ppermute x12, starting transfers between devices, on_device(): pieces.append(lax.ppermute(payload, 'y', shift(4, by)))  13.7 us
  transfers between devices with their start and end apart: 50, of which 37 were waited for; matrix products, arithmetic and copies ran while one was open for 0% of the time, Pallas kernels for 12%

profile of v4, /device:TPU:1, one launch (start us, length us, event | category | flops | bytes accessed | tf_op | source)
XLA Modules:
  0.0 307.5 jit_solution(11577746019487960905)
XLA Ops:
  1.1 3.6 %collective-permute-start.2 = (bf16[128,640]{1,0:T(8,128)(2,1)S(1)}, bf16[128,640]{1,0:T(8,128)(2,1)S(1)}, u32[]{:S(2)}, u32[]{:S(2)}) collective-permute-start(bf16[128,640]{1,0:T(8,128)(2,1)S(1)} %get-tuple-element.84.payload_ref), channel_id=1, source_target_pairs={{0,6},{2,0},{4,2},{6,4},{1,7},{3,1},{5,3},{7,5},{8,14},{10,8},{12,... | collective-permute-start | bytes 491528 | tf_op jit(solution)/shard_map/ppermute | solution.py:490
  5.8 5.4 %collective-permute-done.2 = bf16[128,640]{1,0:T(8,128)(2,1)S(1)} collective-permute-done((bf16[128,640]{1,0:T(8,128)(2,1)S(1)}, bf16[128,640]{1,0:T(8,128)(2,1)S(1)}, u32[]{:S(2)}, u32[]{:S(2)}) %collective-permute-start.2) | collective-permute-done | bytes 163872 | tf_op jit(solution)/shard_map/ppermute | solution.py:490
  11.2 4.7 %collective-permute-done = bf16[128,640]{1,0:T(8,128)(2,1)S(1)} collective-permute-done((bf16[128,640]{1,0:T(8,128)(2,1)S(1)}, bf16[128,640]{1,0:T(8,128)(2,1)S(1)}, u32[]{:S(2)}, u32[]{:S(2)}) %collective-permute-start) | collective-permute-done | bytes 163872 | tf_op jit(solution)/shard_map/ppermute | solution.py:490
  18.3 2.9 shard_map.84
  21.2 7.6 %all-to-all-start = ((bf16[16,128,256]{2,1,0:T(8,128)(2,1)}), bf16[16,128,256]{2,1,0:T(8,128)(2,1)S(1)}, u32[]{:S(2)}, u32[]{:S(2)}) async-start(bf16[16,128,256]{2,1,0:T(8,128)(2,1)} %get-tuple-element.87), calls=%async_computation | async-start | bytes 2097152 | tf_op jit(solution)/shard_map/all_to_all | solution.py:556
  37.5 5.5 %shard_map.85.q_ref = bf16[128,640]{1,0:T(8,128)(2,1)S(1)} custom-call(bf16[128,5120]{1,0:T(8,128)(2,1)} %get-tuple-element.85.refs_0_, bf16[5120,640]{1,0:T(8,128)(2,1)} %refs_4_.1), custom_call_target="tpu_custom_call" | custom-call | flops 838860800 | bytes 8000000 | tf_op jit(solution)/shard_map/pallas_call | solution.py:211
  44.6 5.5 %shard_map.86 = (f32[64,5120]{1,0:T(8,128)S(1)}, bf16[64,5120]{1,0:T(8,128)(2,1)S(1)}) custom-call(bf16[128,640]{1,0:T(8,128)(2,1)S(1)} %shard_map.85.q_ref, f32[128,128]{1,0:T(8,128)S(1)} %get-tuple-element.86.scale_ref, bf16[16,128,256]{2,1,0:T(8,128)(2,1)S(1)} %all-to-all-done.kv_ref, bf16[640,5120]{1,0:T(8,128)(2,1)} %w_ref.7), custom_call_target="tpu_custom_call" | custom-call | flops 1509949440 | bytes 9000000 | tf_op jit(solution)/shard_map/pallas_call | solution.py:43
  50.1 3.1 %collective-permute-start.8 = (bf16[64,5120]{1,0:T(8,128)(2,1)S(1)}, bf16[64,5120]{1,0:T(8,128)(2,1)S(1)}, u32[]{:S(2)}, u32[]{:S(2)}) collective-permute-start(bf16[64,5120]{1,0:T(8,128)(2,1)S(1)} %get-tuple-element.95), channel_id=1, source_target_pairs={{0,1},{1,0},{2,3},{3,2},{4,5},{5,4},{6,7},{7,6},{8,9},{9,8},{10,11... | collective-permute-start | bytes 1966088 | tf_op jit(solution)/shard_map/ppermute | solution.py:584
  56.8 3.8 %collective-permute-done.9.a_ref = bf16[16,5120]{1,0:T(8,128)(2,1)S(1)} collective-permute-done((bf16[16,5120]{1,0:T(8,128)(2,1)S(1)}, bf16[16,5120]{1,0:T(8,128)(2,1)S(1)}, u32[]{:S(2)}, u32[]{:S(2)}) %collective-permute-start.9) | collective-permute-done | bytes 163872 | tf_op jit(solution)/shard_map/ppermute | solution.py:588
  62.2 4.5 %collective-permute-done.11.d_ref = bf16[16,5120]{1,0:T(8,128)(2,1)S(1)} collective-permute-done((bf16[16,5120]{1,0:T(8,128)(2,1)S(1)}, bf16[16,5120]{1,0:T(8,128)(2,1)S(1)}, u32[]{:S(2)}, u32[]{:S(2)}) %collective-permute-start.11) | collective-permute-done | bytes 163872 | tf_op jit(solution)/shard_map/ppermute | solution.py:588
  69.9 7.4 %collective-permute-done.12 = bf16[16,5120]{1,0:T(8,128)(2,1)S(1)} collective-permute-done((bf16[16,5120]{1,0:T(8,128)(2,1)S(1)}, bf16[16,5120]{1,0:T(8,128)(2,1)S(1)}, u32[]{:S(2)}, u32[]{:S(2)}) %collective-permute-start.12) | collective-permute-done | bytes 163872 | tf_op jit(solution)/shard_map/ppermute | solution.py:490
  80.9 2.8 shard_map.90
  83.8 3.7 %all-to-all-start.1 = ((bf16[16,128,256]{2,1,0:T(8,128)(2,1)}), bf16[16,128,256]{2,1,0:T(8,128)(2,1)S(1)}, u32[]{:S(2)}, u32[]{:S(2)}) async-start(bf16[16,128,256]{2,1,0:T(8,128)(2,1)} %get-tuple-element.106), calls=%async_computation.1 | async-start | bytes 2097152 | tf_op jit(solution)/shard_map/all_to_all | solution.py:556
  87.5 5.5 %shard_map.91.q_ref = bf16[128,640]{1,0:T(8,128)(2,1)S(1)} custom-call(bf16[128,5120]{1,0:T(8,128)(2,1)} %get-tuple-element.104.refs_0_.refs_3_.refs_1_, bf16[5120,640]{1,0:T(8,128)(2,1)} %refs_4_.1), custom_call_target="tpu_custom_call" | custom-call | flops 838860800 | bytes 8000000 | tf_op jit(solution)/shard_map/pallas_call | solution.py:211
  93.0 11.0 %all-to-all-done.1.kv_ref = bf16[16,128,256]{2,1,0:T(8,128)(2,1)S(1)} async-done(((bf16[16,128,256]{2,1,0:T(8,128)(2,1)}), bf16[16,128,256]{2,1,0:T(8,128)(2,1)S(1)}, u32[]{:S(2)}, u32[]{:S(2)}) %all-to-all-start.1) | async-done | bytes 1048608 | tf_op jit(solution)/shard_map/all_to_all | solution.py:556
  103.9 5.5 %shard_map.92 = (f32[64,5120]{1,0:T(8,128)S(1)}, bf16[64,5120]{1,0:T(8,128)(2,1)S(1)}) custom-call(bf16[128,640]{1,0:T(8,128)(2,1)S(1)} %shard_map.91.q_ref, f32[128,128]{1,0:T(8,128)S(1)} %get-tuple-element.105.scale_ref, bf16[16,128,256]{2,1,0:T(8,128)(2,1)S(1)} %all-to-all-done.1.kv_ref, bf16[640,5120]{1,0:T(8,128)(2,1)} %w_ref.7), custom_call_target="tpu_custom_call" | custom-call | flops 1509949440 | bytes 9000000 | tf_op jit(solution)/shard_map/pallas_call | solution.py:43
  109.4 2.3 collective-permute-start.16
  113.7 2.4 collective-permute-start.17
  119.7 3.1 collective-permute-done.18.b_ref
  122.8 3.9 %collective-permute-done.19.d_ref = bf16[16,5120]{1,0:T(8,128)(2,1)S(1)} collective-permute-done((bf16[16,5120]{1,0:T(8,128)(2,1)S(1)}, bf16[16,5120]{1,0:T(8,128)(2,1)S(1)}, u32[]{:S(2)}, u32[]{:S(2)}) %collective-permute-start.19) | collective-permute-done | bytes 163872 | tf_op jit(solution)/shard_map/ppermute | solution.py:588
  132.7 7.3 %collective-permute-done.20 = bf16[16,5120]{1,0:T(8,128)(2,1)S(1)} collective-permute-done((bf16[16,5120]{1,0:T(8,128)(2,1)S(1)}, bf16[16,5120]{1,0:T(8,128)(2,1)S(1)}, u32[]{:S(2)}, u32[]{:S(2)}) %collective-permute-start.20) | collective-permute-done | bytes 163872 | tf_op jit(solution)/shard_map/ppermute | solution.py:490
  142.0 5.0 %all-to-all-start.2 = ((f32[128,1,128]{2,1,0:T(1,128)}), f32[128,1,128]{2,1,0:T(1,128)S(1)}, u32[]{:S(2)}, u32[]{:S(2)}) async-start(f32[128,1,128]{2,1,0:T(1,128)} %get-tuple-element.112), calls=%async_computation.2 | async-start | bytes 131072 | tf_op jit(solution)/shard_map/all_to_all | solution.py:492
  147.0 3.6 %shard_map.95 = (bf16[128,5120]{1,0:T(8,128)(2,1)}, f32[128,384]{1,0:T(8,128)S(1)}) custom-call(bf16[5120,128]{1,0:T(8,128)(2,1)} %refs_0_.3, bf16[5120,128]{1,0:T(8,128)(2,1)} %refs_1_.7, f32[1,5120]{1,0:T(1,128)S(1)} %bitcast.14, bf16[128,5120]{1,0:T(8,128)(2,1)} %get-tuple-element.104.refs_0_.refs_3_.refs_1_, ...), custom_call_target="tpu_custom_call" | custom-call | flops 335544320 | bytes 4000000 | tf_op jit(solution)/shard_map/pallas_call | solution.py:43
  150.5 5.9 %all-to-all-done.2.refs_0_ = f32[128,1,128]{2,1,0:T(1,128)S(1)} async-done(((f32[128,1,128]{2,1,0:T(1,128)}), f32[128,1,128]{2,1,0:T(1,128)S(1)}, u32[]{:S(2)}, u32[]{:S(2)}) %all-to-all-start.2) | async-done | bytes 65568 | tf_op jit(solution)/shard_map/all_to_all | solution.py:492
  157.9 3.7 %all-to-all-start.3 = ((bf16[16,128,256]{2,1,0:T(8,128)(2,1)}), bf16[16,128,256]{2,1,0:T(8,128)(2,1)S(1)}, u32[]{:S(2)}, u32[]{:S(2)}) async-start(bf16[16,128,256]{2,1,0:T(8,128)(2,1)} %get-tuple-element.119), calls=%async_computation.3 | async-start | bytes 2097152 | tf_op jit(solution)/shard_map/all_to_all | solution.py:556
  164.8 3.0 collective-permute-done.26.refs_6_
  167.8 2.6 collective-permute-done.25.refs_5_
  170.4 4.6 %collective-permute-done.24.refs_4_ = f32[2,2,16,640]{3,2,1,0:T(8,128)S(1)} collective-permute-done((f32[2,2,16,640]{3,2,1,0:T(8,128)}, f32[2,2,16,640]{3,2,1,0:T(8,128)S(1)}, u32[]{:S(2)}, u32[]{:S(2)}) %collective-permute-start.24) | collective-permute-done | bytes 163872 | tf_op jit(solution)/shard_map/ppermute | solution.py:451
  176.7 5.9 %shard_map.97.q_ref = bf16[128,640]{1,0:T(8,128)(2,1)S(1)} custom-call(f32[1,128]{1,0:T(1,128)S(1)} %get-tuple-element.116.refs_0_.share_ref, bf16[128,5120]{1,0:T(8,128)(2,1)} %get-tuple-element.104.refs_0_.refs_3_.refs_1_, bf16[128,5120]{1,0:T(8,128)(2,1)} %get-tuple-element.117.refs_2_.refs_4_, bf16[5120,640]{1,0:T(8,128)(2,1)} %refs_4_.1), custom_call_target="tpu_custom_call" | custom-call | flops 838860800 | bytes 8000000 | tf_op jit(solution)/shard_map/pallas_call | solution.py:211
  182.7 5.5 %shard_map.99 = (f32[64,5120]{1,0:T(8,128)S(1)}, bf16[64,5120]{1,0:T(8,128)(2,1)S(1)}) custom-call(bf16[128,640]{1,0:T(8,128)(2,1)S(1)} %shard_map.97.q_ref, f32[128,128]{1,0:T(8,128)S(1)} %get-tuple-element.118.scale_ref, bf16[16,128,256]{2,1,0:T(8,128)(2,1)S(1)} %all-to-all-done.3.kv_ref, bf16[640,5120]{1,0:T(8,128)(2,1)} %w_ref.7), custom_call_target="tpu_custom_call" | custom-call | flops 1509949440 | bytes 9000000 | tf_op jit(solution)/shard_map/pallas_call | solution.py:43
  192.7 3.6 %collective-permute-done.29.a_ref = bf16[16,5120]{1,0:T(8,128)(2,1)S(1)} collective-permute-done((bf16[16,5120]{1,0:T(8,128)(2,1)S(1)}, bf16[16,5120]{1,0:T(8,128)(2,1)S(1)}, u32[]{:S(2)}, u32[]{:S(2)}) %collective-permute-start.29) | collective-permute-done | bytes 163872 | tf_op jit(solution)/shard_map/ppermute | solution.py:588
  197.8 4.2 %collective-permute-done.31.d_ref = bf16[16,5120]{1,0:T(8,128)(2,1)S(1)} collective-permute-done((bf16[16,5120]{1,0:T(8,128)(2,1)S(1)}, bf16[16,5120]{1,0:T(8,128)(2,1)S(1)}, u32[]{:S(2)}, u32[]{:S(2)}) %collective-permute-start.31) | collective-permute-done | bytes 163872 | tf_op jit(solution)/shard_map/ppermute | solution.py:588
  206.8 6.9 %collective-permute-done.32 = bf16[16,5120]{1,0:T(8,128)(2,1)S(1)} collective-permute-done((bf16[16,5120]{1,0:T(8,128)(2,1)S(1)}, bf16[16,5120]{1,0:T(8,128)(2,1)S(1)}, u32[]{:S(2)}, u32[]{:S(2)}) %collective-permute-start.32) | collective-permute-done | bytes 163872 | tf_op jit(solution)/shard_map/ppermute | solution.py:490
  215.8 8.5 %all-to-all-start.4 = ((f32[128,1,128]{2,1,0:T(1,128)}), f32[128,1,128]{2,1,0:T(1,128)S(1)}, u32[]{:S(2)}, u32[]{:S(2)}) async-start(f32[128,1,128]{2,1,0:T(1,128)} %get-tuple-element.136), calls=%async_computation.4 | async-start | bytes 131072 | tf_op jit(solution)/shard_map/all_to_all | solution.py:492
  224.3 5.7 %shard_map.102 = (bf16[128,5120]{1,0:T(8,128)(2,1)}, f32[128,384]{1,0:T(8,128)S(1)}) custom-call(bf16[5120,128]{1,0:T(8,128)(2,1)} %refs_0_.3, bf16[5120,128]{1,0:T(8,128)(2,1)} %refs_1_.7, f32[1,5120]{1,0:T(1,128)S(1)} %bitcast.16, bf16[128,5120]{1,0:T(8,128)(2,1)} %get-tuple-element.104.refs_0_.refs_3_.refs_1_, ...), custom_call_target="tpu_custom_call" | custom-call | flops 335544320 | bytes 4000000 | tf_op jit(solution)/shard_map/pallas_call | solution.py:43
  230.0 3.8 %all-to-all-done.4.refs_1_ = f32[128,1,128]{2,1,0:T(1,128)S(1)} async-done(((f32[128,1,128]{2,1,0:T(1,128)}), f32[128,1,128]{2,1,0:T(1,128)S(1)}, u32[]{:S(2)}, u32[]{:S(2)}) %all-to-all-start.4) | async-done | bytes 65568 | tf_op jit(solution)/shard_map/all_to_all | solution.py:492
  235.4 3.7 %all-to-all-start.5 = ((bf16[16,128,256]{2,1,0:T(8,128)(2,1)}), bf16[16,128,256]{2,1,0:T(8,128)(2,1)S(1)}, u32[]{:S(2)}, u32[]{:S(2)}) async-start(bf16[16,128,256]{2,1,0:T(8,128)(2,1)} %get-tuple-element.142), calls=%async_computation.5 | async-start | bytes 2097152 | tf_op jit(solution)/shard_map/all_to_all | solution.py:556
  239.1 6.2 %shard_map.104.q_ref = bf16[128,640]{1,0:T(8,128)(2,1)S(1)} custom-call(f32[1,128]{1,0:T(1,128)S(1)} %get-tuple-element.139.refs_0_.share_ref, bf16[128,5120]{1,0:T(8,128)(2,1)} %get-tuple-element.104.refs_0_.refs_3_.refs_1_, bf16[128,5120]{1,0:T(8,128)(2,1)} %get-tuple-element.117.refs_2_.refs_4_, bf16[128,5120]{1,0:T(8,128)(2,1)} %get-tuple-element.140.refs_3_, ...), custom_call_target="tpu_custom_call" | custom-call | flops 838860800 | bytes 8000000 | tf_op jit(solution)/shard_map/pallas_call | solution.py:211
  245.3 9.4 %all-to-all-done.5.kv_ref = bf16[16,128,256]{2,1,0:T(8,128)(2,1)S(1)} async-done(((bf16[16,128,256]{2,1,0:T(8,128)(2,1)}), bf16[16,128,256]{2,1,0:T(8,128)(2,1)S(1)}, u32[]{:S(2)}, u32[]{:S(2)}) %all-to-all-start.5) | async-done | bytes 1048608 | tf_op jit(solution)/shard_map/all_to_all | solution.py:556
  254.8 5.4 %shard_map.105 = (f32[64,5120]{1,0:T(8,128)S(1)}, bf16[64,5120]{1,0:T(8,128)(2,1)S(1)}) custom-call(bf16[128,640]{1,0:T(8,128)(2,1)S(1)} %shard_map.104.q_ref, f32[128,128]{1,0:T(8,128)S(1)} %get-tuple-element.141.scale_ref, bf16[16,128,256]{2,1,0:T(8,128)(2,1)S(1)} %all-to-all-done.5.kv_ref, bf16[640,5120]{1,0:T(8,128)(2,1)} %w_ref.7), custom_call_target="tpu_custom_call" | custom-call | flops 1509949440 | bytes 9000000 | tf_op jit(solution)/shard_map/pallas_call | solution.py:43
  260.2 3.1 %collective-permute-start.36 = (bf16[64,5120]{1,0:T(8,128)(2,1)S(1)}, bf16[64,5120]{1,0:T(8,128)(2,1)S(1)}, u32[]{:S(2)}, u32[]{:S(2)}) collective-permute-start(bf16[64,5120]{1,0:T(8,128)(2,1)S(1)} %get-tuple-element.144), channel_id=1, source_target_pairs={{0,1},{1,0},{2,3},{3,2},{4,5},{5,4},{6,7},{7,6},{8,9},{9,8},{10,11... | collective-permute-start | bytes 1966088 | tf_op jit(solution)/shard_map/ppermute | solution.py:584
  265.2 2.4 collective-permute-start.37
  268.9 2.5 collective-permute-done.37.a_ref
  271.4 2.9 collective-permute-done.38.b_ref
  274.3 4.5 %collective-permute-done.39.d_ref = bf16[16,5120]{1,0:T(8,128)(2,1)S(1)} collective-permute-done((bf16[16,5120]{1,0:T(8,128)(2,1)S(1)}, bf16[16,5120]{1,0:T(8,128)(2,1)S(1)}, u32[]{:S(2)}, u32[]{:S(2)}) %collective-permute-start.39) | collective-permute-done | bytes 163872 | tf_op jit(solution)/shard_map/ppermute | solution.py:588
  281.6 4.0 %collective-permute-done.42.refs_11_ = f32[2,2,16,640]{3,2,1,0:T(8,128)S(1)} collective-permute-done((f32[2,2,16,640]{3,2,1,0:T(8,128)}, f32[2,2,16,640]{3,2,1,0:T(8,128)S(1)}, u32[]{:S(2)}, u32[]{:S(2)}) %collective-permute-start.42) | collective-permute-done | bytes 163872 | tf_op jit(solution)/shard_map/ppermute | solution.py:451
  286.7 4.9 %collective-permute-done.40.refs_9_ = f32[2,2,16,640]{3,2,1,0:T(8,128)S(1)} collective-permute-done((f32[2,2,16,640]{3,2,1,0:T(8,128)}, f32[2,2,16,640]{3,2,1,0:T(8,128)S(1)}, u32[]{:S(2)}, u32[]{:S(2)}) %collective-permute-start.40) | collective-permute-done | bytes 163872 | tf_op jit(solution)/shard_map/ppermute | solution.py:451
  293.0 13.2 %all_to_all.35.refs_2_ = f32[128,1,128]{2,1,0:T(1,128)S(1)} all-to-all(f32[128,1,128]{2,1,0:T(1,128)} %get-tuple-element.152), channel_id=1, replica_groups=mesh['x'=4,'z'=4,'y'=4,'c'=2] {'x','z','y','c'}, dimensions={0} | all-to-all | bytes 131072 | tf_op jit(solution)/shard_map/all_to_all | solution.py:642
  (149 shorter events, 70.5 us)
Async XLA Ops:
  1.1 10.1 %collective-permute-start.2 = (bf16[128,640]{1,0:T(8,128)(2,1)S(1)}, bf16[128,640]{1,0:T(8,128)(2,1)S(1)}, u32[]{:S(2)}, u32[]{:S(2)}) collective-permute-start(bf16[128,640]{1,0:T(8,128)(2,1)S(1)} %get-tuple-element.84.payload_ref), channel_id=1, source_target_pairs={{0,6},{2,0},{4,2},{6,4},{1,7},{3,1},{5,3},{7,5},{8,14},{10,8},{12,... | collective-permute-start | bytes 491528 | tf_op jit(solution)/shard_map/ppermute | solution.py:490
  4.7 6.4 %collective-permute-start.1 = (bf16[128,640]{1,0:T(8,128)(2,1)S(1)}, bf16[128,640]{1,0:T(8,128)(2,1)S(1)}, u32[]{:S(2)}, u32[]{:S(2)}) collective-permute-start(bf16[128,640]{1,0:T(8,128)(2,1)S(1)} %get-tuple-element.84.payload_ref), channel_id=1, source_target_pairs={{0,4},{2,6},{4,0},{6,2},{1,5},{3,7},{5,1},{7,3},{8,12},{10,14},{12... | collective-permute-start | bytes 491528 | tf_op jit(solution)/shard_map/ppermute | solution.py:490
  5.1 10.8 %collective-permute-start = (bf16[128,640]{1,0:T(8,128)(2,1)S(1)}, bf16[128,640]{1,0:T(8,128)(2,1)S(1)}, u32[]{:S(2)}, u32[]{:S(2)}) collective-permute-start(bf16[128,640]{1,0:T(8,128)(2,1)S(1)} %get-tuple-element.84.payload_ref), channel_id=1, source_target_pairs={{0,2},{2,4},{4,6},{6,0},{1,3},{3,5},{5,7},{7,1},{8,10},{10,12},{12... | collective-permute-start | bytes 491528 | tf_op jit(solution)/shard_map/ppermute | solution.py:490
  21.2 23.3 %all-to-all-start = ((bf16[16,128,256]{2,1,0:T(8,128)(2,1)}), bf16[16,128,256]{2,1,0:T(8,128)(2,1)S(1)}, u32[]{:S(2)}, u32[]{:S(2)}) async-start(bf16[16,128,256]{2,1,0:T(8,128)(2,1)} %get-tuple-element.87), calls=%async_computation | async-start | bytes 2097152 | tf_op jit(solution)/shard_map/all_to_all | solution.py:556
  28.9 3.4 %collective-permute-start.6 = (bf16[2,2,16,640]{3,2,1,0:T(8,128)(2,1)S(1)}, bf16[2,2,16,640]{3,2,1,0:T(8,128)(2,1)S(1)}, u32[]{:S(2)}, u32[]{:S(2)}) collective-permute-start(bf16[2,2,16,640]{3,2,1,0:T(8,128)(2,1)S(1)} %get-tuple-element.91), channel_id=1, source_target_pairs={{0,6},{2,0},{4,2},{6,4},{1,7},{3,1},{5,3},{7,5},{8,14},{10,8},{12,... | collective-permute-start | bytes 245768 | tf_op jit(solution)/shard_map/ppermute | solution.py:451
  29.2 5.1 %collective-permute-start.5 = (bf16[2,2,16,640]{3,2,1,0:T(8,128)(2,1)S(1)}, bf16[2,2,16,640]{3,2,1,0:T(8,128)(2,1)S(1)}, u32[]{:S(2)}, u32[]{:S(2)}) collective-permute-start(bf16[2,2,16,640]{3,2,1,0:T(8,128)(2,1)S(1)} %get-tuple-element.90), channel_id=1, source_target_pairs={{0,4},{2,6},{4,0},{6,2},{1,5},{3,7},{5,1},{7,3},{8,12},{10,14},{12... | collective-permute-start | bytes 245768 | tf_op jit(solution)/shard_map/ppermute | solution.py:451
  29.6 6.9 %collective-permute-start.4 = (bf16[2,2,16,640]{3,2,1,0:T(8,128)(2,1)S(1)}, bf16[2,2,16,640]{3,2,1,0:T(8,128)(2,1)S(1)}, u32[]{:S(2)}, u32[]{:S(2)}) collective-permute-start(bf16[2,2,16,640]{3,2,1,0:T(8,128)(2,1)S(1)} %get-tuple-element.89), channel_id=1, source_target_pairs={{0,2},{2,4},{4,6},{6,0},{1,3},{3,5},{5,7},{7,1},{8,10},{10,12},{12... | collective-permute-start | bytes 245768 | tf_op jit(solution)/shard_map/ppermute | solution.py:451
  36.5 6.5 %collective-permute-start.7 = (bf16[4,2,16,640]{3,2,1,0:T(8,128)(2,1)S(1)}, bf16[4,2,16,640]{3,2,1,0:T(8,128)(2,1)S(1)}, u32[]{:S(2)}, u32[]{:S(2)}) collective-permute-start(bf16[4,2,16,640]{3,2,1,0:T(8,128)(2,1)S(1)} %pad_maximum_fusion.3), channel_id=1, source_target_pairs={{0,1},{1,0},{2,3},{3,2},{4,5},{5,4},{6,7},{7,6},{8,9},{9,8},{10,11... | collective-permute-start | bytes 491528 | tf_op jit(solution)/shard_map/ppermute | solution.py:453
  50.1 4.8 %collective-permute-start.8 = (bf16[64,5120]{1,0:T(8,128)(2,1)S(1)}, bf16[64,5120]{1,0:T(8,128)(2,1)S(1)}, u32[]{:S(2)}, u32[]{:S(2)}) collective-permute-start(bf16[64,5120]{1,0:T(8,128)(2,1)S(1)} %get-tuple-element.95), channel_id=1, source_target_pairs={{0,1},{1,0},{2,3},{3,2},{4,5},{5,4},{6,7},{7,6},{8,9},{9,8},{10,11... | collective-permute-start | bytes 1966088 | tf_op jit(solution)/shard_map/ppermute | solution.py:584
  55.1 5.5 %collective-permute-start.9 = (bf16[16,5120]{1,0:T(8,128)(2,1)S(1)}, bf16[16,5120]{1,0:T(8,128)(2,1)S(1)}, u32[]{:S(2)}, u32[]{:S(2)}) collective-permute-start(bf16[16,5120]{1,0:T(8,128)(2,1)S(1)} %get-tuple-element.182), channel_id=1, source_target_pairs={{0,6},{2,0},{4,2},{6,4},{1,7},{3,1},{5,3},{7,5},{8,14},{10,8},{12,... | collective-permute-start | bytes 491528 | tf_op jit(solution)/shard_map/ppermute | solution.py:588
  55.5 6.6 %collective-permute-start.10 = (bf16[16,5120]{1,0:T(8,128)(2,1)S(1)}, bf16[16,5120]{1,0:T(8,128)(2,1)S(1)}, u32[]{:S(2)}, u32[]{:S(2)}) collective-permute-start(bf16[16,5120]{1,0:T(8,128)(2,1)S(1)} %get-tuple-element.181), channel_id=1, source_target_pairs={{0,4},{2,6},{4,0},{6,2},{1,5},{3,7},{5,1},{7,3},{8,12},{10,14},{12... | collective-permute-start | bytes 491528 | tf_op jit(solution)/shard_map/ppermute | solution.py:588
  55.8 10.8 %collective-permute-start.11 = (bf16[16,5120]{1,0:T(8,128)(2,1)S(1)}, bf16[16,5120]{1,0:T(8,128)(2,1)S(1)}, u32[]{:S(2)}, u32[]{:S(2)}) collective-permute-start(bf16[16,5120]{1,0:T(8,128)(2,1)S(1)} %get-tuple-element.180), channel_id=1, source_target_pairs={{0,2},{2,4},{4,6},{6,0},{1,3},{3,5},{5,7},{7,1},{8,10},{10,12},{12... | collective-permute-start | bytes 491528 | tf_op jit(solution)/shard_map/ppermute | solution.py:588
  67.0 10.3 %collective-permute-start.12 = (bf16[16,5120]{1,0:T(8,128)(2,1)S(1)}, bf16[16,5120]{1,0:T(8,128)(2,1)S(1)}, u32[]{:S(2)}, u32[]{:S(2)}) collective-permute-start(bf16[16,5120]{1,0:T(8,128)(2,1)S(1)} %get-tuple-element.103.payload_ref), channel_id=1, source_target_pairs={{0,2},{2,4},{4,6},{6,0},{1,3},{3,5},{5,7},{7,1},{8,10},{10,12},{12... | collective-permute-start | bytes 491528 | tf_op jit(solution)/shard_map/ppermute | solution.py:490
  67.1 10.2 %collective-permute-start.13 = (bf16[16,5120]{1,0:T(8,128)(2,1)S(1)}, bf16[16,5120]{1,0:T(8,128)(2,1)S(1)}, u32[]{:S(2)}, u32[]{:S(2)}) collective-permute-start(bf16[16,5120]{1,0:T(8,128)(2,1)S(1)} %get-tuple-element.103.payload_ref), channel_id=1, source_target_pairs={{0,4},{2,6},{4,0},{6,2},{1,5},{3,7},{5,1},{7,3},{8,12},{10,14},{12... | collective-permute-start | bytes 491528 | tf_op jit(solution)/shard_map/ppermute | solution.py:490
  68.2 9.4 %collective-permute-start.14 = (bf16[16,5120]{1,0:T(8,128)(2,1)S(1)}, bf16[16,5120]{1,0:T(8,128)(2,1)S(1)}, u32[]{:S(2)}, u32[]{:S(2)}) collective-permute-start(bf16[16,5120]{1,0:T(8,128)(2,1)S(1)} %get-tuple-element.103.payload_ref), channel_id=1, source_target_pairs={{0,6},{2,0},{4,2},{6,4},{1,7},{3,1},{5,3},{7,5},{8,14},{10,8},{12,... | collective-permute-start | bytes 491528 | tf_op jit(solution)/shard_map/ppermute | solution.py:490
  77.5 3.4 %collective-permute-start.15 = (bf16[64,5120]{1,0:T(8,128)(2,1)S(1)}, bf16[64,5120]{1,0:T(8,128)(2,1)S(1)}, u32[]{:S(2)}, u32[]{:S(2)}) collective-permute-start(bf16[64,5120]{1,0:T(8,128)(2,1)S(1)} %constant_dynamic-update-slice_fusion.refs_2_), channel_id=1, source_target_pairs={{0,1},{1,0},{2,3},{3,2},{4,5},{5,4},{6,7},{7,6},{8,9},{9,8},{10,11... | collective-permute-start | bytes 1966088 | tf_op jit(solution)/shard_map/ppermute | solution.py:505
  83.8 20.1 %all-to-all-start.1 = ((bf16[16,128,256]{2,1,0:T(8,128)(2,1)}), bf16[16,128,256]{2,1,0:T(8,128)(2,1)S(1)}, u32[]{:S(2)}, u32[]{:S(2)}) async-start(bf16[16,128,256]{2,1,0:T(8,128)(2,1)} %get-tuple-element.106), calls=%async_computation.1 | async-start | bytes 2097152 | tf_op jit(solution)/shard_map/all_to_all | solution.py:556
  109.4 4.0 %collective-permute-start.16 = (bf16[64,5120]{1,0:T(8,128)(2,1)S(1)}, bf16[64,5120]{1,0:T(8,128)(2,1)S(1)}, u32[]{:S(2)}, u32[]{:S(2)}) collective-permute-start(bf16[64,5120]{1,0:T(8,128)(2,1)S(1)} %get-tuple-element.108), channel_id=1, source_target_pairs={{0,1},{1,0},{2,3},{3,2},{4,5},{5,4},{6,7},{7,6},{8,9},{9,8},{10,11... | collective-permute-start | bytes 1966088 | tf_op jit(solution)/shard_map/ppermute | solution.py:584
  113.7 6.0 %collective-permute-start.17 = (bf16[16,5120]{1,0:T(8,128)(2,1)S(1)}, bf16[16,5120]{1,0:T(8,128)(2,1)S(1)}, u32[]{:S(2)}, u32[]{:S(2)}) collective-permute-start(bf16[16,5120]{1,0:T(8,128)(2,1)S(1)} %get-tuple-element.179), channel_id=1, source_target_pairs={{0,6},{2,0},{4,2},{6,4},{1,7},{3,1},{5,3},{7,5},{8,14},{10,8},{12,... | collective-permute-start | bytes 491528 | tf_op jit(solution)/shard_map/ppermute | solution.py:588
  116.1 6.7 %collective-permute-start.18 = (bf16[16,5120]{1,0:T(8,128)(2,1)S(1)}, bf16[16,5120]{1,0:T(8,128)(2,1)S(1)}, u32[]{:S(2)}, u32[]{:S(2)}) collective-permute-start(bf16[16,5120]{1,0:T(8,128)(2,1)S(1)} %get-tuple-element.178), channel_id=1, source_target_pairs={{0,4},{2,6},{4,0},{6,2},{1,5},{3,7},{5,1},{7,3},{8,12},{10,14},{12... | collective-permute-start | bytes 491528 | tf_op jit(solution)/shard_map/ppermute | solution.py:588
  116.1 10.6 %collective-permute-start.19 = (bf16[16,5120]{1,0:T(8,128)(2,1)S(1)}, bf16[16,5120]{1,0:T(8,128)(2,1)S(1)}, u32[]{:S(2)}, u32[]{:S(2)}) collective-permute-start(bf16[16,5120]{1,0:T(8,128)(2,1)S(1)} %get-tuple-element.177), channel_id=1, source_target_pairs={{0,2},{2,4},{4,6},{6,0},{1,3},{3,5},{5,7},{7,1},{8,10},{10,12},{12... | collective-permute-start | bytes 491528 | tf_op jit(solution)/shard_map/ppermute | solution.py:588
  129.7 10.2 %collective-permute-start.20 = (bf16[16,5120]{1,0:T(8,128)(2,1)S(1)}, bf16[16,5120]{1,0:T(8,128)(2,1)S(1)}, u32[]{:S(2)}, u32[]{:S(2)}) collective-permute-start(bf16[16,5120]{1,0:T(8,128)(2,1)S(1)} %get-tuple-element.114), channel_id=1, source_target_pairs={{0,2},{2,4},{4,6},{6,0},{1,3},{3,5},{5,7},{7,1},{8,10},{10,12},{12... | collective-permute-start | bytes 491528 | tf_op jit(solution)/shard_map/ppermute | solution.py:490
  129.8 10.1 %collective-permute-start.21 = (bf16[16,5120]{1,0:T(8,128)(2,1)S(1)}, bf16[16,5120]{1,0:T(8,128)(2,1)S(1)}, u32[]{:S(2)}, u32[]{:S(2)}) collective-permute-start(bf16[16,5120]{1,0:T(8,128)(2,1)S(1)} %get-tuple-element.114), channel_id=1, source_target_pairs={{0,4},{2,6},{4,0},{6,2},{1,5},{3,7},{5,1},{7,3},{8,12},{10,14},{12... | collective-permute-start | bytes 491528 | tf_op jit(solution)/shard_map/ppermute | solution.py:490
  131.0 9.0 %collective-permute-start.22 = (bf16[16,5120]{1,0:T(8,128)(2,1)S(1)}, bf16[16,5120]{1,0:T(8,128)(2,1)S(1)}, u32[]{:S(2)}, u32[]{:S(2)}) collective-permute-start(bf16[16,5120]{1,0:T(8,128)(2,1)S(1)} %get-tuple-element.114), channel_id=1, source_target_pairs={{0,6},{2,0},{4,2},{6,4},{1,7},{3,1},{5,3},{7,5},{8,14},{10,8},{12,... | collective-permute-start | bytes 491528 | tf_op jit(solution)/shard_map/ppermute | solution.py:490
  140.0 6.9 %collective-permute-start.23 = (bf16[64,5120]{1,0:T(8,128)(2,1)S(1)}, bf16[64,5120]{1,0:T(8,128)(2,1)S(1)}, u32[]{:S(2)}, u32[]{:S(2)}) collective-permute-start(bf16[64,5120]{1,0:T(8,128)(2,1)S(1)} %constant_dynamic-update-slice_fusion.4.refs_4_), channel_id=1, source_target_pairs={{0,1},{1,0},{2,3},{3,2},{4,5},{5,4},{6,7},{7,6},{8,9},{9,8},{10,11... | collective-permute-start | bytes 1966088 | tf_op jit(solution)/shard_map/ppermute | solution.py:505
  142.0 14.5 %all-to-all-start.2 = ((f32[128,1,128]{2,1,0:T(1,128)}), f32[128,1,128]{2,1,0:T(1,128)S(1)}, u32[]{:S(2)}, u32[]{:S(2)}) async-start(f32[128,1,128]{2,1,0:T(1,128)} %get-tuple-element.112), calls=%async_computation.2 | async-start | bytes 131072 | tf_op jit(solution)/shard_map/all_to_all | solution.py:492
  157.9 24.7 %all-to-all-start.3 = ((bf16[16,128,256]{2,1,0:T(8,128)(2,1)}), bf16[16,128,256]{2,1,0:T(8,128)(2,1)S(1)}, u32[]{:S(2)}, u32[]{:S(2)}) async-start(bf16[16,128,256]{2,1,0:T(8,128)(2,1)} %get-tuple-element.119), calls=%async_computation.3 | async-start | bytes 2097152 | tf_op jit(solution)/shard_map/all_to_all | solution.py:556
  162.7 5.2 %collective-permute-start.26 = (f32[2,2,16,640]{3,2,1,0:T(8,128)}, f32[2,2,16,640]{3,2,1,0:T(8,128)S(1)}, u32[]{:S(2)}, u32[]{:S(2)}) collective-permute-start(f32[2,2,16,640]{3,2,1,0:T(8,128)} %get-tuple-element.129), channel_id=1, source_target_pairs={{0,6},{2,0},{4,2},{6,4},{1,7},{3,1},{5,3},{7,5},{8,14},{10,8},{12,... | collective-permute-start | bytes 491528 | tf_op jit(solution)/shard_map/ppermute | solution.py:451
  163.8 6.6 %collective-permute-start.25 = (f32[2,2,16,640]{3,2,1,0:T(8,128)}, f32[2,2,16,640]{3,2,1,0:T(8,128)S(1)}, u32[]{:S(2)}, u32[]{:S(2)}) collective-permute-start(f32[2,2,16,640]{3,2,1,0:T(8,128)} %get-tuple-element.128), channel_id=1, source_target_pairs={{0,4},{2,6},{4,0},{6,2},{1,5},{3,7},{5,1},{7,3},{8,12},{10,14},{12... | collective-permute-start | bytes 491528 | tf_op jit(solution)/shard_map/ppermute | solution.py:451
  164.8 10.2 %collective-permute-start.24 = (f32[2,2,16,640]{3,2,1,0:T(8,128)}, f32[2,2,16,640]{3,2,1,0:T(8,128)S(1)}, u32[]{:S(2)}, u32[]{:S(2)}) collective-permute-start(f32[2,2,16,640]{3,2,1,0:T(8,128)} %get-tuple-element.127), channel_id=1, source_target_pairs={{0,2},{2,4},{4,6},{6,0},{1,3},{3,5},{5,7},{7,1},{8,10},{10,12},{12... | collective-permute-start | bytes 491528 | tf_op jit(solution)/shard_map/ppermute | solution.py:451
  176.1 6.6 %collective-permute-start.27 = (f32[4,2,16,640]{3,2,1,0:T(8,128)S(1)}, f32[4,2,16,640]{3,2,1,0:T(8,128)S(1)}, u32[]{:S(2)}, u32[]{:S(2)}) collective-permute-start(f32[4,2,16,640]{3,2,1,0:T(8,128)S(1)} %pad_maximum_fusion.1), channel_id=1, source_target_pairs={{0,1},{1,0},{2,3},{3,2},{4,5},{5,4},{6,7},{7,6},{8,9},{9,8},{10,11... | collective-permute-start | bytes 983048 | tf_op jit(solution)/shard_map/ppermute | solution.py:453
  190.6 5.7 %collective-permute-start.29 = (bf16[16,5120]{1,0:T(8,128)(2,1)S(1)}, bf16[16,5120]{1,0:T(8,128)(2,1)S(1)}, u32[]{:S(2)}, u32[]{:S(2)}) collective-permute-start(bf16[16,5120]{1,0:T(8,128)(2,1)S(1)} %get-tuple-element.176), channel_id=1, source_target_pairs={{0,6},{2,0},{4,2},{6,4},{1,7},{3,1},{5,3},{7,5},{8,14},{10,8},{12,... | collective-permute-start | bytes 491528 | tf_op jit(solution)/shard_map/ppermute | solution.py:588
  190.9 6.9 %collective-permute-start.30 = (bf16[16,5120]{1,0:T(8,128)(2,1)S(1)}, bf16[16,5120]{1,0:T(8,128)(2,1)S(1)}, u32[]{:S(2)}, u32[]{:S(2)}) collective-permute-start(bf16[16,5120]{1,0:T(8,128)(2,1)S(1)} %get-tuple-element.175), channel_id=1, source_target_pairs={{0,4},{2,6},{4,0},{6,2},{1,5},{3,7},{5,1},{7,3},{8,12},{10,14},{12... | collective-permute-start | bytes 491528 | tf_op jit(solution)/shard_map/ppermute | solution.py:588
  191.9 10.1 %collective-permute-start.31 = (bf16[16,5120]{1,0:T(8,128)(2,1)S(1)}, bf16[16,5120]{1,0:T(8,128)(2,1)S(1)}, u32[]{:S(2)}, u32[]{:S(2)}) collective-permute-start(bf16[16,5120]{1,0:T(8,128)(2,1)S(1)} %get-tuple-element.174), channel_id=1, source_target_pairs={{0,2},{2,4},{4,6},{6,0},{1,3},{3,5},{5,7},{7,1},{8,10},{10,12},{12... | collective-permute-start | bytes 491528 | tf_op jit(solution)/shard_map/ppermute | solution.py:588
  203.5 10.2 %collective-permute-start.32 = (bf16[16,5120]{1,0:T(8,128)(2,1)S(1)}, bf16[16,5120]{1,0:T(8,128)(2,1)S(1)}, u32[]{:S(2)}, u32[]{:S(2)}) collective-permute-start(bf16[16,5120]{1,0:T(8,128)(2,1)S(1)} %get-tuple-element.137), channel_id=1, source_target_pairs={{0,2},{2,4},{4,6},{6,0},{1,3},{3,5},{5,7},{7,1},{8,10},{10,12},{12... | collective-permute-start | bytes 491528 | tf_op jit(solution)/shard_map/ppermute | solution.py:490
  203.6 10.1 %collective-permute-start.33 = (bf16[16,5120]{1,0:T(8,128)(2,1)S(1)}, bf16[16,5120]{1,0:T(8,128)(2,1)S(1)}, u32[]{:S(2)}, u32[]{:S(2)}) collective-permute-start(bf16[16,5120]{1,0:T(8,128)(2,1)S(1)} %get-tuple-element.137), channel_id=1, source_target_pairs={{0,4},{2,6},{4,0},{6,2},{1,5},{3,7},{5,1},{7,3},{8,12},{10,14},{12... | collective-permute-start | bytes 491528 | tf_op jit(solution)/shard_map/ppermute | solution.py:490
  205.0 9.1 %collective-permute-start.34 = (bf16[16,5120]{1,0:T(8,128)(2,1)S(1)}, bf16[16,5120]{1,0:T(8,128)(2,1)S(1)}, u32[]{:S(2)}, u32[]{:S(2)}) collective-permute-start(bf16[16,5120]{1,0:T(8,128)(2,1)S(1)} %get-tuple-element.137), channel_id=1, source_target_pairs={{0,6},{2,0},{4,2},{6,4},{1,7},{3,1},{5,3},{7,5},{8,14},{10,8},{12,... | collective-permute-start | bytes 491528 | tf_op jit(solution)/shard_map/ppermute | solution.py:490
  214.1 10.2 %collective-permute-start.35 = (bf16[64,5120]{1,0:T(8,128)(2,1)S(1)}, bf16[64,5120]{1,0:T(8,128)(2,1)}, u32[]{:S(2)}, u32[]{:S(2)}) collective-permute-start(bf16[64,5120]{1,0:T(8,128)(2,1)S(1)} %constant_dynamic-update-slice_fusion.8.refs_5_), channel_id=1, source_target_pairs={{0,1},{1,0},{2,3},{3,2},{4,5},{5,4},{6,7},{7,6},{8,9},{9,8},{10,11... | collective-permute-start | bytes 1966088 | tf_op jit(solution)/shard_map/ppermute | solution.py:505
  215.8 18.1 %all-to-all-start.4 = ((f32[128,1,128]{2,1,0:T(1,128)}), f32[128,1,128]{2,1,0:T(1,128)S(1)}, u32[]{:S(2)}, u32[]{:S(2)}) async-start(f32[128,1,128]{2,1,0:T(1,128)} %get-tuple-element.136), calls=%async_computation.4 | async-start | bytes 131072 | tf_op jit(solution)/shard_map/all_to_all | solution.py:492
  235.4 19.3 %all-to-all-start.5 = ((bf16[16,128,256]{2,1,0:T(8,128)(2,1)}), bf16[16,128,256]{2,1,0:T(8,128)(2,1)S(1)}, u32[]{:S(2)}, u32[]{:S(2)}) async-start(bf16[16,128,256]{2,1,0:T(8,128)(2,1)} %get-tuple-element.142), calls=%async_computation.5 | async-start | bytes 2097152 | tf_op jit(solution)/shard_map/all_to_all | solution.py:556
  260.2 4.8 %collective-permute-start.36 = (bf16[64,5120]{1,0:T(8,128)(2,1)S(1)}, bf16[64,5120]{1,0:T(8,128)(2,1)S(1)}, u32[]{:S(2)}, u32[]{:S(2)}) collective-permute-start(bf16[64,5120]{1,0:T(8,128)(2,1)S(1)} %get-tuple-element.144), channel_id=1, source_target_pairs={{0,1},{1,0},{2,3},{3,2},{4,5},{5,4},{6,7},{7,6},{8,9},{9,8},{10,11... | collective-permute-start | bytes 1966088 | tf_op jit(solution)/shard_map/ppermute | solution.py:584
  265.2 6.1 %collective-permute-start.37 = (bf16[16,5120]{1,0:T(8,128)(2,1)S(1)}, bf16[16,5120]{1,0:T(8,128)(2,1)S(1)}, u32[]{:S(2)}, u32[]{:S(2)}) collective-permute-start(bf16[16,5120]{1,0:T(8,128)(2,1)S(1)} %get-tuple-element.173), channel_id=1, source_target_pairs={{0,6},{2,0},{4,2},{6,4},{1,7},{3,1},{5,3},{7,5},{8,14},{10,8},{12,... | collective-permute-start | bytes 491528 | tf_op jit(solution)/shard_map/ppermute | solution.py:588
  267.6 6.6 %collective-permute-start.38 = (bf16[16,5120]{1,0:T(8,128)(2,1)S(1)}, bf16[16,5120]{1,0:T(8,128)(2,1)S(1)}, u32[]{:S(2)}, u32[]{:S(2)}) collective-permute-start(bf16[16,5120]{1,0:T(8,128)(2,1)S(1)} %get-tuple-element.172), channel_id=1, source_target_pairs={{0,4},{2,6},{4,0},{6,2},{1,5},{3,7},{5,1},{7,3},{8,12},{10,14},{12... | collective-permute-start | bytes 491528 | tf_op jit(solution)/shard_map/ppermute | solution.py:588
  268.1 10.7 %collective-permute-start.39 = (bf16[16,5120]{1,0:T(8,128)(2,1)S(1)}, bf16[16,5120]{1,0:T(8,128)(2,1)S(1)}, u32[]{:S(2)}, u32[]{:S(2)}) collective-permute-start(bf16[16,5120]{1,0:T(8,128)(2,1)S(1)} %get-tuple-element.171), channel_id=1, source_target_pairs={{0,2},{2,4},{4,6},{6,0},{1,3},{3,5},{5,7},{7,1},{8,10},{10,12},{12... | collective-permute-start | bytes 491528 | tf_op jit(solution)/shard_map/ppermute | solution.py:588
  280.0 5.5 %collective-permute-start.42 = (f32[2,2,16,640]{3,2,1,0:T(8,128)}, f32[2,2,16,640]{3,2,1,0:T(8,128)S(1)}, u32[]{:S(2)}, u32[]{:S(2)}) collective-permute-start(f32[2,2,16,640]{3,2,1,0:T(8,128)} %get-tuple-element.161), channel_id=1, source_target_pairs={{0,6},{2,0},{4,2},{6,4},{1,7},{3,1},{5,3},{7,5},{8,14},{10,8},{12,... | collective-permute-start | bytes 491528 | tf_op jit(solution)/shard_map/ppermute | solution.py:451
  280.1 6.5 %collective-permute-start.41 = (f32[2,2,16,640]{3,2,1,0:T(8,128)}, f32[2,2,16,640]{3,2,1,0:T(8,128)S(1)}, u32[]{:S(2)}, u32[]{:S(2)}) collective-permute-start(f32[2,2,16,640]{3,2,1,0:T(8,128)} %get-tuple-element.160), channel_id=1, source_target_pairs={{0,4},{2,6},{4,0},{6,2},{1,5},{3,7},{5,1},{7,3},{8,12},{10,14},{12... | collective-permute-start | bytes 491528 | tf_op jit(solution)/shard_map/ppermute | solution.py:451
  280.6 10.9 %collective-permute-start.40 = (f32[2,2,16,640]{3,2,1,0:T(8,128)}, f32[2,2,16,640]{3,2,1,0:T(8,128)S(1)}, u32[]{:S(2)}, u32[]{:S(2)}) collective-permute-start(f32[2,2,16,640]{3,2,1,0:T(8,128)} %get-tuple-element.159), channel_id=1, source_target_pairs={{0,2},{2,4},{4,6},{6,0},{1,3},{3,5},{5,7},{7,1},{8,10},{10,12},{12... | collective-permute-start | bytes 491528 | tf_op jit(solution)/shard_map/ppermute | solution.py:451
  292.5 13.8 %collective-permute-start.43 = (f32[4,2,16,640]{3,2,1,0:T(8,128)S(1)}, f32[4,2,16,640]{3,2,1,0:T(8,128)S(1)}, u32[]{:S(2)}, u32[]{:S(2)}) collective-permute-start(f32[4,2,16,640]{3,2,1,0:T(8,128)S(1)} %pad_maximum_fusion.2), channel_id=1, source_target_pairs={{0,1},{1,0},{2,3},{3,2},{4,5},{5,4},{6,7},{7,6},{8,9},{9,8},{10,11... | collective-permute-start | bytes 983048 | tf_op jit(solution)/shard_map/ppermute | solution.py:453
  (18 other events, 186.2 us)
